TPU v7x, 16 devices: a whole 2x2x2 slice. The times are simulated.
16 devices in a mesh: hp: 4 (over z, y), cp: 4 (over x, core).
Axes of the slice: x: 2, y: 2, z: 2, core: 2. Of those that a mesh axis runs over, the one named last changes fastest.
Arguments:
- q: bfloat16 [6144, 8, 128], P('cp', 'hp'), parts along dimension 1
- k: bfloat16 [6144, 8, 128], P('cp', 'hp'), parts along dimension 1
- v: bfloat16 [6144, 8, 128], P('cp', 'hp'), parts along dimension 1
- u_bias: float32 [8, 128], P('hp'), parts along dimension 0
- v_bias: float32 [8, 128], P('hp'), parts along dimension 0
- rel_table: bfloat16 [6144, 1024], P('cp')
- w_rel: bfloat16 [1024, 8, 128], P(None, 'hp'), parts along dimension 1
- d_out: bfloat16 [6144, 8, 128], P('cp', 'hp'), parts along dimension 1
Outputs:
- output 1: bfloat16 [6144, 8, 128], P('cp', 'hp'), parts along dimension 1
- output 2: bfloat16 [6144, 8, 128], P('cp', 'hp'), parts along dimension 1
- output 3: bfloat16 [6144, 8, 128], P('cp', 'hp'), parts along dimension 1
- output 4: bfloat16 [6144, 8, 128], P('cp', 'hp'), parts along dimension 1
- output 5: float32 [8, 128], P('hp'), parts along dimension 0
- output 6: float32 [8, 128], P('hp'), parts along dimension 0
- output 7: float32 [1024, 8, 128], P(None, 'hp'), parts along dimension 1
There are 4 independent parts. A program takes and returns all parts, laid end to end along the dimension named above; an argument that names none is the same for every part.
All inputs are finite; a program needn't handle non-finite values.
Results may differ from a plain program's by a relative error of at most 0.0150476.
Values are sent between devices in bfloat16 or wider.
A program may use at most 1 GiB of HBM per device.

v0:
```python
import jax
import jax.numpy as jnp
from jax import lax
from jax.sharding import PartitionSpec as P


def skew_scores(by_offset):
    lead_dims = by_offset.shape[:-2]
    block_len = by_offset.shape[-2]
    flat_view = by_offset.reshape(lead_dims + (2 * block_len * block_len,))
    kept_view = flat_view[..., block_len - 1:block_len - 1 + block_len * (2 * block_len - 1)]
    return kept_view.reshape(lead_dims + (block_len, 2 * block_len - 1))[..., :block_len]


def unskew_scores(by_key):
    lead_dims = by_key.shape[:-2]
    block_len = by_key.shape[-1]
    pad_lead = [(0, 0)] * len(lead_dims)
    widened = jnp.pad(by_key, pad_lead + [(0, 0), (0, block_len - 1)])
    flat_view = widened.reshape(lead_dims + (block_len * (2 * block_len - 1),))
    flat_view = jnp.pad(flat_view, pad_lead + [(block_len - 1, 1)])
    return flat_view.reshape(lead_dims + (block_len, 2 * block_len))


def solution(mesh):
    n_dev = mesh.shape['cp']
    shift_pairs = [(src_dev, (src_dev + 1) % n_dev) for src_dev in range(n_dev)]
    last_step = n_dev - 1
    seq_spec = P('cp', 'hp', None)
    head_spec = P('hp', None)
    weight_spec = P(None, 'hp', None)

    def local_fn(q, k, v, u_bias, v_bias, rel_table, w_rel, d_out):
        block_len, num_heads, head_dim = q.shape
        inv_sqrt = head_dim ** -0.5
        my_block = lax.axis_index('cp')
        rel_mine = jnp.einsum('uo,ojf->ujf', rel_table, w_rel, preferred_element_type=jnp.float32).astype(jnp.bfloat16)
        rel_flipped = lax.all_gather(rel_mine[::-1], 'cp')
        q_wide = q.astype(jnp.float32)
        q_u = (q_wide + u_bias).astype(jnp.bfloat16)
        q_v = (q_wide + v_bias).astype(jnp.bfloat16)
        row_ids = jnp.arange(block_len)
        above_diag = row_ids[None, :] > row_ids[:, None]

        def rel_window(distance):
            near_blk = lax.dynamic_index_in_dim(rel_flipped, distance, 0, keepdims=False)
            far_blk = lax.dynamic_index_in_dim(rel_flipped, jnp.maximum(distance - 1, 0), 0, keepdims=False)
            return jnp.concatenate([near_blk, far_blk], axis=0)

        def block_scores(k_blk, window, distance):
            content = jnp.einsum('qhd,khd->hqk', q_u, k_blk, preferred_element_type=jnp.float32)
            by_offset = jnp.einsum('qhd,shd->hqs', q_v, window, preferred_element_type=jnp.float32)
            score_ij = (content + skew_scores(by_offset)) * inv_sqrt
            return jnp.where(above_diag & (distance == 0), -jnp.inf, score_ij)

        def attend(distance, k_blk, v_blk, run_stats):
            run_max, run_sum, out_acc = run_stats
            score_ij = block_scores(k_blk, rel_window(distance), distance)
            new_max = jnp.maximum(run_max, score_ij.max(axis=-1))
            prob_ij = jnp.exp(score_ij - new_max[..., None])
            rescale = jnp.exp(run_max - new_max)
            run_sum = rescale * run_sum + prob_ij.sum(axis=-1)
            out_acc = out_acc * rescale.T[:, :, None] + jnp.einsum('hqk,khd->qhd', prob_ij.astype(jnp.bfloat16), v_blk, preferred_element_type=jnp.float32)
            return new_max, run_sum, out_acc

        def fwd_step(step_idx, carry):
            k_blk, v_blk, run_stats = carry
            run_stats = lax.cond(step_idx <= my_block, lambda stats_in: attend(step_idx, k_blk, v_blk, stats_in), lambda stats_in: stats_in, run_stats)
            k_blk = lax.ppermute(k_blk, 'cp', shift_pairs)
            v_blk = lax.ppermute(v_blk, 'cp', shift_pairs)
            return k_blk, v_blk, run_stats

        run_stats = (
            jnp.full((num_heads, block_len), -jnp.inf, jnp.float32),
            jnp.zeros((num_heads, block_len), jnp.float32),
            jnp.zeros((block_len, num_heads, head_dim), jnp.float32),
        )
        k_blk, v_blk, run_stats = lax.fori_loop(0, last_step, fwd_step, (k, v, run_stats))
        run_stats = lax.cond(last_step <= my_block, lambda stats_in: attend(last_step, k_blk, v_blk, stats_in), lambda stats_in: stats_in, run_stats)
        run_max, run_sum, out_acc = run_stats
        out_full = out_acc / run_sum.T[:, :, None]
        log_norm = run_max + jnp.log(run_sum)
        row_delta = jnp.sum(d_out.astype(jnp.float32) * out_full, axis=-1).T

        def grad_block(distance, k_blk, v_blk, grad_state):
            dk_acc, dv_acc, grad_qu, grad_qv, grad_rel = grad_state
            window = rel_window(distance)
            score_ij = block_scores(k_blk, window, distance)
            prob_ij = jnp.exp(score_ij - log_norm[..., None])
            d_prob = jnp.einsum('qhd,khd->hqk', d_out, v_blk, preferred_element_type=jnp.float32)
            d_score = (prob_ij * (d_prob - row_delta[..., None]) * inv_sqrt).astype(jnp.bfloat16)
            dv_acc = dv_acc + jnp.einsum('hqk,qhd->khd', prob_ij.astype(jnp.bfloat16), d_out, preferred_element_type=jnp.float32)
            dk_acc = dk_acc + jnp.einsum('hqk,qhd->khd', d_score, q_u, preferred_element_type=jnp.float32)
            grad_qu = grad_qu + jnp.einsum('hqk,khd->qhd', d_score, k_blk, preferred_element_type=jnp.float32)
            d_wide = unskew_scores(d_score)
            grad_qv = grad_qv + jnp.einsum('hqs,shd->qhd', d_wide, window, preferred_element_type=jnp.float32)
            d_window = jnp.einsum('hqs,qhd->shd', d_wide, q_v, preferred_element_type=jnp.float32)
            near_sum = lax.dynamic_index_in_dim(grad_rel, distance, 0, keepdims=False) + d_window[:block_len]
            grad_rel = lax.dynamic_update_index_in_dim(grad_rel, near_sum, distance, 0)
            far_idx = jnp.maximum(distance - 1, 0)
            far_sum = lax.dynamic_index_in_dim(grad_rel, far_idx, 0, keepdims=False) + d_window[block_len:]
            grad_rel = lax.dynamic_update_index_in_dim(grad_rel, far_sum, far_idx, 0)
            return dk_acc, dv_acc, grad_qu, grad_qv, grad_rel

        def bwd_step(step_idx, carry):
            k_blk, v_blk, grad_state = carry
            grad_state = lax.cond(step_idx <= my_block, lambda grads_in: grad_block(step_idx, k_blk, v_blk, grads_in), lambda grads_in: grads_in, grad_state)
            dk_acc, dv_acc, grad_qu, grad_qv, grad_rel = grad_state
            k_blk = lax.ppermute(k_blk, 'cp', shift_pairs)
            v_blk = lax.ppermute(v_blk, 'cp', shift_pairs)
            dk_acc = lax.ppermute(dk_acc, 'cp', shift_pairs)
            dv_acc = lax.ppermute(dv_acc, 'cp', shift_pairs)
            return k_blk, v_blk, (dk_acc, dv_acc, grad_qu, grad_qv, grad_rel)

        blk_zeros = jnp.zeros((block_len, num_heads, head_dim), jnp.float32)
        grad_state = (blk_zeros, blk_zeros, blk_zeros, blk_zeros, jnp.zeros((n_dev, block_len, num_heads, head_dim), jnp.float32))
        k_blk, v_blk, grad_state = lax.fori_loop(0, last_step, bwd_step, (k, v, grad_state))
        grad_state = lax.cond(last_step <= my_block, lambda grads_in: grad_block(last_step, k_blk, v_blk, grads_in), lambda grads_in: grads_in, grad_state)
        dk_acc, dv_acc, grad_qu, grad_qv, grad_rel = grad_state
        dk_acc = lax.ppermute(dk_acc, 'cp', shift_pairs)
        dv_acc = lax.ppermute(dv_acc, 'cp', shift_pairs)
        rel_grad_mine = lax.psum_scatter(grad_rel, 'cp', scatter_dimension=0, tiled=False)
        d_rel = rel_grad_mine[::-1].astype(jnp.bfloat16)
        d_w_rel = lax.psum(jnp.einsum('uo,ujf->ojf', rel_table, d_rel, preferred_element_type=jnp.float32), 'cp')
        d_u_bias = lax.psum(grad_qu.sum(axis=0), 'cp')
        d_v_bias = lax.psum(grad_qv.sum(axis=0), 'cp')
        return (
            out_full.astype(jnp.bfloat16),
            (grad_qu + grad_qv).astype(jnp.bfloat16),
            dk_acc.astype(jnp.bfloat16),
            dv_acc.astype(jnp.bfloat16),
            d_u_bias,
            d_v_bias,
            d_w_rel,
        )

    return jax.shard_map(
        local_fn,
        mesh=mesh,
        in_specs=(seq_spec, seq_spec, seq_spec, head_spec, head_spec, P('cp', None), weight_spec, seq_spec),
        out_specs=(seq_spec, seq_spec, seq_spec, seq_spec, head_spec, head_spec, weight_spec),
        check_vma=False,
    )
```

profile of v0, /device:TPU:0, one launch (start us, length us, event | category | flops | bytes accessed | tf_op | source)
XLA Modules:
  0.0 3980.6 jit_solution(13781208100804512539)
XLA Ops:
  36.1 17.2 all-gather.3.cloned.1.call-done
  59.4 812.4 %while.48 = (s32[]{:T(128)}, bf16[1536,2,128]{2,0,1:T(8,128)(2,1)}, bf16[1536,2,128]{2,0,1:T(8,128)(2,1)}, f32[2,1536]{1,0:T(2,128)}, f32[2,1536]{1,0:T(2,128)},...) while((s32[]{:T(128)}, bf16[1536,2,128]{2,0,1:T(8,128)(2,1)}, ...), condition=%wide.region_5.6_spmd.clone, body=%wide.region_0.5_spmd.clone.sunk | while | flops 4878246912 | bytes 635707840 | solution.py:78
  73.5 372.8 %conditional.10 = ((f32[2,1536]{1,0:T(2,128)}, f32[2,1536]{1,0:T(2,128)}, f32[1536,2,128]{2,0,1:T(8,128)})) conditional(s32[]{:T(128)} %convert_element_type.127, (f32[2,1536]{1,0:T(2,128)}, f32[2,1536]{1,0:T(2,128)}, f32[1536,2,128]{2,0,1:T(8,128)}) %tuple.145, (s32[]{:T(128)}, s32[1536,1536]{0,1:T(8,128)}, bf16[1536,2,128]{2,0,1:T(8,128)(2,1)}, ...), branch_computations={%region_1.0_spmd, %region_2.4_spmd} | conditional | flops 4878246912 | bytes 607395968 | solution.py:68
  89.8 36.8 copy.83
  126.6 61.9 %copy.138 = f32[1,2,1536,3072]{3,1,2,0:T(2,128)} copy(f32[1,2,1536,3072]{3,2,1,0:T(8,128)} %bitcast.172) | data formatting | bytes 75497472 | tf_op jit(solution)/shard_map/while/body/eval_jaxpr/cond
  188.5 44.4 %slice.44 = f32[2,4717056]{1,0:T(2,128)} slice(f32[2,4718592]{1,0:T(2,128)} %bitcast.174), slice={[0:2], [1535:4718591]} | slice | bytes 75472896 | tf_op jit(solution)/shard_map/while/body/eval_jaxpr/cond/branch_1_fun/slice | solution.py:11
  232.9 82.9 %reshape.65 = f32[9434112]{0:T(1024)} reshape(f32[2,4717056]{1,0:T(2,128)} %slice.44) | data formatting | bytes 75472896 | tf_op jit(solution)/shard_map/while/body/eval_jaxpr/cond
  315.8 51.9 %reshape.50 = f32[2,1536,3071]{2,1,0:T(8,128)} reshape(f32[9434112]{0:T(1024)} %reshape.65) | data formatting | bytes 75472896 | tf_op jit(solution)/shard_map/while/body/eval_jaxpr/cond/branch_1_fun/reshape | solution.py:12
  382.1 18.7 copy.133
  476.5 372.3 %collective-permute-start = (bf16[1536,2,128]{2,0,1:T(8,128)(2,1)}, bf16[1536,2,128]{2,0,1:T(8,128)(2,1)}, u32[]{:S(2)}, u32[]{:S(2)}) collective-permute-start(bf16[1536,2,128]{2,0,1:T(8,128)(2,1)} %copy.216), channel_id=1, source_target_pairs={{0,1},{1,2},{2,3},{3,0},{4,5},{5,6},{6,7},{7,4},{8,9},{9,10},{10,1... | collective-permute-start | bytes 2359304 | tf_op jit(solution)/shard_map/while/body/eval_jaxpr/ppermute | solution.py:69
  885.7 24.4 multiply_reduce_fusion
  919.9 2443.8 %while.49 = (s32[]{:T(128)}, bf16[1536,2,128]{2,0,1:T(8,128)(2,1)}, bf16[1536,2,128]{2,0,1:T(8,128)(2,1)}, f32[1536,2,128]{2,0,1:T(8,128)}, f32[1536,2,128]{2,0,...) while((s32[]{:T(128)}, bf16[1536,2,128]{2,0,1:T(8,128)(2,1)}, ...), condition=%wide.region_14.15_spmd.clone, body=%wide.region_11.14_spmd.clone.sunk | while | flops 13343391744 | bytes 936555136 | solution.py:117
  933.4 505.9 %conditional.11 = ((f32[1536,2,128]{2,0,1:T(8,128)}, f32[1536,2,128]{2,0,1:T(8,128)}, f32[1536,2,128]{2,0,1:T(8,128)}, f32[1536,2,128]{0,2,1:T(8,128)}, f32[4,1536,2,128]{3,1,2,0:T(8,128)})) conditional(s32[]{:T(128)} %convert_element_type.128, (f32[1536,2,128]{2,0,1:T(8,128)}, f32[1536,2,128]{2,0,1:T(8,128)}, f32[1536,2,128]{2,0,1:T(8,128)}, ...), branch_computations={%region_12.12_spmd, %region_13.13_spmd} | conditional | flops 13343391744 | bytes 889368832 | solution.py:107
  950.8 36.8 copy.86
  987.6 61.9 %copy.139 = f32[1,2,1536,3072]{3,1,2,0:T(2,128)} copy(f32[1,2,1536,3072]{3,2,1,0:T(8,128)} %bitcast.173) | data formatting | bytes 75497472 | tf_op jit(solution)/shard_map/while/body/eval_jaxpr/cond
  1049.5 44.7 %slice.46 = f32[2,4717056]{1,0:T(2,128)} slice(f32[2,4718592]{1,0:T(2,128)} %bitcast.175), slice={[0:2], [1535:4718591]} | slice | bytes 75472896 | tf_op jit(solution)/shard_map/while/body/eval_jaxpr/cond/branch_1_fun/slice | solution.py:11
  1094.2 83.0 %reshape.67 = f32[9434112]{0:T(1024)} reshape(f32[2,4717056]{1,0:T(2,128)} %slice.46) | data formatting | bytes 75472896 | tf_op jit(solution)/shard_map/while/body/eval_jaxpr/cond
  1177.2 51.9 %reshape.54 = f32[2,1536,3071]{2,1,0:T(8,128)} reshape(f32[9434112]{0:T(1024)} %reshape.67) | data formatting | bytes 75472896 | tf_op jit(solution)/shard_map/while/body/eval_jaxpr/cond/branch_1_fun/reshape | solution.py:12
  1239.4 17.2 fusion.27
  1277.7 45.4 %reshape.69 = bf16[9434112]{0:T(1024)(128)(2,1)} reshape(bf16[2,1536,3071]{2,1,0:T(8,128)(2,1)} %pad.10) | data formatting | bytes 37736448 | tf_op jit(solution)/shard_map/while/body/eval_jaxpr/cond
  1323.2 23.6 reshape.55
  1346.8 29.4 pad.11
  1394.8 18.4 fusion.46
  1439.6 372.0 %collective-permute-start.5 = (f32[1536,2,128]{2,0,1:T(8,128)}, f32[1536,2,128]{2,0,1:T(8,128)}, u32[]{:S(2)}, u32[]{:S(2)}) collective-permute-start(f32[1536,2,128]{2,0,1:T(8,128)} %get-tuple-element.1179), channel_id=1, source_target_pairs={{0,1},{1,2},{2,3},{3,0},{4,5},{5,6},{6,7},{7,4},{8,9},{9,10},{10,1... | collective-permute-start | bytes 4718600 | tf_op jit(solution)/shard_map/while/body/eval_jaxpr/ppermute | solution.py:112
  1811.7 354.9 %collective-permute-start.2 = (bf16[1536,2,128]{2,0,1:T(8,128)(2,1)}, bf16[1536,2,128]{2,0,1:T(8,128)(2,1)}, u32[]{:S(2)}, u32[]{:S(2)}) collective-permute-start(bf16[1536,2,128]{2,0,1:T(8,128)(2,1)} %copy.242), channel_id=1, source_target_pairs={{0,1},{1,2},{2,3},{3,0},{4,5},{5,6},{6,7},{7,4},{8,9},{9,10},{10,1... | collective-permute-start | bytes 2359304 | tf_op jit(solution)/shard_map/while/body/eval_jaxpr/ppermute | solution.py:109
  2166.6 17.5 collective-permute-done.4
  2231.5 488.7 %collective-permute-start.4 = (f32[1536,2,128]{2,0,1:T(8,128)}, f32[1536,2,128]{2,0,1:T(8,128)}, u32[]{:S(2)}, u32[]{:S(2)}) collective-permute-start(f32[1536,2,128]{2,0,1:T(8,128)} %get-tuple-element.1178), channel_id=1, source_target_pairs={{0,1},{1,2},{2,3},{3,0},{4,5},{5,6},{6,7},{7,4},{8,9},{9,10},{10,1... | collective-permute-start | bytes 4718600 | tf_op jit(solution)/shard_map/while/body/eval_jaxpr/ppermute | solution.py:111
  2737.0 17.5 collective-permute-done.4
  2801.5 494.1 %collective-permute-start.5 = (f32[1536,2,128]{2,0,1:T(8,128)}, f32[1536,2,128]{2,0,1:T(8,128)}, u32[]{:S(2)}, u32[]{:S(2)}) collective-permute-start(f32[1536,2,128]{2,0,1:T(8,128)} %get-tuple-element.1179), channel_id=1, source_target_pairs={{0,1},{1,2},{2,3},{3,0},{4,5},{5,6},{6,7},{7,4},{8,9},{9,10},{10,1... | collective-permute-start | bytes 4718600 | tf_op jit(solution)/shard_map/while/body/eval_jaxpr/ppermute | solution.py:112
  3307.3 17.5 collective-permute-done.4
  3363.6 16.0 conditional.5
  3393.1 525.4 %reduce-scatter.2.cloned.1.call-done = f32[1,1536,2,128]{3,1,2,0:T(8,128)} async-done(((f32[4,1536,2,128]{3,1,2,0:T(8,128)}), f32[1,1536,2,128]{3,1,2,0:T(8,128)}) %reduce-scatter.2.cloned.1.call-update) | async-done | bytes 1572880 | tf_op jit(solution)/shard_map/reduce_scatter | solution.py:122
  (180 shorter events, 523.4 us)
Async XLA Ops:
  7.2 46.1 %all-gather.3.cloned.1.call-start = ((), (), s32[]{:S(2)}) async-start(), calls=%async_computation.3 | async-start | bytes 3932160 | tf_op jit(solution)/shard_map/all_gather | solution.py:38
  23.9 3894.5 %reduce-scatter.2.cloned.1.call-start = ((), (), s32[]{:S(2)}) async-start(), calls=%async_computation.1 | async-start | bytes 7864320 | tf_op jit(solution)/shard_map/reduce_scatter | solution.py:122
  62.0 384.3 %collective-permute-start = (bf16[1536,2,128]{2,0,1:T(8,128)(2,1)}, bf16[1536,2,128]{2,0,1:T(8,128)(2,1)}, u32[]{:S(2)}, u32[]{:S(2)}) collective-permute-start(bf16[1536,2,128]{2,0,1:T(8,128)(2,1)} %copy.216), channel_id=1, source_target_pairs={{0,1},{1,2},{2,3},{3,0},{4,5},{5,6},{6,7},{7,4},{8,9},{9,10},{10,1... | collective-permute-start | bytes 2359304 | tf_op jit(solution)/shard_map/while/body/eval_jaxpr/ppermute | solution.py:69
  64.3 382.0 %collective-permute-start.1 = (bf16[1536,2,128]{2,0,1:T(8,128)(2,1)}, bf16[1536,2,128]{2,0,1:T(8,128)(2,1)}, u32[]{:S(2)}, u32[]{:S(2)}) collective-permute-start(bf16[1536,2,128]{2,0,1:T(8,128)(2,1)} %copy.217), channel_id=1, source_target_pairs={{0,1},{1,2},{2,3},{3,0},{4,5},{5,6},{6,7},{7,4},{8,9},{9,10},{10,1... | collective-permute-start | bytes 2359304 | tf_op jit(solution)/shard_map/while/body/eval_jaxpr/ppermute | solution.py:70
  400.8 10.3 copy-start.2
  411.1 13.2 copy-start.32
  454.4 14.3 collective-permute-start
  456.9 17.3 collective-permute-start.1
  476.5 383.5 %collective-permute-start = (bf16[1536,2,128]{2,0,1:T(8,128)(2,1)}, bf16[1536,2,128]{2,0,1:T(8,128)(2,1)}, u32[]{:S(2)}, u32[]{:S(2)}) collective-permute-start(bf16[1536,2,128]{2,0,1:T(8,128)(2,1)} %copy.216), channel_id=1, source_target_pairs={{0,1},{1,2},{2,3},{3,0},{4,5},{5,6},{6,7},{7,4},{8,9},{9,10},{10,1... | collective-permute-start | bytes 2359304 | tf_op jit(solution)/shard_map/while/body/eval_jaxpr/ppermute | solution.py:69
  850.8 16.0 collective-permute-start.1
  1229.0 10.4 copy-start.3
  1229.0 10.4 copy-start.6
  1346.8 29.4 copy-start.14
  1346.8 44.6 %slice-start = ((s8[6291456]{0:T(1024)(128)(4,1)}), s8[4194304]{0:T(1024)(128)(4,1)S(1)}, s32[]{:S(2)}) async-start(s8[6291456]{0:T(1024)(128)(4,1)} %bitcast.178), calls=%async_computation.4 | async-start | bytes 8388608 | tf_op jit(solution)/shard_map/while/body/eval_jaxpr/cond
  1376.3 15.1 slice-start.1
  1394.8 18.4 copy-start.4
  1394.8 18.4 copy-start.17
  1439.3 744.9 %collective-permute-start.4 = (f32[1536,2,128]{2,0,1:T(8,128)}, f32[1536,2,128]{2,0,1:T(8,128)}, u32[]{:S(2)}, u32[]{:S(2)}) collective-permute-start(f32[1536,2,128]{2,0,1:T(8,128)} %get-tuple-element.1178), channel_id=1, source_target_pairs={{0,1},{1,2},{2,3},{3,0},{4,5},{5,6},{6,7},{7,4},{8,9},{9,10},{10,1... | collective-permute-start | bytes 4718600 | tf_op jit(solution)/shard_map/while/body/eval_jaxpr/ppermute | solution.py:111
  1439.6 761.4 %collective-permute-start.5 = (f32[1536,2,128]{2,0,1:T(8,128)}, f32[1536,2,128]{2,0,1:T(8,128)}, u32[]{:S(2)}, u32[]{:S(2)}) collective-permute-start(f32[1536,2,128]{2,0,1:T(8,128)} %get-tuple-element.1179), channel_id=1, source_target_pairs={{0,1},{1,2},{2,3},{3,0},{4,5},{5,6},{6,7},{7,4},{8,9},{9,10},{10,1... | collective-permute-start | bytes 4718600 | tf_op jit(solution)/shard_map/while/body/eval_jaxpr/ppermute | solution.py:112
  1811.7 397.8 %collective-permute-start.2 = (bf16[1536,2,128]{2,0,1:T(8,128)(2,1)}, bf16[1536,2,128]{2,0,1:T(8,128)(2,1)}, u32[]{:S(2)}, u32[]{:S(2)}) collective-permute-start(bf16[1536,2,128]{2,0,1:T(8,128)(2,1)} %copy.242), channel_id=1, source_target_pairs={{0,1},{1,2},{2,3},{3,0},{4,5},{5,6},{6,7},{7,4},{8,9},{9,10},{10,1... | collective-permute-start | bytes 2359304 | tf_op jit(solution)/shard_map/while/body/eval_jaxpr/ppermute | solution.py:109
  2166.5 51.3 %collective-permute-start.3 = (bf16[1536,2,128]{2,0,1:T(8,128)(2,1)}, bf16[1536,2,128]{2,0,1:T(8,128)(2,1)}, u32[]{:S(2)}, u32[]{:S(2)}) collective-permute-start(bf16[1536,2,128]{2,0,1:T(8,128)(2,1)} %copy.243), channel_id=1, source_target_pairs={{0,1},{1,2},{2,3},{3,0},{4,5},{5,6},{6,7},{7,4},{8,9},{9,10},{10,1... | collective-permute-start | bytes 2359304 | tf_op jit(solution)/shard_map/while/body/eval_jaxpr/ppermute | solution.py:110
  2231.5 523.0 %collective-permute-start.4 = (f32[1536,2,128]{2,0,1:T(8,128)}, f32[1536,2,128]{2,0,1:T(8,128)}, u32[]{:S(2)}, u32[]{:S(2)}) collective-permute-start(f32[1536,2,128]{2,0,1:T(8,128)} %get-tuple-element.1178), channel_id=1, source_target_pairs={{0,1},{1,2},{2,3},{3,0},{4,5},{5,6},{6,7},{7,4},{8,9},{9,10},{10,1... | collective-permute-start | bytes 4718600 | tf_op jit(solution)/shard_map/while/body/eval_jaxpr/ppermute | solution.py:111
  2720.2 51.2 %collective-permute-start.5 = (f32[1536,2,128]{2,0,1:T(8,128)}, f32[1536,2,128]{2,0,1:T(8,128)}, u32[]{:S(2)}, u32[]{:S(2)}) collective-permute-start(f32[1536,2,128]{2,0,1:T(8,128)} %get-tuple-element.1179), channel_id=1, source_target_pairs={{0,1},{1,2},{2,3},{3,0},{4,5},{5,6},{6,7},{7,4},{8,9},{9,10},{10,1... | collective-permute-start | bytes 4718600 | tf_op jit(solution)/shard_map/while/body/eval_jaxpr/ppermute | solution.py:112
  2722.7 57.1 %collective-permute-start.2 = (bf16[1536,2,128]{2,0,1:T(8,128)(2,1)}, bf16[1536,2,128]{2,0,1:T(8,128)(2,1)}, u32[]{:S(2)}, u32[]{:S(2)}) collective-permute-start(bf16[1536,2,128]{2,0,1:T(8,128)(2,1)} %copy.242), channel_id=1, source_target_pairs={{0,1},{1,2},{2,3},{3,0},{4,5},{5,6},{6,7},{7,4},{8,9},{9,10},{10,1... | collective-permute-start | bytes 2359304 | tf_op jit(solution)/shard_map/while/body/eval_jaxpr/ppermute | solution.py:109
  2736.9 51.3 %collective-permute-start.3 = (bf16[1536,2,128]{2,0,1:T(8,128)(2,1)}, bf16[1536,2,128]{2,0,1:T(8,128)(2,1)}, u32[]{:S(2)}, u32[]{:S(2)}) collective-permute-start(bf16[1536,2,128]{2,0,1:T(8,128)(2,1)} %copy.243), channel_id=1, source_target_pairs={{0,1},{1,2},{2,3},{3,0},{4,5},{5,6},{6,7},{7,4},{8,9},{9,10},{10,1... | collective-permute-start | bytes 2359304 | tf_op jit(solution)/shard_map/while/body/eval_jaxpr/ppermute | solution.py:110
  2801.5 523.4 %collective-permute-start.4 = (f32[1536,2,128]{2,0,1:T(8,128)}, f32[1536,2,128]{2,0,1:T(8,128)}, u32[]{:S(2)}, u32[]{:S(2)}) collective-permute-start(f32[1536,2,128]{2,0,1:T(8,128)} %get-tuple-element.1178), channel_id=1, source_target_pairs={{0,1},{1,2},{2,3},{3,0},{4,5},{5,6},{6,7},{7,4},{8,9},{9,10},{10,1... | collective-permute-start | bytes 4718600 | tf_op jit(solution)/shard_map/while/body/eval_jaxpr/ppermute | solution.py:111
  2801.5 540.2 %collective-permute-start.5 = (f32[1536,2,128]{2,0,1:T(8,128)}, f32[1536,2,128]{2,0,1:T(8,128)}, u32[]{:S(2)}, u32[]{:S(2)}) collective-permute-start(f32[1536,2,128]{2,0,1:T(8,128)} %get-tuple-element.1179), channel_id=1, source_target_pairs={{0,1},{1,2},{2,3},{3,0},{4,5},{5,6},{6,7},{7,4},{8,9},{9,10},{10,1... | collective-permute-start | bytes 4718600 | tf_op jit(solution)/shard_map/while/body/eval_jaxpr/ppermute | solution.py:112
  3295.6 54.5 %collective-permute-start.2 = (bf16[1536,2,128]{2,0,1:T(8,128)(2,1)}, bf16[1536,2,128]{2,0,1:T(8,128)(2,1)}, u32[]{:S(2)}, u32[]{:S(2)}) collective-permute-start(bf16[1536,2,128]{2,0,1:T(8,128)(2,1)} %copy.242), channel_id=1, source_target_pairs={{0,1},{1,2},{2,3},{3,0},{4,5},{5,6},{6,7},{7,4},{8,9},{9,10},{10,1... | collective-permute-start | bytes 2359304 | tf_op jit(solution)/shard_map/while/body/eval_jaxpr/ppermute | solution.py:109
  3307.3 51.3 %collective-permute-start.3 = (bf16[1536,2,128]{2,0,1:T(8,128)(2,1)}, bf16[1536,2,128]{2,0,1:T(8,128)(2,1)}, u32[]{:S(2)}, u32[]{:S(2)}) collective-permute-start(bf16[1536,2,128]{2,0,1:T(8,128)(2,1)} %copy.243), channel_id=1, source_target_pairs={{0,1},{1,2},{2,3},{3,0},{4,5},{5,6},{6,7},{7,4},{8,9},{9,10},{10,1... | collective-permute-start | bytes 2359304 | tf_op jit(solution)/shard_map/while/body/eval_jaxpr/ppermute | solution.py:110
  3379.7 587.3 %all-reduce.7.cloned.1.call-start = ((), (), s32[]{:S(2)}) async-start(), calls=%async_computation.2 | async-start | bytes 2097152 | tf_op jit(solution)/shard_map/psum | solution.py:124
  3386.6 568.1 %collective-permute-start.6 = (bf16[1536,2,128]{2,1,0:T(2,128)(2,1)}, bf16[1536,2,128]{2,1,0:T(2,128)(2,1)}, u32[]{:S(2)}, u32[]{:S(2)}) collective-permute-start(bf16[1536,2,128]{2,1,0:T(2,128)(2,1)} %copy.118), channel_id=1, source_target_pairs={{0,1},{1,2},{2,3},{3,0},{4,5},{5,6},{6,7},{7,4},{8,9},{9,10},{10,1... | collective-permute-start | bytes 2359304 | tf_op jit(solution)/shard_map/ppermute | solution.py:120
  3393.1 561.7 %collective-permute-start.7 = (bf16[1536,2,128]{2,1,0:T(2,128)(2,1)}, bf16[1536,2,128]{2,1,0:T(2,128)(2,1)}, u32[]{:S(2)}, u32[]{:S(2)}) collective-permute-start(bf16[1536,2,128]{2,1,0:T(2,128)(2,1)} %copy.119), channel_id=1, source_target_pairs={{0,1},{1,2},{2,3},{3,0},{4,5},{5,6},{6,7},{7,4},{8,9},{9,10},{10,1... | collective-permute-start | bytes 2359304 | tf_op jit(solution)/shard_map/ppermute | solution.py:121
  (16 other events, 67.6 us)
Sparse Core Ops, SparseCore 0:
  24.0 29.1 all-gather.2
  3379.8 538.6 reduce-scatter.1
  3934.3 32.6 all-reduce.6
where the time goes:
time: 4000 us; the launch traced here: 3980 us
  starting transfers between devices  2110 us (53%)
  local copies, waits for them, and re-layouts  882 us (22%)
  waiting for transfers between devices  705 us (18%)
  matrix products  146 us (4%)
  other arithmetic  68.5 us (2%)
  loops' own time  45.9 us (1%)
    ppermute x3, starting transfers between devices, bwd_step(): dv_acc = lax.ppermute(dv_acc, 'cp', shift_pairs)  869 us
    reduce_scatter x1, waiting for transfers between devices, local_fn(): lax.psum_scatter(grad_rel, 'cp', scatter_dimension=0, tiled=False)  525 us
    ppermute x3, starting transfers between devices, bwd_step(): dk_acc = lax.ppermute(dk_acc, 'cp', shift_pairs)  489 us
    ppermute x3, starting transfers between devices, bwd_step(): k_blk = lax.ppermute(k_blk, 'cp', shift_pairs)  381 us
    ppermute x3, starting transfers between devices, fwd_step(): k_blk = lax.ppermute(k_blk, 'cp', shift_pairs)  373 us
    cond x47, local copies, waits for them, and re-layouts  362 us
    reshape x2, local copies, waits for them, and re-layouts, skew_scores(): kept_view.reshape(lead_dims + (block_len, 2 * block_len - 1))  104 us
    slice x2, local copies, waits for them, and re-layouts, skew_scores(): flat_view[..., block_len - 1:block_len - 1 + block_len * (2 * block_len -...  89 us
  transfers between devices with their start and end apart: 23, of which 17 were waited for; matrix products, arithmetic and copies ran while one was open for 12% of the time, Pallas kernels for 0%

commit v1 on v0

v1 whole, which is shorter than its diff:
```python
import functools

import jax
import jax.numpy as jnp
from jax import lax
from jax.experimental import pallas as pl
from jax.experimental.pallas import tpu as pltpu
from jax.sharding import PartitionSpec as P

TILE = 512
SUB = 128
NSUB = TILE // SUB
LOG2E = 1.4426950408889634
F32 = jnp.float32
BF16 = jnp.bfloat16


def dot(lhs, rhs):
    return jnp.dot(lhs, rhs, preferred_element_type=F32)


def sub(idx):
    return slice(idx * SUB, (idx + 1) * SUB)


def roll_left(part, flip):
    groups = []
    for start in range(0, SUB, 8):
        rows = jnp.take_along_axis(part[start:start + 8], flip, axis=0)
        rows = pltpu.roll(rows, (SUB - 8 - start) % SUB, 1, stride=1, stride_axis=0)
        groups.append(jnp.take_along_axis(rows, flip, axis=0))
    return jnp.concatenate(groups, axis=0)


def attn_kernel(num_tiles, inv_sqrt, u_ref, v_ref, own_ref, own_p_ref, cross_ref, cross_p_ref,
                rows_ref, keep_ref, send_ref, bias_ref,
                full_ref, acc_ref, kt_ref, valt_ref, relt_ref, sc_ref, rot_ref, ds_ref, dw_ref, p_ref,
                qu_ref, qv_ref, qut_ref, qvt_ref, dot_ref, max_ref, sum_ref, gu_ref, gv_ref, row_ref, in_sems, out_sems):
    step = pl.program_id(0)
    steps = pl.num_programs(0)
    dev = lax.axis_index('cp')
    chip, core = lax.div(dev, 2), lax.rem(dev, 2)
    odd = lax.rem(step, 2)
    blk = 2 * step + odd + core - 2 * odd * core
    scale = inv_sqrt * LOG2E
    block_len = own_ref.shape[1]
    k_ref, val_ref, rel_ref = full_ref.at[0], full_ref.at[1], full_ref.at[2]
    q_ref, do_ref = full_ref.at[3], full_ref.at[4]
    dk_ref, dv_ref, drel_ref = acc_ref.at[0], acc_ref.at[1], acc_ref.at[2]

    def cols(tile):
        return pl.ds(pl.multiple_of(tile * TILE, TILE), TILE)

    @pl.when(step == 0)
    def _():
        my_core = [core, 1 - core]
        my_chip = [chip, 1 - chip]
        copies = []
        for piece, src in enumerate((own_ref, own_p_ref, cross_ref, cross_p_ref)):
            block = 2 * my_chip[piece // 2] + my_core[piece % 2]
            for arr in range(5):
                at = 3 - block if arr == 2 else block
                dst = full_ref.at[arr, pl.ds(pl.multiple_of(at * block_len, block_len), block_len)]
                copies.append(pltpu.make_async_copy(src.at[arr], dst, in_sems.at[piece, arr]))
        for copy in copies:
            copy.start()
        for copy in copies:
            copy.wait()

        def prep(tile, _):
            kt_ref[:, cols(tile)] = k_ref[cols(tile), :].T
            valt_ref[:, cols(tile)] = val_ref[cols(tile), :].T
            relt_ref[:, cols(tile)] = rel_ref[cols(tile), :].T
            acc_ref[:, :, cols(tile)] = jnp.zeros((3, SUB, TILE), F32)
            return 0
        lax.fori_loop(0, num_tiles, prep, 0)
        bias_ref[...] = jnp.zeros_like(bias_ref)

    rows_at = cols(blk)
    d_out = do_ref[rows_at, :]
    q_wide = q_ref[rows_at, :].astype(F32)
    q_u = (q_wide + u_ref[...]).astype(BF16)
    q_v = (q_wide + v_ref[...]).astype(BF16)
    qu_ref[...] = q_u
    qv_ref[...] = q_v
    qut_ref[...] = q_u.T
    qvt_ref[...] = q_v.T
    dot_ref[...] = d_out.T
    max_ref[...] = jnp.full_like(max_ref, -jnp.inf)
    sum_ref[...] = jnp.zeros_like(sum_ref)
    gu_ref[...] = jnp.zeros_like(gu_ref)
    gv_ref[...] = jnp.zeros_like(gv_ref)
    lane = lax.broadcasted_iota(jnp.int32, (SUB, SUB), 1)
    row = lax.broadcasted_iota(jnp.int32, (SUB, SUB), 0)
    upper = lane > row
    flip = 7 - lax.broadcasted_iota(jnp.int32, (8, SUB), 0)
    lower = lane + row < SUB - 1
    first_rel = num_tiles - 1 - blk

    def rotate_rel(tile, slot):
        for half in range(2):
            start = pl.multiple_of(tile * TILE + half * 256, 256)
            by_offset = dot(qv_ref[...], relt_ref[:, pl.ds(start, 256)])
            for a in range(NSUB):
                for c in range(2):
                    part = by_offset[sub(a), sub(c)]
                    rot_ref[slot, sub(a), sub(half * 2 + c)] = pltpu.roll(part, 1, 1, stride=1, stride_axis=0)

    rotate_rel(first_rel, 0)

    def score_tile(tile, diag):
        left = lax.rem(tile, 2)
        right = 1 - left
        if not diag:
            rotate_rel(first_rel + tile + 1, right)
        for half in range(2):
            start = pl.multiple_of(tile * TILE + half * 256, 256)
            content = dot(qu_ref[...], kt_ref[:, pl.ds(start, 256)])
            for a in range(NSUB):
                run_max = max_ref[sub(a), :]
                for c2 in range(2):
                    c = half * 2 + c2
                    hi, lo = c - a + NSUB, c - a + NSUB - 1
                    if diag and c > a:
                        score = jnp.full((SUB, SUB), -jnp.inf, F32)
                    else:
                        low_part = rot_ref[left if lo < NSUB else right, sub(a), sub(lo % NSUB)]
                        if diag and c == a:
                            score = jnp.where(upper, -jnp.inf, content[sub(a), sub(c2)] + low_part)
                        else:
                            high_part = rot_ref[left if hi < NSUB else right, sub(a), sub(hi % NSUB)]
                            score = content[sub(a), sub(c2)] + jnp.where(upper, high_part, low_part)
                    run_max = jnp.maximum(run_max, score)
                    sc_ref[sub(a), pl.ds(pl.multiple_of(tile * TILE + c * SUB, SUB), SUB)] = score
                max_ref[sub(a), :] = run_max

    def score_body(tile, _):
        score_tile(tile, False)
        return 0

    lax.fori_loop(0, blk, score_body, 0)
    score_tile(blk, True)
    row_ref[...] = jnp.broadcast_to(jnp.max(max_ref[...], axis=1, keepdims=True) * scale, (TILE, SUB))

    def prob_body(tile, _):
        for a in range(NSUB):
            run_sum = sum_ref[sub(a), :]
            row_max = row_ref[sub(a), :]
            for c in range(NSUB):
                where = pl.ds(pl.multiple_of(tile * TILE + c * SUB, SUB), SUB)
                prob = jnp.exp2(sc_ref[sub(a), where] * scale - row_max)
                sc_ref[sub(a), where] = prob
                p_ref[sub(a), sub(c)] = prob.astype(BF16)
                run_sum = run_sum + prob
            sum_ref[sub(a), :] = run_sum
        gu_ref[...] += dot(p_ref[...], val_ref[cols(tile), :])
        return 0

    lax.fori_loop(0, blk + 1, prob_body, 0)
    inv_sum = 1.0 / jnp.sum(sum_ref[...], axis=1, keepdims=True)
    out = gu_ref[...] * inv_sum
    rows_ref[0, 0] = out.astype(BF16)
    delta = jnp.sum(out * do_ref[rows_at, :].astype(F32), axis=1, keepdims=True)
    row_ref[...] = jnp.broadcast_to(delta, (TILE, SUB))
    sum_ref[...] = jnp.broadcast_to(inv_sum, (TILE, SUB))
    gu_ref[...] = jnp.zeros_like(gu_ref)
    ds_ref[1, :, :] = jnp.zeros((TILE, TILE), F32)

    def grad_body(tile, _):
        now = lax.rem(tile, 2)
        old = 1 - now
        for half in range(2):
            start = pl.multiple_of(tile * TILE + half * 256, 256)
            d_prob = dot(do_ref[rows_at, :], valt_ref[:, pl.ds(start, 256)])
            for a in range(NSUB):
                inv = sum_ref[sub(a), :]
                shift = row_ref[sub(a), :]
                for c2 in range(2):
                    c = half * 2 + c2
                    prob = sc_ref[sub(a), pl.ds(pl.multiple_of(tile * TILE + c * SUB, SUB), SUB)] * inv
                    p_ref[sub(a), sub(c)] = prob.astype(BF16)
                    d_score = prob * (d_prob[sub(a), sub(c2)] - shift)
                    dw_ref[sub(a), sub(c)] = d_score.astype(BF16)
                    ds_ref[now, sub(a), sub(c)] = roll_left(d_score, flip)
            win = pl.ds(start, 256)
            dv_ref[:, win] += dot(dot_ref[...], p_ref[:, half * 256:half * 256 + 256])
            dk_ref[:, win] += dot(qut_ref[...], dw_ref[:, half * 256:half * 256 + 256])
        gu_ref[...] += dot(dw_ref[...], k_ref[cols(tile), :])
        for a in range(NSUB):
            for y in range(NSUB):
                c_lo = y + a - NSUB
                c_hi = c_lo + 1
                lo_part = ds_ref[now if c_lo >= 0 else old, sub(a), sub(c_lo % NSUB)]
                hi_part = ds_ref[now if c_hi >= 0 else old, sub(a), sub(c_hi % NSUB)]
                p_ref[sub(a), sub(y)] = jnp.where(lower, lo_part, hi_part).astype(BF16)
        rel_tile = first_rel + tile
        gv_ref[...] += dot(p_ref[...], rel_ref[cols(rel_tile), :])
        for half in range(2):
            start = pl.multiple_of(rel_tile * TILE + half * 256, 256)
            drel_ref[:, pl.ds(start, 256)] += dot(qvt_ref[...], p_ref[:, half * 256:half * 256 + 256])
        return 0

    lax.fori_loop(0, blk + 1, grad_body, 0)
    grad_u = gu_ref[...] * inv_sqrt
    grad_v = gv_ref[...] * inv_sqrt
    rows_ref[0, 1] = (grad_u + grad_v).astype(BF16)
    bias_ref[0:1, :] += jnp.sum(grad_u, axis=0, keepdims=True)
    bias_ref[1:2, :] += jnp.sum(grad_v, axis=0, keepdims=True)

    @pl.when(step == steps - 1)
    def _():
        copies = []
        for half in range(2):
            for to, (dst, which) in enumerate(((keep_ref, core), (send_ref, 1 - core))):
                block = 2 * half + which
                for arr in range(3):
                    at = 3 - block if arr == 2 else block
                    src = acc_ref.at[arr, :, pl.ds(pl.multiple_of(at * block_len, block_len), block_len)]
                    copies.append(pltpu.make_async_copy(src, dst.at[arr, half], out_sems.at[half, to, arr]))
        for copy in copies:
            copy.start()
        for copy in copies:
            copy.wait()


def run_attn(u_bias, v_bias, own, own_p, cross, cross_p):
    _, block_len, head_dim = own.shape
    seq_len = 4 * block_len
    num_tiles = seq_len // TILE
    steps = num_tiles // 2
    vec = pl.BlockSpec(memory_space=pltpu.VMEM)
    hbm = pl.BlockSpec(memory_space=pl.ANY)
    part = jax.ShapeDtypeStruct((3, 2, head_dim, block_len), F32)
    return pl.pallas_call(
        functools.partial(attn_kernel, num_tiles, head_dim ** -0.5),
        grid=(steps,),
        in_specs=[vec, vec, hbm, hbm, hbm, hbm],
        out_specs=[pl.BlockSpec((1, 2, TILE, head_dim), lambda i: (i, 0, 0, 0)), hbm, hbm, vec],
        scratch_shapes=[
            pltpu.VMEM((5, seq_len, head_dim), BF16),
            pltpu.VMEM((3, head_dim, seq_len), F32),
            pltpu.VMEM((head_dim, seq_len), BF16),
            pltpu.VMEM((head_dim, seq_len), BF16),
            pltpu.VMEM((head_dim, seq_len), BF16),
            pltpu.VMEM((TILE, seq_len), F32),
            pltpu.VMEM((2, TILE, TILE), F32),
            pltpu.VMEM((2, TILE, TILE), F32),
            pltpu.VMEM((TILE, TILE), BF16),
            pltpu.VMEM((TILE, TILE), BF16),
            pltpu.VMEM((TILE, head_dim), BF16),
            pltpu.VMEM((TILE, head_dim), BF16),
            pltpu.VMEM((head_dim, TILE), BF16),
            pltpu.VMEM((head_dim, TILE), BF16),
            pltpu.VMEM((head_dim, TILE), BF16),
            pltpu.VMEM((TILE, SUB), F32),
            pltpu.VMEM((TILE, SUB), F32),
            pltpu.VMEM((TILE, head_dim), F32),
            pltpu.VMEM((TILE, head_dim), F32),
            pltpu.VMEM((TILE, SUB), F32),
            pltpu.SemaphoreType.DMA((4, 5)),
            pltpu.SemaphoreType.DMA((2, 2, 3)),
        ],
        out_shape=[jax.ShapeDtypeStruct((steps, 2, TILE, head_dim), BF16), part, part, jax.ShapeDtypeStruct((2, head_dim), F32)],
        compiler_params=pltpu.CompilerParams(dimension_semantics=("arbitrary",), vmem_limit_bytes=60 * 1024 * 1024),
        name="attn_rows",
    )(u_bias, v_bias, own, own_p, cross, cross_p)


def exchange_matrix():
    row = lax.broadcasted_iota(jnp.int32, (SUB, SUB), 0)
    col = lax.broadcasted_iota(jnp.int32, (SUB, SUB), 1)
    return jnp.where(row + col == SUB - 1, 1.0, 0.0).astype(BF16)


def pack_kernel(k_ref, v_ref, q_ref, do_ref, table_ref, w_ref, own_ref, send_ref):
    chip = lax.div(lax.axis_index('cp'), 2)
    flip = exchange_matrix()
    weights = jnp.swapaxes(w_ref[...], 0, 1)

    def put(arr, at, heads):
        first = chip == 0
        own_ref[arr, at] = jnp.where(first, heads[0], heads[1])
        send_ref[arr, at] = jnp.where(first, heads[1], heads[0])

    for arr, src in ((0, k_ref), (1, v_ref), (3, q_ref), (4, do_ref)):
        put(arr, slice(None), jnp.swapaxes(src[...], 0, 1))
    chunks = table_ref.shape[0] // SUB
    both = jnp.concatenate([weights[0], weights[1]], axis=1)
    for chunk in range(chunks):
        rel = dot(table_ref[sub(chunk), :], both).astype(BF16)
        rel = dot(flip, rel).astype(BF16)
        put(2, sub(chunks - 1 - chunk), (rel[:, :SUB], rel[:, SUB:]))


def merge_kernel(inv_sqrt, keep_ref, got_ref, rows_ref, rows_p_ref, own_ref, send_ref):
    dev = lax.axis_index('cp')
    chip, core = lax.div(dev, 2), lax.rem(dev, 2)
    flip = exchange_matrix()
    block_len = keep_ref.shape[3]
    tiles = block_len // TILE

    def fill(half, out_ref):
        for arr in range(2):
            for tile in range(tiles):
                part = slice(tile * TILE, (tile + 1) * TILE)
                total = keep_ref[arr, half, :, part] + got_ref[arr, half, :, part]
                if arr == 0:
                    total = total * inv_sqrt
                out_ref[2 + arr, part] = total.astype(BF16).T
        chunks = block_len // SUB
        for chunk in range(chunks):
            total = ((keep_ref[2, half, :, sub(chunk)] + got_ref[2, half, :, sub(chunk)]) * inv_sqrt).astype(BF16)
            back = lax.dot_general(flip, total, (((1,), (1,)), ((), ())), preferred_element_type=F32)
            out_ref[4, sub(chunks - 1 - chunk)] = back.astype(BF16)
        for tile in range(tiles):
            blk = (2 * half + core) * tiles + tile
            step = lax.div(blk, 2)
            mine = lax.rem(blk + step + core, 2) == 0
            part = slice(tile * TILE, (tile + 1) * TILE)
            for arr in range(2):
                out_ref[arr, part] = jnp.where(mine, rows_ref[step, arr], rows_p_ref[step, arr])

    for half in range(2):
        @pl.when(chip == half)
        def _():
            fill(half, own_ref)

        @pl.when(chip != half)
        def _():
            fill(half, send_ref)


def unpack_kernel(own_ref, got_ref, table_ref, o_ref, dq_ref, dk_ref, dv_ref, dw_ref):
    chip = lax.div(lax.axis_index('cp'), 2)

    def heads(arr):
        own, got = own_ref[arr], got_ref[arr]
        return jnp.where(chip == 0, own, got), jnp.where(chip == 0, got, own)

    for arr, dst in enumerate((o_ref, dq_ref, dk_ref, dv_ref)):
        dst[...] = jnp.stack(heads(arr), axis=1)
    d_rel = jnp.concatenate(heads(4), axis=1)
    for part in range(table_ref.shape[1] // 256):
        at = slice(part * 256, part * 256 + 256)
        d_w = lax.dot_general(table_ref[:, at], d_rel, (((0,), (0,)), ((), ())), preferred_element_type=F32)
        dw_ref[at] = jnp.stack([d_w[:, :SUB], d_w[:, SUB:]], axis=1)


def simple_call(body, out_shape, name):
    vmem = pl.BlockSpec(memory_space=pltpu.VMEM)
    return pl.pallas_call(
        body, out_shape=out_shape, out_specs=[vmem] * len(out_shape), name=name,
        compiler_params=pltpu.CompilerParams(vmem_limit_bytes=48 * 1024 * 1024))


def solution(mesh):
    seq_spec = P('cp', 'hp', None)
    head_spec = P('hp', None)
    weight_spec = P(None, 'hp', None)
    cross_pairs = [(0, 2), (2, 0), (1, 3), (3, 1)]
    core_pairs = [(0, 1), (1, 0), (2, 3), (3, 2)]

    def local_fn(q, k, v, u_bias, v_bias, rel_table, w_rel, d_out):
        block_len, num_heads, head_dim = q.shape
        chip = lax.axis_index('cp') // 2
        five = jax.ShapeDtypeStruct((5, block_len, head_dim), BF16)
        seq = jax.ShapeDtypeStruct(q.shape, BF16)
        d_weights = jax.ShapeDtypeStruct(w_rel.shape, F32)
        own, send = simple_call(pack_kernel, [five, five], "pack")(k, v, q, d_out, rel_table, w_rel)
        cross = lax.ppermute(send, 'cp', cross_pairs)
        own_p = lax.ppermute(own, 'cp', core_pairs)
        cross_p = lax.ppermute(cross, 'cp', core_pairs)
        u_mine = lax.dynamic_slice_in_dim(u_bias, chip, 1)
        v_mine = lax.dynamic_slice_in_dim(v_bias, chip, 1)
        rows, keep, away, bias_grad = run_attn(u_mine, v_mine, own, own_p, cross, cross_p)
        rows_p = lax.ppermute(rows, 'cp', core_pairs)
        away_p = lax.ppermute(away, 'cp', core_pairs)
        merge = functools.partial(merge_kernel, head_dim ** -0.5)
        out_own, out_send = simple_call(merge, [five, five], "merge")(keep, away_p, rows, rows_p)
        got = lax.ppermute(out_send, 'cp', cross_pairs)
        out, dq, dk, dv, d_w_rel = simple_call(unpack_kernel, [seq] * 4 + [d_weights], "unpack")(out_own, got, rel_table)
        head_mask = (jnp.arange(num_heads) == chip)[:, None, None]
        bias_grad = lax.psum(jnp.where(head_mask, bias_grad[None], 0.0), 'cp')
        return out, dq, dk, dv, bias_grad[:, 0], bias_grad[:, 1], lax.psum(d_w_rel, 'cp')

    return jax.shard_map(
        local_fn,
        mesh=mesh,
        in_specs=(seq_spec, seq_spec, seq_spec, head_spec, head_spec, P('cp', None), weight_spec, seq_spec),
        out_specs=(seq_spec, seq_spec, seq_spec, seq_spec, head_spec, head_spec, weight_spec),
        check_vma=False,
    )
```

time: 4000 us -> 316 us (0.08)
  starting transfers between devices: 2110 us -> 5.56 us
  local copies, waits for them, and re-layouts: 882 us -> 12.5 us
  waiting for transfers between devices: 705 us -> 126 us
  Pallas kernels: 0 us -> 150 us
  matrix products: 146 us -> 0 us
  other arithmetic: 68.5 us -> 0.08 us
  loops' own time: 45.9 us -> 0 us
    ppermute x20 -> x6, starting transfers between devices: 2110 us -> 5.52 us  [the longest x1 3.23 us: local_fn(): cross = lax.ppermute(send, 'cp', cross_pairs)]
    reduce_scatter x1 -> x0, waiting for transfers between devices: 525 us -> none  [local_fn(): lax.psum_scatter(grad_rel, 'cp', scatter_dimension=0, tiled=False)]
    cond x50 -> x0, local copies, waits for them, and re-layouts: 379 us -> none
    pallas_call x0 -> x4, Pallas kernels: none -> 150 us  [the longest x1 119 us: run_attn(): pl.pallas_call(functools.partial(attn_kernel, num_tiles, head_dim ** (-0....]
    dot_general x13 -> x0, matrix products: 146 us -> none  [the longest x2 30.4 us: block_scores(): jnp.einsum('qhd,khd->hqk', q_u, k_blk, preferred_element_type=jnp.float32)]
    reshape x3 -> x0, local copies, waits for them, and re-layouts: 127 us -> none  [the longest x2 104 us: skew_scores(): kept_view.reshape(lead_dims + (block_len, 2 * block_len - 1))]
    slice x3 -> x0, local copies, waits for them, and re-layouts: 104 us -> none  [the longest x2 89 us: skew_scores(): flat_view[..., block_len - 1:block_len - 1 + block_len * (2 * block_len -...]
    dot_general x2 -> x0, local copies, waits for them, and re-layouts: 73.7 us -> none  [block_scores(): jnp.einsum('qhd,shd->hqs', q_v, window, preferred_element_type=jnp.float32)]
  transfers between devices with their start and end apart: 23 -> 7, of which waited for: 17 -> 5; matrix products, arithmetic and copies ran while one was open for 12% -> 0% of each run, Pallas kernels for 0% -> 0%
where the time goes in v1:
time: 316 us; the launch traced here: 315 us
  Pallas kernels  150 us (47%)
  waiting for transfers between devices  126 us (40%)
  between operations  14.1 us (4%)
  local copies, waits for them, and re-layouts  12.5 us (4%)
  blocking collectives  6.3 us (2%)
  starting transfers between devices  5.56 us (2%)
    pallas_call x1, Pallas kernels, run_attn(): pl.pallas_call(functools.partial(attn_kernel, num_tiles, head_dim ** (-0....  119 us
    ppermute x1, waiting for transfers between devices, local_fn(): got = lax.ppermute(out_send, 'cp', cross_pairs)  43.2 us
    ppermute x1, waiting for transfers between devices, local_fn(): cross = lax.ppermute(send, 'cp', cross_pairs)  42.8 us
    psum x1, waiting for transfers between devices, local_fn(): lax.psum(d_w_rel, 'cp')  27.2 us
    pallas_call x1, Pallas kernels, local_fn(): simple_call(unpack_kernel, [seq] * 4 + [d_weights], 'unpack')  17 us
    unnamed x23, local copies, waits for them, and re-layouts  11.4 us
    ppermute x1, waiting for transfers between devices, local_fn(): rows_p = lax.ppermute(rows, 'cp', core_pairs)  9.65 us
    pallas_call x1, Pallas kernels, local_fn(): simple_call(pack_kernel, [five, five], 'pack')  7.66 us
  transfers between devices with their start and end apart: 7, of which 5 were waited for; matrix products, arithmetic and copies ran while one was open for 0% of the time, Pallas kernels for 0%

profile of v1, /device:TPU:0, one launch (start us, length us, event | category | flops | bytes accessed | tf_op | source)
XLA Modules:
  0.0 315.1 jit_solution(6432418429967076683)
XLA Ops:
  7.2 0.0 all-reduce.2.cloned.1.call-start
  7.2 1.1 copy-done.2
  8.4 1.1 copy-done.3
  9.5 1.1 copy-done.4
  10.6 1.1 copy-done.5
  11.8 1.0 copy-done.6
  12.8 7.7 %pack.1 = (bf16[5,1536,128]{2,1,0:T(8,128)(2,1)S(1)}, bf16[5,1536,128]{2,1,0:T(8,128)(2,1)}) custom-call(bf16[1536,2,128]{2,1,0:T(2,128)(2,1)S(1)} %copy-done.2, bf16[1536,2,128]{2,1,0:T(2,128)(2,1)S(1)} %copy-done.3, bf16[1536,2,128]{2,1,0:T(2,128)(2,1)S(1)} %copy-done.4, bf16[1536,2,128]{2,1,0:T(2,128)(2,1)S(1)} %copy-done.5, ...), custom_call_target="tpu_custom_call" | custom-call | tf_op jit(solution)/shard_map/pack/pallas_call | solution.py:369
  20.5 3.2 %collective-permute-start.1 = (bf16[5,1536,128]{2,1,0:T(8,128)(2,1)}, bf16[5,1536,128]{2,1,0:T(8,128)(2,1)}, u32[]{:S(2)}, u32[]{:S(2)}) collective-permute-start(bf16[5,1536,128]{2,1,0:T(8,128)(2,1)} %get-tuple-element.21), channel_id=1, source_target_pairs={{0,2},{2,0},{1,3},{3,1},{4,6},{6,4},{5,7},{7,5},{8,10},{10,8},{9,1... | collective-permute-start | bytes 5898248 | tf_op jit(solution)/shard_map/ppermute | solution.py:370
  23.7 0.0 collective-permute-start
  23.7 42.8 %collective-permute-done.1.cross_ref = bf16[5,1536,128]{2,1,0:T(8,128)(2,1)} collective-permute-done((bf16[5,1536,128]{2,1,0:T(8,128)(2,1)}, bf16[5,1536,128]{2,1,0:T(8,128)(2,1)}, u32[]{:S(2)}, u32[]{:S(2)}) %collective-permute-start.1) | collective-permute-done | bytes 1966112 | tf_op jit(solution)/shard_map/ppermute | solution.py:370
  66.5 0.0 collective-permute-start.2
  66.5 0.0 copy-done.10
  66.5 0.5 constant_dynamic-slice_fusion
  67.0 0.0 collective-permute-done.own_p_ref
  67.0 3.4 %collective-permute-done.2.cross_p_ref = bf16[5,1536,128]{2,1,0:T(8,128)(2,1)} collective-permute-done((bf16[5,1536,128]{2,1,0:T(8,128)(2,1)}, bf16[5,1536,128]{2,1,0:T(8,128)(2,1)}, u32[]{:S(2)}, u32[]{:S(2)}) %collective-permute-start.2) | collective-permute-done | bytes 1966112 | tf_op jit(solution)/shard_map/ppermute | solution.py:372
  70.4 119.3 %attn_rows.1 = (bf16[6,2,512,128]{3,2,1,0:T(8,128)(2,1)}, f32[3,2,128,1536]{3,2,1,0:T(8,128)}, f32[3,2,128,1536]{3,2,1,0:T(8,128)}, f32[2,128]{1,0:T(2,128)}) custom-call(f32[1,128]{1,0:T(1,128)} %get-tuple-element.36.u_ref, f32[1,128]{1,0:T(1,128)} %get-tuple-element.35.v_ref, bf16[5,1536,128]{2,1,0:T(8,128)(2,1)} %copy-done, ...), custom_call_target="tpu_custom_call" | custom-call | tf_op jit(solution)/shard_map/attn_rows/pallas_call | solution.py:234
  189.7 0.2 collective-permute-start.3
  189.9 0.3 collective-permute-start.4
  190.3 9.6 %collective-permute-done.4.rows_p_ref = bf16[6,2,512,128]{3,2,1,0:T(8,128)(2,1)S(1)} collective-permute-done((bf16[6,2,512,128]{3,2,1,0:T(8,128)(2,1)}, bf16[6,2,512,128]{3,2,1,0:T(8,128)(2,1)S(1)}, u32[]{:S(2)}, u32[]{:S(2)}) %collective-permute-start.4) | collective-permute-done | bytes 1572896 | tf_op jit(solution)/shard_map/ppermute | solution.py:376
  199.9 0.0 collective-permute-done.3.got_ref
  199.9 2.2 copy-done.7
  202.1 1.4 copy-done.1
  203.5 6.4 %merge.1 = (bf16[5,1536,128]{2,1,0:T(8,128)(2,1)S(1)}, bf16[5,1536,128]{2,1,0:T(8,128)(2,1)}) custom-call(f32[3,2,128,1536]{3,2,1,0:T(8,128)} %get-tuple-element.22.keep_ref, f32[3,2,128,1536]{3,2,1,0:T(8,128)} %copy-done.7, bf16[6,2,512,128]{3,2,1,0:T(8,128)(2,1)S(1)} %copy-done.1, bf16[6,2,512,128]{3,2,1,0:T(8,128)(2,1)S(1)} %collective-permute-done.4.rows_p_ref), custom_call_target="tpu_custom_call" | custom-call | tf_op jit(solution)/shard_map/merge/pallas_call | solution.py:379
  209.9 1.7 collective-permute-start.5
  211.7 43.2 %collective-permute-done.5.got_ref = bf16[5,1536,128]{2,1,0:T(8,128)(2,1)S(1)} collective-permute-done((bf16[5,1536,128]{2,1,0:T(8,128)(2,1)}, bf16[5,1536,128]{2,1,0:T(8,128)(2,1)S(1)}, u32[]{:S(2)}, u32[]{:S(2)}) %collective-permute-start.5) | collective-permute-done | bytes 1966112 | tf_op jit(solution)/shard_map/ppermute | solution.py:380
  254.8 17.0 %unpack.1 = (bf16[1536,2,128]{2,1,0:T(2,128)(2,1)}, bf16[1536,2,128]{2,1,0:T(2,128)(2,1)}, bf16[1536,2,128]{2,1,0:T(2,128)(2,1)}, bf16[1536,2,128]{2,1,0:T(2,128)(2,1)}, f32[1024,2,128]{2,1,0:T(2,128)}) custom-call(bf16[5,1536,128]{2,1,0:T(8,128)(2,1)S(1)} %get-tuple-element.25.own_ref, bf16[5,1536,128]{2,1,0:T(8,128)(2,1)S(1)} %collective-permute-done.5.got_ref, ...), custom_call_target="tpu_custom_call" | custom-call | tf_op jit(solution)/shard_map/unpack/pallas_call | solution.py:381
  271.8 0.0 all-reduce.2.cloned.1.call-update
  271.9 0.1 broadcast_select_fusion
  271.9 6.3 %psum.14 = f32[2,2,128]{2,0,1:T(2,128)S(1)} all-reduce(f32[2,2,128]{2,0,1:T(2,128)S(1)} %broadcast_select_fusion), channel_id=1, replica_groups=mesh['hp'=4,'cp'=4] {'cp'}, use_global_device_ids=true, to_apply=%region_0.1 | all-reduce | flops 512 | bytes 4096 | tf_op jit(solution)/shard_map/psum | solution.py:383
  278.2 0.6 slice_bitcast_fusion
  278.8 27.2 %all-reduce.2.cloned.1.call-done = f32[1024,2,128]{2,1,0:T(2,128)} async-done(((f32[1024,2,128]{2,1,0:T(2,128)}), f32[1024,2,128]{2,1,0:T(2,128)}) %all-reduce.2.cloned.1.call-update) | async-done | bytes 1048592 | tf_op jit(solution)/shard_map/psum | solution.py:384
  306.0 2.3 copy.16
  (15 shorter events, 0.0 us)
Async XLA Ops:
  7.2 298.8 %all-reduce.2.cloned.1.call-start = ((), (), s32[]{:S(2)}) async-start(), calls=%async_computation | async-start | bytes 2097152 | tf_op jit(solution)/shard_map/psum | solution.py:384
  7.2 1.1 copy-start.2
  8.3 1.1 copy-start.3
  9.5 1.1 copy-start.4
  10.6 1.1 copy-start.5
  11.8 1.0 copy-start.6
  12.8 53.7 %copy-start.9 = (f32[2,128]{1,0:T(2,128)S(1)}, f32[2,128]{1,0:T(2,128)}, u32[]{:S(2)}) copy-start(f32[2,128]{1,0:T(2,128)} %param.12) | copy-start | bytes 3076
  12.8 53.7 %copy-start.10 = (f32[2,128]{1,0:T(2,128)S(1)}, f32[2,128]{1,0:T(2,128)}, u32[]{:S(2)}) copy-start(f32[2,128]{1,0:T(2,128)} %param.11) | copy-start | bytes 3076
  20.5 50.0 %copy-start = (bf16[5,1536,128]{2,1,0:T(8,128)(2,1)}, bf16[5,1536,128]{2,1,0:T(8,128)(2,1)S(1)}, u32[]{:S(2)}) copy-start(bf16[5,1536,128]{2,1,0:T(8,128)(2,1)S(1)} %get-tuple-element.20.own_ref) | copy-start | bytes 5898244
  20.5 46.0 %collective-permute-start.1 = (bf16[5,1536,128]{2,1,0:T(8,128)(2,1)}, bf16[5,1536,128]{2,1,0:T(8,128)(2,1)}, u32[]{:S(2)}, u32[]{:S(2)}) collective-permute-start(bf16[5,1536,128]{2,1,0:T(8,128)(2,1)} %get-tuple-element.21), channel_id=1, source_target_pairs={{0,2},{2,0},{1,3},{3,1},{4,6},{6,4},{5,7},{7,5},{8,10},{10,8},{9,1... | collective-permute-start | bytes 5898248 | tf_op jit(solution)/shard_map/ppermute | solution.py:370
  23.7 43.4 %collective-permute-start = (bf16[5,1536,128]{2,1,0:T(8,128)(2,1)S(1)}, bf16[5,1536,128]{2,1,0:T(8,128)(2,1)}, u32[]{:S(2)}, u32[]{:S(2)}) collective-permute-start(bf16[5,1536,128]{2,1,0:T(8,128)(2,1)S(1)} %get-tuple-element.20.own_ref), channel_id=1, source_target_pairs={{0,1},{1,0},{2,3},{3,2},{4,5},{5,4},{6,7},{7,6},{8,9},{9,8},{10,11... | collective-permute-start | bytes 5898248 | tf_op jit(solution)/shard_map/ppermute | solution.py:371
  66.5 3.9 %collective-permute-start.2 = (bf16[5,1536,128]{2,1,0:T(8,128)(2,1)}, bf16[5,1536,128]{2,1,0:T(8,128)(2,1)}, u32[]{:S(2)}, u32[]{:S(2)}) collective-permute-start(bf16[5,1536,128]{2,1,0:T(8,128)(2,1)} %collective-permute-done.1.cross_ref), channel_id=1, source_target_pairs={{0,1},{1,0},{2,3},{3,2},{4,5},{5,4},{6,7},{7,6},{8,9},{9,8},{10,11... | collective-permute-start | bytes 5898248 | tf_op jit(solution)/shard_map/ppermute | solution.py:372
  189.7 10.2 %collective-permute-start.3 = (f32[3,2,128,1536]{3,2,1,0:T(8,128)}, f32[3,2,128,1536]{3,2,1,0:T(8,128)S(1)}, u32[]{:S(2)}, u32[]{:S(2)}) collective-permute-start(f32[3,2,128,1536]{3,2,1,0:T(8,128)} %get-tuple-element.23), channel_id=1, source_target_pairs={{0,1},{1,0},{2,3},{3,2},{4,5},{5,4},{6,7},{7,6},{8,9},{9,8},{10,11... | collective-permute-start | bytes 14155784 | tf_op jit(solution)/shard_map/ppermute | solution.py:377
  189.9 10.0 %collective-permute-start.4 = (bf16[6,2,512,128]{3,2,1,0:T(8,128)(2,1)}, bf16[6,2,512,128]{3,2,1,0:T(8,128)(2,1)S(1)}, u32[]{:S(2)}, u32[]{:S(2)}) collective-permute-start(bf16[6,2,512,128]{3,2,1,0:T(8,128)(2,1)} %get-tuple-element.24.rows_ref), channel_id=1, source_target_pairs={{0,1},{1,0},{2,3},{3,2},{4,5},{5,4},{6,7},{7,6},{8,9},{9,8},{10,11... | collective-permute-start | bytes 4718600 | tf_op jit(solution)/shard_map/ppermute | solution.py:376
  199.9 2.2 copy-start.7
  202.1 1.4 copy-start.1
  209.9 44.9 %collective-permute-start.5 = (bf16[5,1536,128]{2,1,0:T(8,128)(2,1)}, bf16[5,1536,128]{2,1,0:T(8,128)(2,1)S(1)}, u32[]{:S(2)}, u32[]{:S(2)}) collective-permute-start(bf16[5,1536,128]{2,1,0:T(8,128)(2,1)} %get-tuple-element.26), channel_id=1, source_target_pairs={{0,2},{2,0},{1,3},{3,1},{4,6},{6,4},{5,7},{7,5},{8,10},{10,8},{9,1... | collective-permute-start | bytes 5898248 | tf_op jit(solution)/shard_map/ppermute | solution.py:380
  254.8 17.0 %copy-start.8 = (f32[2,128]{1,0:T(2,128)S(1)}, f32[2,128]{1,0:T(2,128)}, u32[]{:S(2)}) copy-start(f32[2,128]{1,0:T(2,128)} %get-tuple-element.31) | copy-start | bytes 3076
Sparse Core Ops, SparseCore 0:
  272.0 33.9 all-reduce.1

commit v2 on v1

--- a/solution.py
+++ b/solution.py
@@ -32,18 +32,25 @@
     return jnp.concatenate(groups, axis=0)
 
 
-def attn_kernel(num_tiles, inv_sqrt, u_ref, v_ref, own_ref, own_p_ref, cross_ref, cross_p_ref,
-                rows_ref, keep_ref, send_ref, bias_ref,
+def attn_kernel(num_tiles, inv_sqrt, u_ref, v_ref, own_ref, away_ref,
+                res_own_ref, res_got_ref, bias_ref,
                 full_ref, acc_ref, kt_ref, valt_ref, relt_ref, sc_ref, rot_ref, ds_ref, dw_ref, p_ref,
-                qu_ref, qv_ref, qut_ref, qvt_ref, dot_ref, max_ref, sum_ref, gu_ref, gv_ref, row_ref, in_sems, out_sems):
+                qu_ref, qv_ref, qut_ref, qvt_ref, dot_ref, max_ref, sum_ref, gu_ref, gv_ref, row_ref,
+                st_rows_ref, st_grad_ref, part_ref,
+                local_sems, own_send, own_recv, cross_send, cross_recv, fwd_send, fwd_recv,
+                part_send, part_recv, rows_send, grad_send, res_sems):
     step = pl.program_id(0)
-    steps = pl.num_programs(0)
+    last = pl.num_programs(0) - 1
     dev = lax.axis_index('cp')
     chip, core = lax.div(dev, 2), lax.rem(dev, 2)
-    odd = lax.rem(step, 2)
-    blk = 2 * step + odd + core - 2 * odd * core
+    core_peer, chip_peer = dev + 1 - 2 * core, dev + 2 - 4 * chip
+    half_steps = num_tiles // 4
+    pair = jnp.where(step < half_steps, step + half_steps * chip, (3 - chip) * half_steps - 1 - step)
+    odd = lax.rem(pair, 2)
+    blk = 2 * pair + odd + core - 2 * odd * core
     scale = inv_sqrt * LOG2E
     block_len = own_ref.shape[1]
+    block_tiles = block_len // TILE
     k_ref, val_ref, rel_ref = full_ref.at[0], full_ref.at[1], full_ref.at[2]
     q_ref, do_ref = full_ref.at[3], full_ref.at[4]
     dk_ref, dv_ref, drel_ref = acc_ref.at[0], acc_ref.at[1], acc_ref.at[2]
@@ -51,30 +58,120 @@
     def cols(tile):
         return pl.ds(pl.multiple_of(tile * TILE, TILE), TILE)
 
+    def place(arr, block):
+        at = 3 - block if arr == 2 else block
+        return full_ref.at[arr, pl.ds(pl.multiple_of(at * block_len, block_len), block_len)]
+
+    def to_device(src, dst, send_sem, recv_sem, peer):
+        return pltpu.make_async_remote_copy(
+            src_ref=src, dst_ref=dst, send_sem=send_sem, recv_sem=recv_sem,
+            device_id={'cp': peer}, device_id_type=pl.DeviceIdType.MESH)
+
+    def own_copy(arr):
+        return to_device(own_ref.at[arr], place(arr, dev), own_send.at[arr], own_recv.at[arr], core_peer)
+
+    def cross_copy(arr):
+        return to_device(away_ref.at[arr], place(arr, dev), cross_send.at[arr], cross_recv.at[arr], chip_peer)
+
+    def fwd_copy(arr):
+        return to_device(place(arr, chip_peer), place(arr, chip_peer), fwd_send.at[arr], fwd_recv.at[arr], core_peer)
+
+    def transpose_half(arr, which):
+        dst = (kt_ref, valt_ref, relt_ref)[arr]
+        first = (1 - which if arr == 2 else which) * (num_tiles // 2)
+
+        def body(idx, _):
+            dst[:, cols(first + idx)] = full_ref[arr, cols(first + idx), :].T
+            return 0
+        lax.fori_loop(0, num_tiles // 2, body, 0)
+
+    def arrive(arrays):
+        for arr in arrays:
+            cross_copy(arr).wait_recv()
+            fwd_copy(arr).start()
+        for arr in arrays:
+            fwd_copy(arr).wait_recv()
+            if arr < 3:
+                transpose_half(arr, 1 - chip)
+
+    def part_copy(slot, pair_idx, arr):
+        tile = 2 * pair_idx + 1 - core
+        at = num_tiles - 1 - tile if arr == 2 else tile
+        return to_device(acc_ref.at[arr, :, cols(at)], part_ref.at[slot, arr],
+                         part_send.at[slot, arr], part_recv.at[slot, arr], core_peer)
+
+    def start_parts(slot, pair_idx):
+        for arr in range(3):
+            part_copy(slot, pair_idx, arr).start()
+
+    def deliver(tile, stage, part, send_sem, start):
+        owner = lax.div(tile, block_tiles)
+        local = tile - owner * block_tiles
+        where = pl.ds(0, 2) if part == 0 else pl.ds(2, 3)
+
+        @pl.when(owner == dev)
+        def _():
+            if start:
+                pltpu.make_async_copy(stage, res_own_ref.at[local, where], res_sems.at[0, part, local]).start()
+
+        @pl.when(owner == core_peer)
+        def _():
+            copy = to_device(stage, res_own_ref.at[local, where], send_sem, res_sems.at[0, part, local], owner)
+            copy.start() if start else copy.wait_send()
+
+        @pl.when(lax.div(owner, 2) != chip)
+        def _():
+            copy = to_device(stage, res_got_ref.at[local, where], send_sem, res_sems.at[1, part, local], owner)
+            copy.start() if start else copy.wait_send()
+
+    def finish_parts(slot, pair_idx):
+        tile = 2 * pair_idx + core
+        for arr in range(3):
+            part_copy(slot, pair_idx, arr).wait_recv()
+        d_key = (acc_ref[0, :, cols(tile)] + part_ref[slot, 0]) * inv_sqrt
+        st_grad_ref[slot, 0] = d_key.astype(BF16).T
+        d_val = acc_ref[1, :, cols(tile)] + part_ref[slot, 1]
+        st_grad_ref[slot, 1] = d_val.astype(BF16).T
+        d_off = ((acc_ref[2, :, cols(num_tiles - 1 - tile)] + part_ref[slot, 2]) * inv_sqrt).astype(BF16)
+        flip_rows = exchange_matrix()
+        for chunk in range(NSUB):
+            back = lax.dot_general(flip_rows, d_off[:, sub(chunk)], (((1,), (1,)), ((), ())), preferred_element_type=F32)
+            st_grad_ref[slot, 2, sub(NSUB - 1 - chunk)] = back.astype(BF16)
+        deliver(tile, st_grad_ref.at[slot], 1, grad_send.at[slot], True)
+
+    def pair_of(idx):
+        return jnp.where(idx < half_steps, (2 - chip) * half_steps - 1 - idx, idx - half_steps + half_steps * chip)
+
     @pl.when(step == 0)
     def _():
-        my_core = [core, 1 - core]
-        my_chip = [chip, 1 - chip]
-        copies = []
-        for piece, src in enumerate((own_ref, own_p_ref, cross_ref, cross_p_ref)):
-            block = 2 * my_chip[piece // 2] + my_core[piece % 2]
-            for arr in range(5):
-                at = 3 - block if arr == 2 else block
-                dst = full_ref.at[arr, pl.ds(pl.multiple_of(at * block_len, block_len), block_len)]
-                copies.append(pltpu.make_async_copy(src.at[arr], dst, in_sems.at[piece, arr]))
-        for copy in copies:
-            copy.start()
-        for copy in copies:
-            copy.wait()
-
-        def prep(tile, _):
-            kt_ref[:, cols(tile)] = k_ref[cols(tile), :].T
-            valt_ref[:, cols(tile)] = val_ref[cols(tile), :].T
-            relt_ref[:, cols(tile)] = rel_ref[cols(tile), :].T
+        barrier = pltpu.get_barrier_semaphore()
+        for peer in (core_peer, chip_peer, 3 - dev):
+            pl.semaphore_signal(barrier, inc=1, device_id={'cp': peer}, device_id_type=pl.DeviceIdType.MESH)
+        pl.semaphore_wait(barrier, 3)
+        local = [pltpu.make_async_copy(own_ref.at[arr], place(arr, dev), local_sems.at[arr]) for arr in range(5)]
+        for arr in range(5):
+            cross_copy(arr).start()
+            own_copy(arr).start()
+            local[arr].start()
+
+        def clear(tile, _):
             acc_ref[:, :, cols(tile)] = jnp.zeros((3, SUB, TILE), F32)
             return 0
-        lax.fori_loop(0, num_tiles, prep, 0)
+        lax.fori_loop(0, num_tiles, clear, 0)
         bias_ref[...] = jnp.zeros_like(bias_ref)
+        for arr in range(5):
+            local[arr].wait()
+            own_copy(arr).wait_recv()
+            if arr < 3:
+                transpose_half(arr, chip)
+
+    @pl.when(step == half_steps * (1 - chip))
+    def _():
+        arrive((0, 1, 2))
+
+    @pl.when(step == half_steps)
+    def _():
+        arrive((3, 4))
 
     rows_at = cols(blk)
     d_out = do_ref[rows_at, :]
@@ -159,7 +256,7 @@
     lax.fori_loop(0, blk + 1, prob_body, 0)
     inv_sum = 1.0 / jnp.sum(sum_ref[...], axis=1, keepdims=True)
     out = gu_ref[...] * inv_sum
-    rows_ref[0, 0] = out.astype(BF16)
+    st_rows_ref[step, 0] = out.astype(BF16)
     delta = jnp.sum(out * do_ref[rows_at, :].astype(F32), axis=1, keepdims=True)
     row_ref[...] = jnp.broadcast_to(delta, (TILE, SUB))
     sum_ref[...] = jnp.broadcast_to(inv_sum, (TILE, SUB))
@@ -200,42 +297,70 @@
             drel_ref[:, pl.ds(start, 256)] += dot(qvt_ref[...], p_ref[:, half * 256:half * 256 + 256])
         return 0
 
+    @pl.when(step > half_steps)
+    def _():
+        finish_parts(step - half_steps - 1, pair_of(step - half_steps - 1))
+
     lax.fori_loop(0, blk + 1, grad_body, 0)
     grad_u = gu_ref[...] * inv_sqrt
     grad_v = gv_ref[...] * inv_sqrt
-    rows_ref[0, 1] = (grad_u + grad_v).astype(BF16)
+    st_rows_ref[step, 1] = (grad_u + grad_v).astype(BF16)
     bias_ref[0:1, :] += jnp.sum(grad_u, axis=0, keepdims=True)
     bias_ref[1:2, :] += jnp.sum(grad_v, axis=0, keepdims=True)
-
-    @pl.when(step == steps - 1)
+    deliver(blk, st_rows_ref.at[step], 0, rows_send.at[step], True)
+
+    @pl.when(step >= half_steps)
     def _():
-        copies = []
-        for half in range(2):
-            for to, (dst, which) in enumerate(((keep_ref, core), (send_ref, 1 - core))):
-                block = 2 * half + which
-                for arr in range(3):
-                    at = 3 - block if arr == 2 else block
-                    src = acc_ref.at[arr, :, pl.ds(pl.multiple_of(at * block_len, block_len), block_len)]
-                    copies.append(pltpu.make_async_copy(src, dst.at[arr, half], out_sems.at[half, to, arr]))
-        for copy in copies:
-            copy.start()
-        for copy in copies:
-            copy.wait()
-
-
-def run_attn(u_bias, v_bias, own, own_p, cross, cross_p):
+        start_parts(step - half_steps, pair)
+
+    @pl.when(step == last)
+    def _():
+        def start_rest(idx, _):
+            start_parts(idx, pair_of(idx))
+            return 0
+
+        def finish_rest(idx, _):
+            finish_parts(idx, pair_of(idx))
+            return 0
+
+        def drain(idx, _):
+            for arr in range(3):
+                part_copy(idx, pair_of(idx), arr).wait_send()
+            deliver(2 * pair_of(idx) + core, st_grad_ref.at[idx], 1, grad_send.at[idx], False)
+            pair_idx = jnp.where(idx < half_steps, idx + half_steps * chip, (3 - chip) * half_steps - 1 - idx)
+            odd_idx = lax.rem(pair_idx, 2)
+            deliver(2 * pair_idx + odd_idx + core - 2 * odd_idx * core, st_rows_ref.at[idx], 0, rows_send.at[idx], False)
+            return 0
+
+        lax.fori_loop(half_steps, 2 * half_steps, start_rest, 0)
+        lax.fori_loop(half_steps - 1, 2 * half_steps, finish_rest, 0)
+        lax.fori_loop(0, 2 * half_steps, drain, 0)
+        for arr in range(5):
+            own_copy(arr).wait_send()
+            cross_copy(arr).wait_send()
+            fwd_copy(arr).wait_send()
+        for which, res in enumerate((res_own_ref, res_got_ref)):
+            for local in range(block_tiles):
+                for part, where in enumerate((pl.ds(0, 2), pl.ds(2, 3))):
+                    dst = res.at[local, where]
+                    pltpu.make_async_copy(dst, dst, res_sems.at[which, part, local]).wait()
+
+
+def run_attn(u_bias, v_bias, own, away):
     _, block_len, head_dim = own.shape
     seq_len = 4 * block_len
     num_tiles = seq_len // TILE
     steps = num_tiles // 2
+    block_tiles = block_len // TILE
     vec = pl.BlockSpec(memory_space=pltpu.VMEM)
     hbm = pl.BlockSpec(memory_space=pl.ANY)
-    part = jax.ShapeDtypeStruct((3, 2, head_dim, block_len), F32)
+    result = jax.ShapeDtypeStruct((block_tiles, 5, TILE, head_dim), BF16)
+    dma = pltpu.SemaphoreType.DMA
     return pl.pallas_call(
         functools.partial(attn_kernel, num_tiles, head_dim ** -0.5),
         grid=(steps,),
-        in_specs=[vec, vec, hbm, hbm, hbm, hbm],
-        out_specs=[pl.BlockSpec((1, 2, TILE, head_dim), lambda i: (i, 0, 0, 0)), hbm, hbm, vec],
+        in_specs=[vec, vec, hbm, hbm],
+        out_specs=[hbm, hbm, vec],
         scratch_shapes=[
             pltpu.VMEM((5, seq_len, head_dim), BF16),
             pltpu.VMEM((3, head_dim, seq_len), F32),
@@ -257,13 +382,17 @@
             pltpu.VMEM((TILE, head_dim), F32),
             pltpu.VMEM((TILE, head_dim), F32),
             pltpu.VMEM((TILE, SUB), F32),
-            pltpu.SemaphoreType.DMA((4, 5)),
-            pltpu.SemaphoreType.DMA((2, 2, 3)),
+            pltpu.VMEM((steps, 2, TILE, head_dim), BF16),
+            pltpu.VMEM((steps, 3, TILE, head_dim), BF16),
+            pltpu.VMEM((steps, 3, head_dim, TILE), F32),
+            dma((5,)), dma((5,)), dma((5,)), dma((5,)), dma((5,)), dma((5,)), dma((5,)),
+            dma((steps, 3)), dma((steps, 3)), dma((steps,)), dma((steps,)), dma((2, 2, block_tiles)),
         ],
-        out_shape=[jax.ShapeDtypeStruct((steps, 2, TILE, head_dim), BF16), part, part, jax.ShapeDtypeStruct((2, head_dim), F32)],
-        compiler_params=pltpu.CompilerParams(dimension_semantics=("arbitrary",), vmem_limit_bytes=60 * 1024 * 1024),
+        out_shape=[result, result, jax.ShapeDtypeStruct((2, head_dim), F32)],
+        compiler_params=pltpu.CompilerParams(
+            dimension_semantics=("arbitrary",), vmem_limit_bytes=62 * 1024 * 1024, collective_id=0, has_side_effects=True),
         name="attn_rows",
-    )(u_bias, v_bias, own, own_p, cross, cross_p)
+    )(u_bias, v_bias, own, away)
 
 
 def exchange_matrix():
@@ -292,58 +421,89 @@
         put(2, sub(chunks - 1 - chunk), (rel[:, :SUB], rel[:, SUB:]))
 
 
-def merge_kernel(inv_sqrt, keep_ref, got_ref, rows_ref, rows_p_ref, own_ref, send_ref):
+def unpack_kernel(own_ref, got_ref, o_ref, dq_ref, dk_ref, dv_ref):
+    chip = lax.div(lax.axis_index('cp'), 2)
+    for tile in range(own_ref.shape[0]):
+        rows = slice(tile * TILE, (tile + 1) * TILE)
+        for arr, dst in enumerate((o_ref, dq_ref, dk_ref, dv_ref)):
+            own, got = own_ref[tile, arr], got_ref[tile, arr]
+            dst[rows] = jnp.stack([jnp.where(chip == 0, own, got), jnp.where(chip == 0, got, own)], axis=1)
+
+
+def weight_kernel(own_ref, got_ref, table_ref, bias_ref, dw_ref, du_ref, dvb_ref,
+                  part_ref, core_ref, chip_ref, sum_ref, final_ref, send_sems, recv_sems):
     dev = lax.axis_index('cp')
     chip, core = lax.div(dev, 2), lax.rem(dev, 2)
-    flip = exchange_matrix()
-    block_len = keep_ref.shape[3]
-    tiles = block_len // TILE
-
-    def fill(half, out_ref):
-        for arr in range(2):
-            for tile in range(tiles):
-                part = slice(tile * TILE, (tile + 1) * TILE)
-                total = keep_ref[arr, half, :, part] + got_ref[arr, half, :, part]
-                if arr == 0:
-                    total = total * inv_sqrt
-                out_ref[2 + arr, part] = total.astype(BF16).T
-        chunks = block_len // SUB
-        for chunk in range(chunks):
-            total = ((keep_ref[2, half, :, sub(chunk)] + got_ref[2, half, :, sub(chunk)]) * inv_sqrt).astype(BF16)
-            back = lax.dot_general(flip, total, (((1,), (1,)), ((), ())), preferred_element_type=F32)
-            out_ref[4, sub(chunks - 1 - chunk)] = back.astype(BF16)
-        for tile in range(tiles):
-            blk = (2 * half + core) * tiles + tile
-            step = lax.div(blk, 2)
-            mine = lax.rem(blk + step + core, 2) == 0
-            part = slice(tile * TILE, (tile + 1) * TILE)
-            for arr in range(2):
-                out_ref[arr, part] = jnp.where(mine, rows_ref[step, arr], rows_p_ref[step, arr])
-
-    for half in range(2):
-        @pl.when(chip == half)
-        def _():
-            fill(half, own_ref)
-
-        @pl.when(chip != half)
-        def _():
-            fill(half, send_ref)
-
-
-def unpack_kernel(own_ref, got_ref, table_ref, o_ref, dq_ref, dk_ref, dv_ref, dw_ref):
-    chip = lax.div(lax.axis_index('cp'), 2)
-
-    def heads(arr):
-        own, got = own_ref[arr], got_ref[arr]
-        return jnp.where(chip == 0, own, got), jnp.where(chip == 0, got, own)
-
-    for arr, dst in enumerate((o_ref, dq_ref, dk_ref, dv_ref)):
-        dst[...] = jnp.stack(heads(arr), axis=1)
-    d_rel = jnp.concatenate(heads(4), axis=1)
-    for part in range(table_ref.shape[1] // 256):
-        at = slice(part * 256, part * 256 + 256)
-        d_w = lax.dot_general(table_ref[:, at], d_rel, (((0,), (0,)), ((), ())), preferred_element_type=F32)
-        dw_ref[at] = jnp.stack([d_w[:, :SUB], d_w[:, SUB:]], axis=1)
+    core_peer, chip_peer = dev + 1 - 2 * core, dev + 2 - 4 * chip
+    barrier = pltpu.get_barrier_semaphore()
+    for peer in (core_peer, chip_peer):
+        pl.semaphore_signal(barrier, inc=1, device_id={'cp': peer}, device_id_type=pl.DeviceIdType.MESH)
+    pl.semaphore_wait(barrier, 2)
+    own = jnp.concatenate([own_ref[tile, 4] for tile in range(own_ref.shape[0])], axis=0)
+    got = jnp.concatenate([got_ref[tile, 4] for tile in range(got_ref.shape[0])], axis=0)
+    d_rel = jnp.concatenate([jnp.where(chip == 0, own, got), jnp.where(chip == 0, got, own)], axis=1)
+    model_dim = table_ref.shape[1]
+    half_rows = part_ref.shape[1]
+    flat = part_ref.shape[0] * half_rows
+    for start in range(0, flat, 256):
+        size = min(256, model_dim - start) if start < model_dim else 0
+        rows = []
+        if size > 0:
+            rows.append(lax.dot_general(table_ref[:, start:start + size], d_rel, (((0,), (0,)), ((), ())), preferred_element_type=F32))
+        else:
+            bias = bias_ref[...]
+            zero = jnp.zeros_like(bias)
+            both = jnp.concatenate([jnp.where(chip == 0, bias, zero), jnp.where(chip == 0, zero, bias)], axis=1)
+            rows.append(jnp.concatenate([both, jnp.zeros((flat - start - bias.shape[0], both.shape[1]), F32)], axis=0))
+        block = rows[0]
+        for at in range(0, block.shape[0], 8):
+            pos = start + at
+            part_ref[pos // half_rows, pos % half_rows:pos % half_rows + 8] = block[at:at + 8]
+
+    def swap(idx, src, dst, peer):
+        copy = pltpu.make_async_remote_copy(
+            src_ref=src, dst_ref=dst, send_sem=send_sems.at[idx], recv_sem=recv_sems.at[idx],
+            device_id={'cp': peer}, device_id_type=pl.DeviceIdType.MESH)
+        copy.start()
+        return copy
+
+    first = swap(0, part_ref.at[1 - core], core_ref, core_peer)
+    first.wait()
+    sum_ref[...] = part_ref[core] + core_ref[...]
+    second = swap(1, sum_ref, chip_ref, chip_peer)
+    second.wait()
+    final_ref[core] = sum_ref[...] + chip_ref[...]
+    third = swap(2, final_ref.at[core], final_ref.at[core], core_peer)
+    third.wait()
+    total = jnp.concatenate([final_ref[0], final_ref[1]], axis=0)
+    dw_ref[...] = jnp.stack([total[:model_dim, :SUB], total[:model_dim, SUB:]], axis=1)
+    du_ref[...] = jnp.concatenate([total[model_dim:model_dim + 1, :SUB], total[model_dim:model_dim + 1, SUB:]], axis=0)
+    dvb_ref[...] = jnp.concatenate([total[model_dim + 1:model_dim + 2, :SUB], total[model_dim + 1:model_dim + 2, SUB:]], axis=0)
+
+
+def weight_grad(own, got, rel_table, bias_grad, w_shape):
+    model_dim = w_shape[0]
+    half_rows = model_dim // 2 + 8
+    wide = 2 * SUB
+    vmem = pl.BlockSpec(memory_space=pltpu.VMEM)
+    bias = jax.ShapeDtypeStruct((2, SUB), F32)
+    return pl.pallas_call(
+        weight_kernel,
+        in_specs=[vmem] * 4,
+        out_specs=[vmem] * 3,
+        out_shape=[jax.ShapeDtypeStruct(w_shape, F32), bias, bias],
+        scratch_shapes=[
+            pltpu.VMEM((2, half_rows, wide), F32),
+            pltpu.VMEM((half_rows, wide), F32),
+            pltpu.VMEM((half_rows, wide), F32),
+            pltpu.VMEM((half_rows, wide), F32),
+            pltpu.VMEM((2, half_rows, wide), F32),
+            pltpu.SemaphoreType.DMA((3,)),
+            pltpu.SemaphoreType.DMA((3,)),
+        ],
+        compiler_params=pltpu.CompilerParams(vmem_limit_bytes=48 * 1024 * 1024, collective_id=1, has_side_effects=True),
+        name="weight_grad",
+    )(own, got, rel_table, bias_grad)
 
 
 def simple_call(body, out_shape, name):
@@ -357,31 +517,19 @@
     seq_spec = P('cp', 'hp', None)
     head_spec = P('hp', None)
     weight_spec = P(None, 'hp', None)
-    cross_pairs = [(0, 2), (2, 0), (1, 3), (3, 1)]
-    core_pairs = [(0, 1), (1, 0), (2, 3), (3, 2)]
 
     def local_fn(q, k, v, u_bias, v_bias, rel_table, w_rel, d_out):
-        block_len, num_heads, head_dim = q.shape
+        block_len, _, head_dim = q.shape
         chip = lax.axis_index('cp') // 2
         five = jax.ShapeDtypeStruct((5, block_len, head_dim), BF16)
         seq = jax.ShapeDtypeStruct(q.shape, BF16)
-        d_weights = jax.ShapeDtypeStruct(w_rel.shape, F32)
-        own, send = simple_call(pack_kernel, [five, five], "pack")(k, v, q, d_out, rel_table, w_rel)
-        cross = lax.ppermute(send, 'cp', cross_pairs)
-        own_p = lax.ppermute(own, 'cp', core_pairs)
-        cross_p = lax.ppermute(cross, 'cp', core_pairs)
+        own, away = simple_call(pack_kernel, [five, five], "pack")(k, v, q, d_out, rel_table, w_rel)
         u_mine = lax.dynamic_slice_in_dim(u_bias, chip, 1)
         v_mine = lax.dynamic_slice_in_dim(v_bias, chip, 1)
-        rows, keep, away, bias_grad = run_attn(u_mine, v_mine, own, own_p, cross, cross_p)
-        rows_p = lax.ppermute(rows, 'cp', core_pairs)
-        away_p = lax.ppermute(away, 'cp', core_pairs)
-        merge = functools.partial(merge_kernel, head_dim ** -0.5)
-        out_own, out_send = simple_call(merge, [five, five], "merge")(keep, away_p, rows, rows_p)
-        got = lax.ppermute(out_send, 'cp', cross_pairs)
-        out, dq, dk, dv, d_w_rel = simple_call(unpack_kernel, [seq] * 4 + [d_weights], "unpack")(out_own, got, rel_table)
-        head_mask = (jnp.arange(num_heads) == chip)[:, None, None]
-        bias_grad = lax.psum(jnp.where(head_mask, bias_grad[None], 0.0), 'cp')
-        return out, dq, dk, dv, bias_grad[:, 0], bias_grad[:, 1], lax.psum(d_w_rel, 'cp')
+        res_own, res_got, bias_grad = run_attn(u_mine, v_mine, own, away)
+        d_w_rel, d_u, d_v = weight_grad(res_own, res_got, rel_table, bias_grad, w_rel.shape)
+        out, dq, dk, dv = simple_call(unpack_kernel, [seq] * 4, "unpack")(res_own, res_got)
+        return out, dq, dk, dv, d_u, d_v, d_w_rel
 
     return jax.shard_map(
         local_fn,

time: 316 us -> 227 us (0.72)
  waiting for transfers between devices: 126 us -> 0 us
  Pallas kernels: 150 us -> 212 us
  between operations: 14.1 us -> 0.69 us
  blocking collectives: 6.3 us -> 0 us
  starting transfers between devices: 5.56 us -> 0 us
    ppermute x6 -> x0, waiting for transfers between devices: 99 us -> none  [the longest x1 43.2 us: local_fn(): got = lax.ppermute(out_send, 'cp', cross_pairs)]
    pallas_call x1, Pallas kernels: 119 us -> 176 us  [run_attn(): pl.pallas_call(functools.partial(attn_kernel, num_tiles, head_dim ** (-0....]
    psum x1 -> x0, waiting for transfers between devices: 27.2 us -> none  [local_fn(): lax.psum(d_w_rel, 'cp')]
    psum x1 -> x0, blocking collectives: 6.3 us -> none  [local_fn(): bias_grad = lax.psum(jnp.where(head_mask, bias_grad[None], 0.0), 'cp')]
    ppermute x6 -> x0, starting transfers between devices: 5.52 us -> none  [the longest x1 3.23 us: local_fn(): cross = lax.ppermute(send, 'cp', cross_pairs)]
    pallas_call x2, Pallas kernels: 23.4 us -> 28.7 us  [the longest x1 21.5 us: weight_grad(): pl.pallas_call(weight_kernel, in_specs=[vmem] * 4, out_specs=[vmem] * 3,...]
    unnamed x23 -> x21, local copies, waits for them, and re-layouts: 11.4 us -> 12.6 us
  transfers between devices with their start and end apart: 7 -> 0, of which waited for: 5 -> 0; matrix products, arithmetic and copies ran while one was open for 0% -> 0% of each run, Pallas kernels for 0% -> 0%
where the time goes in v2:
time: 227 us; the launch traced here: 226 us
  Pallas kernels  212 us (93%)
  local copies, waits for them, and re-layouts  13.9 us (6%)
    pallas_call x1, Pallas kernels, run_attn(): pl.pallas_call(functools.partial(attn_kernel, num_tiles, head_dim ** (-0....  176 us
    pallas_call x1, Pallas kernels, weight_grad(): pl.pallas_call(weight_kernel, in_specs=[vmem] * 4, out_specs=[vmem] * 3,...  21.5 us
    unnamed x21, local copies, waits for them, and re-layouts  12.6 us
    pallas_call x1, Pallas kernels, local_fn(): simple_call(pack_kernel, [five, five], 'pack')  7.64 us
    pallas_call x1, Pallas kernels, local_fn(): simple_call(unpack_kernel, [seq] * 4, 'unpack')(res_own, res_got)  7.16 us

profile of v2, /device:TPU:0, one launch (start us, length us, event | category | flops | bytes accessed | tf_op | source)
XLA Modules:
  0.0 226.5 jit_solution(6490257356022921256)
XLA Ops:
  0.6 1.2 constant_dynamic-slice_fusion
  1.9 0.0 copy-start.3
  1.9 1.1 copy-done.3
  3.0 0.0 copy-start.4
  3.0 1.1 copy-done.4
  4.1 0.0 copy-start.5
  4.1 1.1 copy-done.5
  5.3 0.0 copy-start.6
  5.3 1.1 copy-done.6
  6.4 0.0 copy-start.7
  6.4 1.0 copy-done.7
  7.4 7.6 %pack.1 = (bf16[5,1536,128]{2,1,0:T(8,128)(2,1)S(1)}, bf16[5,1536,128]{2,1,0:T(8,128)(2,1)}) custom-call(bf16[1536,2,128]{2,1,0:T(2,128)(2,1)S(1)} %copy-done.3, bf16[1536,2,128]{2,1,0:T(2,128)(2,1)S(1)} %copy-done.4, bf16[1536,2,128]{2,1,0:T(2,128)(2,1)S(1)} %copy-done.5, bf16[1536,2,128]{2,1,0:T(2,128)(2,1)S(1)} %copy-done.6, ...), custom_call_target="tpu_custom_call" | custom-call | tf_op jit(solution)/shard_map/pack/pallas_call | solution.py:526
  15.1 0.0 copy-start.2
  15.1 1.3 copy-done.2
  16.3 175.6 %attn_rows.1 = (bf16[3,5,512,128]{3,2,1,0:T(8,128)(2,1)}, bf16[3,5,512,128]{3,2,1,0:T(8,128)(2,1)}, f32[2,128]{1,0:T(2,128)}) custom-call(f32[1,128]{1,0:T(1,128)} %get-tuple-element.32.u_ref, f32[1,128]{1,0:T(1,128)} %get-tuple-element.31.v_ref, bf16[5,1536,128]{2,1,0:T(8,128)(2,1)} %copy-done.2, bf16[5,1536,128]{2,1,0:T(8,128)(2,1)} %get-tuple-element.20.away_ref), custom_call_target="tpu_custom_call" | custom-call | tf_op jit(solution)/shard_map/attn_rows/pallas_call | solution.py:359
  191.9 0.0 copy-start
  191.9 1.5 copy-done
  193.5 0.0 copy-start.1
  193.5 1.5 copy-done.1
  195.0 0.0 copy-start.8
  195.0 0.6 copy-done.8
  195.6 21.5 %weight_grad.1 = (f32[1024,2,128]{2,1,0:T(2,128)S(1)}, f32[2,128]{1,0:T(2,128)S(1)}, f32[2,128]{1,0:T(2,128)S(1)}) custom-call(bf16[3,5,512,128]{3,2,1,0:T(8,128)(2,1)S(1)} %copy-done, bf16[3,5,512,128]{3,2,1,0:T(8,128)(2,1)S(1)} %copy-done.1, bf16[1536,1024]{1,0:T(8,128)(2,1)} %table_ref.3, f32[2,128]{1,0:T(2,128)S(1)} %copy-done.8), custom_call_target="tpu_custom_call" | custom-call | tf_op jit(solution)/shard_map/weight_grad/pallas_call | solution.py:490
  217.2 7.2 %unpack.1 = (bf16[1536,2,128]{2,1,0:T(2,128)(2,1)}, bf16[1536,2,128]{2,1,0:T(2,128)(2,1)}, bf16[1536,2,128]{2,1,0:T(2,128)(2,1)}, bf16[1536,2,128]{2,1,0:T(2,128)(2,1)}) custom-call(bf16[3,5,512,128]{3,2,1,0:T(8,128)(2,1)S(1)} %copy-done, bf16[3,5,512,128]{3,2,1,0:T(8,128)(2,1)S(1)} %copy-done.1), custom_call_target="tpu_custom_call" | custom-call | tf_op jit(solution)/shard_map/unpack/pallas_call | solution.py:531
  224.4 0.6 copy.18
  224.9 0.6 copy.19
  225.5 1.0 copy.20
Async XLA Ops:
  1.9 1.1 copy-start.3
  3.0 1.1 copy-start.4
  4.1 1.1 copy-start.5
  5.3 1.1 copy-start.6
  6.4 1.0 copy-start.7
  15.1 1.3 copy-start.2
  191.9 1.5 copy-start
  193.5 1.5 copy-start.1
  195.0 0.6 copy-start.8

commit v3 on v2

--- a/solution.py
+++ b/solution.py
@@ -10,6 +10,7 @@
 TILE = 512
 SUB = 128
 NSUB = TILE // SUB
+MROWS = 2
 LOG2E = 1.4426950408889634
 F32 = jnp.float32
 BF16 = jnp.bfloat16
@@ -32,11 +33,11 @@
     return jnp.concatenate(groups, axis=0)
 
 
-def attn_kernel(num_tiles, inv_sqrt, u_ref, v_ref, own_ref, away_ref,
+def attn_kernel(num_tiles, inv_sqrt, u_ref, v_ref, kin_ref, vin_ref, qin_ref, doin_ref, table_in_ref, w_in_ref,
                 res_own_ref, res_got_ref, bias_ref,
                 full_ref, acc_ref, kt_ref, valt_ref, relt_ref, sc_ref, rot_ref, ds_ref, dw_ref, p_ref,
                 qu_ref, qv_ref, qut_ref, qvt_ref, dot_ref, max_ref, sum_ref, gu_ref, gv_ref, row_ref,
-                st_rows_ref, st_grad_ref, part_ref,
+                st_rows_ref, st_grad_ref, part_ref, away_ref, raw_ref, table_ref, w_ref, wide_ref,
                 local_sems, own_send, own_recv, cross_send, cross_recv, fwd_send, fwd_recv,
                 part_send, part_recv, rows_send, grad_send, res_sems):
     step = pl.program_id(0)
@@ -49,7 +50,7 @@
     odd = lax.rem(pair, 2)
     blk = 2 * pair + odd + core - 2 * odd * core
     scale = inv_sqrt * LOG2E
-    block_len = own_ref.shape[1]
+    block_len = away_ref.shape[1]
     block_tiles = block_len // TILE
     k_ref, val_ref, rel_ref = full_ref.at[0], full_ref.at[1], full_ref.at[2]
     q_ref, do_ref = full_ref.at[3], full_ref.at[4]
@@ -68,7 +69,7 @@
             device_id={'cp': peer}, device_id_type=pl.DeviceIdType.MESH)
 
     def own_copy(arr):
-        return to_device(own_ref.at[arr], place(arr, dev), own_send.at[arr], own_recv.at[arr], core_peer)
+        return to_device(place(arr, dev), place(arr, dev), own_send.at[arr], own_recv.at[arr], core_peer)
 
     def cross_copy(arr):
         return to_device(away_ref.at[arr], place(arr, dev), cross_send.at[arr], cross_recv.at[arr], chip_peer)
@@ -142,32 +143,75 @@
     def pair_of(idx):
         return jnp.where(idx < half_steps, (2 - chip) * half_steps - 1 - idx, idx - half_steps + half_steps * chip)
 
+    def put_heads(arr, start, size, first, second):
+        at = 3 - dev if arr == 2 else dev
+        own_at = pl.ds(pl.multiple_of(at * block_len + start, SUB), size)
+        away_at = pl.ds(pl.multiple_of(start, SUB), size)
+        full_ref[arr, own_at] = jnp.where(chip == 0, first, second)
+        away_ref[arr, away_at] = jnp.where(chip == 0, second, first)
+
+    def pack_seq(arr, src):
+        def body(idx, _):
+            heads = jnp.swapaxes(raw_ref[src, cols(idx)], 0, 1)
+            put_heads(arr, idx * TILE, TILE, heads[0], heads[1])
+            return 0
+        lax.fori_loop(0, block_tiles, body, 0)
+
+    def pack_rel():
+        weights = jnp.swapaxes(w_ref[...], 0, 1)
+        wide_ref[:, :SUB] = weights[0]
+        wide_ref[:, SUB:] = weights[1]
+
+        def body(idx, _):
+            rel = dot(table_ref[cols(idx), :], wide_ref[...]).astype(BF16)
+            flip_rows = exchange_matrix()
+            for chunk in range(NSUB):
+                back = dot(flip_rows, rel[sub(NSUB - 1 - chunk)]).astype(BF16)
+                put_heads(2, (block_tiles - 1 - idx) * TILE + chunk * SUB, SUB, back[:, :SUB], back[:, SUB:])
+            return 0
+        lax.fori_loop(0, block_tiles, body, 0)
+
     @pl.when(step == 0)
     def _():
         barrier = pltpu.get_barrier_semaphore()
         for peer in (core_peer, chip_peer, 3 - dev):
             pl.semaphore_signal(barrier, inc=1, device_id={'cp': peer}, device_id_type=pl.DeviceIdType.MESH)
-        pl.semaphore_wait(barrier, 3)
-        local = [pltpu.make_async_copy(own_ref.at[arr], place(arr, dev), local_sems.at[arr]) for arr in range(5)]
-        for arr in range(5):
+        loads = [pltpu.make_async_copy(src, dst, local_sems.at[idx]) for idx, (src, dst) in enumerate((
+            (kin_ref, raw_ref.at[0]), (w_in_ref, w_ref), (table_in_ref, table_ref),
+            (vin_ref, raw_ref.at[1]), (qin_ref, raw_ref.at[2]), (doin_ref, raw_ref.at[3])))]
+        for load in loads:
+            load.start()
+
+        def clear(tile, _):
+            acc_ref[:, :, cols(tile)] = jnp.zeros((3, SUB, TILE), F32)
+            return 0
+
+        def ship(arr):
             cross_copy(arr).start()
             own_copy(arr).start()
-            local[arr].start()
-
-        def clear(tile, _):
-            acc_ref[:, :, cols(tile)] = jnp.zeros((3, SUB, TILE), F32)
-            return 0
+
+        loads[0].wait()
+        pack_seq(0, 0)
+        pl.semaphore_wait(barrier, 3)
+        ship(0)
+        loads[1].wait()
+        loads[2].wait()
+        pack_rel()
+        ship(2)
+        for idx, arr in enumerate((1, 3, 4)):
+            loads[3 + idx].wait()
+            pack_seq(arr, idx + 1)
+            ship(arr)
         lax.fori_loop(0, num_tiles, clear, 0)
         bias_ref[...] = jnp.zeros_like(bias_ref)
-        for arr in range(5):
-            local[arr].wait()
+        for arr in (0, 2, 1, 3, 4):
             own_copy(arr).wait_recv()
             if arr < 3:
                 transpose_half(arr, chip)
 
     @pl.when(step == half_steps * (1 - chip))
     def _():
-        arrive((0, 1, 2))
+        arrive((0, 2))
 
     @pl.when(step == half_steps)
     def _():
@@ -197,23 +241,27 @@
     def rotate_rel(tile, slot):
         for half in range(2):
             start = pl.multiple_of(tile * TILE + half * 256, 256)
-            by_offset = dot(qv_ref[...], relt_ref[:, pl.ds(start, 256)])
             for a in range(NSUB):
+                if a % MROWS == 0:
+                    by_offset = dot(qv_ref[a * SUB:(a + MROWS) * SUB, :], relt_ref[:, pl.ds(start, 256)])
                 for c in range(2):
-                    part = by_offset[sub(a), sub(c)]
+                    part = by_offset[sub(a % MROWS), sub(c)]
                     rot_ref[slot, sub(a), sub(half * 2 + c)] = pltpu.roll(part, 1, 1, stride=1, stride_axis=0)
 
     rotate_rel(first_rel, 0)
 
+    @pl.when(blk > 0)
+    def _():
+        rotate_rel(first_rel + 1, 1)
+
     def score_tile(tile, diag):
-        left = lax.rem(tile, 2)
-        right = 1 - left
-        if not diag:
-            rotate_rel(first_rel + tile + 1, right)
+        left = lax.rem(tile, 3)
+        right = lax.rem(tile + 1, 3)
         for half in range(2):
             start = pl.multiple_of(tile * TILE + half * 256, 256)
-            content = dot(qu_ref[...], kt_ref[:, pl.ds(start, 256)])
             for a in range(NSUB):
+                if a % MROWS == 0:
+                    content = dot(qu_ref[a * SUB:(a + MROWS) * SUB, :], kt_ref[:, pl.ds(start, 256)])
                 run_max = max_ref[sub(a), :]
                 for c2 in range(2):
                     c = half * 2 + c2
@@ -223,13 +271,15 @@
                     else:
                         low_part = rot_ref[left if lo < NSUB else right, sub(a), sub(lo % NSUB)]
                         if diag and c == a:
-                            score = jnp.where(upper, -jnp.inf, content[sub(a), sub(c2)] + low_part)
+                            score = jnp.where(upper, -jnp.inf, (content[sub(a % MROWS), sub(c2)] + low_part) * scale)
                         else:
                             high_part = rot_ref[left if hi < NSUB else right, sub(a), sub(hi % NSUB)]
-                            score = content[sub(a), sub(c2)] + jnp.where(upper, high_part, low_part)
+                            score = (content[sub(a % MROWS), sub(c2)] + jnp.where(upper, high_part, low_part)) * scale
                     run_max = jnp.maximum(run_max, score)
                     sc_ref[sub(a), pl.ds(pl.multiple_of(tile * TILE + c * SUB, SUB), SUB)] = score
                 max_ref[sub(a), :] = run_max
+        if not diag:
+            rotate_rel(jnp.minimum(first_rel + tile + 2, num_tiles - 1), lax.rem(tile + 2, 3))
 
     def score_body(tile, _):
         score_tile(tile, False)
@@ -237,16 +287,19 @@
 
     lax.fori_loop(0, blk, score_body, 0)
     score_tile(blk, True)
-    row_ref[...] = jnp.broadcast_to(jnp.max(max_ref[...], axis=1, keepdims=True) * scale, (TILE, SUB))
+    max_ref[...] = jnp.broadcast_to(jnp.max(max_ref[...], axis=1, keepdims=True), (TILE, SUB))
+
+    @pl.when(step == half_steps * (1 - chip))
+    def _():
+        arrive((1,))
 
     def prob_body(tile, _):
         for a in range(NSUB):
             run_sum = sum_ref[sub(a), :]
-            row_max = row_ref[sub(a), :]
+            row_max = max_ref[sub(a), :]
             for c in range(NSUB):
                 where = pl.ds(pl.multiple_of(tile * TILE + c * SUB, SUB), SUB)
-                prob = jnp.exp2(sc_ref[sub(a), where] * scale - row_max)
-                sc_ref[sub(a), where] = prob
+                prob = jnp.exp2(sc_ref[sub(a), where] - row_max)
                 p_ref[sub(a), sub(c)] = prob.astype(BF16)
                 run_sum = run_sum + prob
             sum_ref[sub(a), :] = run_sum
@@ -254,12 +307,13 @@
         return 0
 
     lax.fori_loop(0, blk + 1, prob_body, 0)
-    inv_sum = 1.0 / jnp.sum(sum_ref[...], axis=1, keepdims=True)
+    total = jnp.sum(sum_ref[...], axis=1, keepdims=True)
+    inv_sum = 1.0 / total
     out = gu_ref[...] * inv_sum
     st_rows_ref[step, 0] = out.astype(BF16)
     delta = jnp.sum(out * do_ref[rows_at, :].astype(F32), axis=1, keepdims=True)
     row_ref[...] = jnp.broadcast_to(delta, (TILE, SUB))
-    sum_ref[...] = jnp.broadcast_to(inv_sum, (TILE, SUB))
+    sum_ref[...] = max_ref[...] + jnp.log2(total)
     gu_ref[...] = jnp.zeros_like(gu_ref)
     ds_ref[1, :, :] = jnp.zeros((TILE, TILE), F32)
 
@@ -268,15 +322,17 @@
         old = 1 - now
         for half in range(2):
             start = pl.multiple_of(tile * TILE + half * 256, 256)
-            d_prob = dot(do_ref[rows_at, :], valt_ref[:, pl.ds(start, 256)])
             for a in range(NSUB):
-                inv = sum_ref[sub(a), :]
+                if a % MROWS == 0:
+                    do_rows = pl.ds(pl.multiple_of(blk * TILE + a * SUB, SUB), MROWS * SUB)
+                    d_prob = dot(do_ref[do_rows, :], valt_ref[:, pl.ds(start, 256)])
+                log_norm = sum_ref[sub(a), :]
                 shift = row_ref[sub(a), :]
                 for c2 in range(2):
                     c = half * 2 + c2
-                    prob = sc_ref[sub(a), pl.ds(pl.multiple_of(tile * TILE + c * SUB, SUB), SUB)] * inv
+                    prob = jnp.exp2(sc_ref[sub(a), pl.ds(pl.multiple_of(tile * TILE + c * SUB, SUB), SUB)] - log_norm)
                     p_ref[sub(a), sub(c)] = prob.astype(BF16)
-                    d_score = prob * (d_prob[sub(a), sub(c2)] - shift)
+                    d_score = prob * (d_prob[sub(a % MROWS), sub(c2)] - shift)
                     dw_ref[sub(a), sub(c)] = d_score.astype(BF16)
                     ds_ref[now, sub(a), sub(c)] = roll_left(d_score, flip)
             win = pl.ds(start, 256)
@@ -346,8 +402,8 @@
                     pltpu.make_async_copy(dst, dst, res_sems.at[which, part, local]).wait()
 
 
-def run_attn(u_bias, v_bias, own, away):
-    _, block_len, head_dim = own.shape
+def run_attn(u_bias, v_bias, k, v, q, d_out, rel_table, w_rel):
+    block_len, _, head_dim = k.shape
     seq_len = 4 * block_len
     num_tiles = seq_len // TILE
     steps = num_tiles // 2
@@ -359,7 +415,7 @@
     return pl.pallas_call(
         functools.partial(attn_kernel, num_tiles, head_dim ** -0.5),
         grid=(steps,),
-        in_specs=[vec, vec, hbm, hbm],
+        in_specs=[vec, vec] + [hbm] * 6,
         out_specs=[hbm, hbm, vec],
         scratch_shapes=[
             pltpu.VMEM((5, seq_len, head_dim), BF16),
@@ -368,7 +424,7 @@
             pltpu.VMEM((head_dim, seq_len), BF16),
             pltpu.VMEM((head_dim, seq_len), BF16),
             pltpu.VMEM((TILE, seq_len), F32),
-            pltpu.VMEM((2, TILE, TILE), F32),
+            pltpu.VMEM((3, TILE, TILE), F32),
             pltpu.VMEM((2, TILE, TILE), F32),
             pltpu.VMEM((TILE, TILE), BF16),
             pltpu.VMEM((TILE, TILE), BF16),
@@ -385,14 +441,19 @@
             pltpu.VMEM((steps, 2, TILE, head_dim), BF16),
             pltpu.VMEM((steps, 3, TILE, head_dim), BF16),
             pltpu.VMEM((steps, 3, head_dim, TILE), F32),
-            dma((5,)), dma((5,)), dma((5,)), dma((5,)), dma((5,)), dma((5,)), dma((5,)),
+            pltpu.VMEM((5, block_len, head_dim), BF16),
+            pltpu.VMEM((4,) + k.shape, BF16),
+            pltpu.VMEM(rel_table.shape, BF16),
+            pltpu.VMEM(w_rel.shape, BF16),
+            pltpu.VMEM((w_rel.shape[0], 2 * head_dim), BF16),
+            dma((6,)), dma((5,)), dma((5,)), dma((5,)), dma((5,)), dma((5,)), dma((5,)),
             dma((steps, 3)), dma((steps, 3)), dma((steps,)), dma((steps,)), dma((2, 2, block_tiles)),
         ],
         out_shape=[result, result, jax.ShapeDtypeStruct((2, head_dim), F32)],
         compiler_params=pltpu.CompilerParams(
-            dimension_semantics=("arbitrary",), vmem_limit_bytes=62 * 1024 * 1024, collective_id=0, has_side_effects=True),
+            dimension_semantics=("arbitrary",), vmem_limit_bytes=67043328, collective_id=0, has_side_effects=True),
         name="attn_rows",
-    )(u_bias, v_bias, own, away)
+    )(u_bias, v_bias, k, v, q, d_out, rel_table, w_rel)
 
 
 def exchange_matrix():
@@ -401,64 +462,34 @@
     return jnp.where(row + col == SUB - 1, 1.0, 0.0).astype(BF16)
 
 
-def pack_kernel(k_ref, v_ref, q_ref, do_ref, table_ref, w_ref, own_ref, send_ref):
-    chip = lax.div(lax.axis_index('cp'), 2)
-    flip = exchange_matrix()
-    weights = jnp.swapaxes(w_ref[...], 0, 1)
-
-    def put(arr, at, heads):
-        first = chip == 0
-        own_ref[arr, at] = jnp.where(first, heads[0], heads[1])
-        send_ref[arr, at] = jnp.where(first, heads[1], heads[0])
-
-    for arr, src in ((0, k_ref), (1, v_ref), (3, q_ref), (4, do_ref)):
-        put(arr, slice(None), jnp.swapaxes(src[...], 0, 1))
-    chunks = table_ref.shape[0] // SUB
-    both = jnp.concatenate([weights[0], weights[1]], axis=1)
-    for chunk in range(chunks):
-        rel = dot(table_ref[sub(chunk), :], both).astype(BF16)
-        rel = dot(flip, rel).astype(BF16)
-        put(2, sub(chunks - 1 - chunk), (rel[:, :SUB], rel[:, SUB:]))
-
-
-def unpack_kernel(own_ref, got_ref, o_ref, dq_ref, dk_ref, dv_ref):
-    chip = lax.div(lax.axis_index('cp'), 2)
-    for tile in range(own_ref.shape[0]):
-        rows = slice(tile * TILE, (tile + 1) * TILE)
-        for arr, dst in enumerate((o_ref, dq_ref, dk_ref, dv_ref)):
-            own, got = own_ref[tile, arr], got_ref[tile, arr]
-            dst[rows] = jnp.stack([jnp.where(chip == 0, own, got), jnp.where(chip == 0, got, own)], axis=1)
-
-
-def weight_kernel(own_ref, got_ref, table_ref, bias_ref, dw_ref, du_ref, dvb_ref,
-                  part_ref, core_ref, chip_ref, sum_ref, final_ref, send_sems, recv_sems):
+def finish_kernel(own_ref, got_ref, table_ref, bias_ref, o_ref, dq_ref, dk_ref, dv_ref, dw_ref, du_ref, dvb_ref,
+                  rel_ref, part_ref, core_ref, sum_ref, chip_ref, final_ref, send_sems, recv_sems):
     dev = lax.axis_index('cp')
     chip, core = lax.div(dev, 2), lax.rem(dev, 2)
     core_peer, chip_peer = dev + 1 - 2 * core, dev + 2 - 4 * chip
     barrier = pltpu.get_barrier_semaphore()
     for peer in (core_peer, chip_peer):
         pl.semaphore_signal(barrier, inc=1, device_id={'cp': peer}, device_id_type=pl.DeviceIdType.MESH)
-    pl.semaphore_wait(barrier, 2)
-    own = jnp.concatenate([own_ref[tile, 4] for tile in range(own_ref.shape[0])], axis=0)
-    got = jnp.concatenate([got_ref[tile, 4] for tile in range(got_ref.shape[0])], axis=0)
-    d_rel = jnp.concatenate([jnp.where(chip == 0, own, got), jnp.where(chip == 0, got, own)], axis=1)
-    model_dim = table_ref.shape[1]
-    half_rows = part_ref.shape[1]
-    flat = part_ref.shape[0] * half_rows
-    for start in range(0, flat, 256):
-        size = min(256, model_dim - start) if start < model_dim else 0
-        rows = []
-        if size > 0:
-            rows.append(lax.dot_general(table_ref[:, start:start + size], d_rel, (((0,), (0,)), ((), ())), preferred_element_type=F32))
-        else:
-            bias = bias_ref[...]
-            zero = jnp.zeros_like(bias)
-            both = jnp.concatenate([jnp.where(chip == 0, bias, zero), jnp.where(chip == 0, zero, bias)], axis=1)
-            rows.append(jnp.concatenate([both, jnp.zeros((flat - start - bias.shape[0], both.shape[1]), F32)], axis=0))
-        block = rows[0]
-        for at in range(0, block.shape[0], 8):
-            pos = start + at
-            part_ref[pos // half_rows, pos % half_rows:pos % half_rows + 8] = block[at:at + 8]
+    tiles = own_ref.shape[0]
+    half = table_ref.shape[1] // 2
+
+    def heads(arr, tile):
+        own, got = own_ref[tile, arr], got_ref[tile, arr]
+        return jnp.where(chip == 0, own, got), jnp.where(chip == 0, got, own)
+
+    for tile in range(tiles):
+        rows = slice(tile * TILE, (tile + 1) * TILE)
+        rel_ref[rows, :SUB], rel_ref[rows, SUB:] = heads(4, tile)
+
+    def partial(which):
+        for start in range(0, half, 256):
+            at = pl.ds(pl.multiple_of(which * half + start, 256), 256)
+            part_ref[which, start:start + 256] = lax.dot_general(
+                table_ref[:, at], rel_ref[...], (((0,), (0,)), ((), ())), preferred_element_type=F32)
+        bias = bias_ref[...]
+        zero = jnp.zeros_like(bias)
+        both = jnp.concatenate([jnp.where(chip == 0, bias, zero), jnp.where(chip == 0, zero, bias)], axis=1)
+        part_ref[which, half:] = jnp.concatenate([both, jnp.zeros((6, both.shape[1]), F32)], axis=0)
 
     def swap(idx, src, dst, peer):
         copy = pltpu.make_async_remote_copy(
@@ -467,32 +498,42 @@
         copy.start()
         return copy
 
+    partial(1 - core)
+    pl.semaphore_wait(barrier, 2)
     first = swap(0, part_ref.at[1 - core], core_ref, core_peer)
+    partial(core)
     first.wait()
     sum_ref[...] = part_ref[core] + core_ref[...]
     second = swap(1, sum_ref, chip_ref, chip_peer)
+    for tile in range(tiles):
+        rows = slice(tile * TILE, (tile + 1) * TILE)
+        for arr, dst in enumerate((o_ref, dq_ref, dk_ref, dv_ref)):
+            dst[rows] = jnp.stack(heads(arr, tile), axis=1)
     second.wait()
     final_ref[core] = sum_ref[...] + chip_ref[...]
     third = swap(2, final_ref.at[core], final_ref.at[core], core_peer)
     third.wait()
-    total = jnp.concatenate([final_ref[0], final_ref[1]], axis=0)
-    dw_ref[...] = jnp.stack([total[:model_dim, :SUB], total[:model_dim, SUB:]], axis=1)
-    du_ref[...] = jnp.concatenate([total[model_dim:model_dim + 1, :SUB], total[model_dim:model_dim + 1, SUB:]], axis=0)
-    dvb_ref[...] = jnp.concatenate([total[model_dim + 1:model_dim + 2, :SUB], total[model_dim + 1:model_dim + 2, SUB:]], axis=0)
-
-
-def weight_grad(own, got, rel_table, bias_grad, w_shape):
-    model_dim = w_shape[0]
-    half_rows = model_dim // 2 + 8
+    for which in range(2):
+        dw_ref[which * half:(which + 1) * half] = jnp.stack(
+            [final_ref[which, :half, :SUB], final_ref[which, :half, SUB:]], axis=1)
+    tail = final_ref[0, half:]
+    du_ref[...] = jnp.concatenate([tail[0:1, :SUB], tail[0:1, SUB:]], axis=0)
+    dvb_ref[...] = jnp.concatenate([tail[1:2, :SUB], tail[1:2, SUB:]], axis=0)
+
+
+def finish(own, got, rel_table, bias_grad, seq_shape, w_shape):
+    half_rows = w_shape[0] // 2 + 8
     wide = 2 * SUB
     vmem = pl.BlockSpec(memory_space=pltpu.VMEM)
     bias = jax.ShapeDtypeStruct((2, SUB), F32)
+    seq = jax.ShapeDtypeStruct(seq_shape, BF16)
     return pl.pallas_call(
-        weight_kernel,
+        finish_kernel,
         in_specs=[vmem] * 4,
-        out_specs=[vmem] * 3,
-        out_shape=[jax.ShapeDtypeStruct(w_shape, F32), bias, bias],
+        out_specs=[vmem] * 7,
+        out_shape=[seq, seq, seq, seq, jax.ShapeDtypeStruct(w_shape, F32), bias, bias],
         scratch_shapes=[
+            pltpu.VMEM((rel_table.shape[0], wide), BF16),
             pltpu.VMEM((2, half_rows, wide), F32),
             pltpu.VMEM((half_rows, wide), F32),
             pltpu.VMEM((half_rows, wide), F32),
@@ -502,15 +543,8 @@
             pltpu.SemaphoreType.DMA((3,)),
         ],
         compiler_params=pltpu.CompilerParams(vmem_limit_bytes=48 * 1024 * 1024, collective_id=1, has_side_effects=True),
-        name="weight_grad",
+        name="finish",
     )(own, got, rel_table, bias_grad)
-
-
-def simple_call(body, out_shape, name):
-    vmem = pl.BlockSpec(memory_space=pltpu.VMEM)
-    return pl.pallas_call(
-        body, out_shape=out_shape, out_specs=[vmem] * len(out_shape), name=name,
-        compiler_params=pltpu.CompilerParams(vmem_limit_bytes=48 * 1024 * 1024))
 
 
 def solution(mesh):
@@ -519,16 +553,11 @@
     weight_spec = P(None, 'hp', None)
 
     def local_fn(q, k, v, u_bias, v_bias, rel_table, w_rel, d_out):
-        block_len, _, head_dim = q.shape
         chip = lax.axis_index('cp') // 2
-        five = jax.ShapeDtypeStruct((5, block_len, head_dim), BF16)
-        seq = jax.ShapeDtypeStruct(q.shape, BF16)
-        own, away = simple_call(pack_kernel, [five, five], "pack")(k, v, q, d_out, rel_table, w_rel)
         u_mine = lax.dynamic_slice_in_dim(u_bias, chip, 1)
         v_mine = lax.dynamic_slice_in_dim(v_bias, chip, 1)
-        res_own, res_got, bias_grad = run_attn(u_mine, v_mine, own, away)
-        d_w_rel, d_u, d_v = weight_grad(res_own, res_got, rel_table, bias_grad, w_rel.shape)
-        out, dq, dk, dv = simple_call(unpack_kernel, [seq] * 4, "unpack")(res_own, res_got)
+        res_own, res_got, bias_grad = run_attn(u_mine, v_mine, k, v, q, d_out, rel_table, w_rel)
+        out, dq, dk, dv, d_w_rel, d_u, d_v = finish(res_own, res_got, rel_table, bias_grad, q.shape, w_rel.shape)
         return out, dq, dk, dv, d_u, d_v, d_w_rel
 
     return jax.shard_map(

time: 227 us -> 192 us (0.85)
  Pallas kernels: 212 us -> 182 us
  local copies, waits for them, and re-layouts: 13.9 us -> 9.03 us
    pallas_call x3 -> x1, Pallas kernels: 36.3 us -> 21.1 us  [finish(): pl.pallas_call(finish_kernel, in_specs=[vmem] * 4, out_specs=[vmem] * 7,...]
    pallas_call x1, Pallas kernels: 176 us -> 161 us  [run_attn(): pl.pallas_call(functools.partial(attn_kernel, num_tiles, head_dim ** (-0....]
    unnamed x21 -> x11, local copies, waits for them, and re-layouts: 12.6 us -> 7.81 us
where the time goes in v3:
time: 192 us
  Pallas kernels  182 us (95%)
  local copies, waits for them, and re-layouts  9.03 us (5%)
    pallas_call x1, Pallas kernels, run_attn(): pl.pallas_call(functools.partial(attn_kernel, num_tiles, head_dim ** (-0....  161 us
    pallas_call x1, Pallas kernels, finish(): pl.pallas_call(finish_kernel, in_specs=[vmem] * 4, out_specs=[vmem] * 7,...  21.1 us
    unnamed x11, local copies, waits for them, and re-layouts  7.81 us

profile of v3, /device:TPU:0, one launch (start us, length us, event | category | flops | bytes accessed | tf_op | source)
XLA Modules:
  0.0 192.1 jit_solution(2873875571219032690)
XLA Ops:
  0.6 1.2 constant_dynamic-slice_fusion
  1.9 161.3 %attn_rows.1 = (bf16[3,5,512,128]{3,2,1,0:T(8,128)(2,1)}, bf16[3,5,512,128]{3,2,1,0:T(8,128)(2,1)}, f32[2,128]{1,0:T(2,128)}) custom-call(f32[1,128]{1,0:T(1,128)} %get-tuple-element.28.u_ref, f32[1,128]{1,0:T(1,128)} %get-tuple-element.27.v_ref, bf16[1536,2,128]{2,1,0:T(2,128)(2,1)} %kin_ref.1, bf16[1536,2,128]{2,1,0:T(2,128)(2,1)} %vin_ref.1, ...), custom_call_target="tpu_custom_call" | custom-call | tf_op jit(solution)/shard_map/attn_rows/pallas_call | solution.py:415
  163.1 0.0 copy-start
  163.2 1.5 copy-done
  164.7 0.0 copy-start.1
  164.7 0.7 copy-done.1
  165.4 21.1 %finish.1 = (bf16[1536,2,128]{2,1,0:T(2,128)(2,1)S(1)}, bf16[1536,2,128]{2,1,0:T(2,128)(2,1)S(1)}, bf16[1536,2,128]{2,1,0:T(2,128)(2,1)S(1)}, bf16[1536,2,128]{2...) custom-call(bf16[3,5,512,128]{3,2,1,0:T(8,128)(2,1)S(1)} %copy-done, ...), custom_call_target="tpu_custom_call" | custom-call | tf_op jit(solution)/shard_map/finish/pallas_call | solution.py:530
  186.5 0.9 copy.22
  187.4 0.9 copy.23
  188.2 0.9 copy.24
  189.1 0.9 copy.25
  190.0 0.6 copy.26
  190.6 0.6 copy.27
  191.1 1.0 copy.28
Async XLA Ops:
  163.1 1.5 copy-start
  164.7 0.7 copy-start.1

commit v4 on v3

--- a/solution.py
+++ b/solution.py
@@ -11,6 +11,7 @@
 SUB = 128
 NSUB = TILE // SUB
 MROWS = 2
+PARTS = (pl.ds(0, 2), pl.ds(2, 2), pl.ds(4, 1))
 LOG2E = 1.4426950408889634
 F32 = jnp.float32
 BF16 = jnp.bfloat16
@@ -46,9 +47,18 @@
     chip, core = lax.div(dev, 2), lax.rem(dev, 2)
     core_peer, chip_peer = dev + 1 - 2 * core, dev + 2 - 4 * chip
     half_steps = num_tiles // 4
-    pair = jnp.where(step < half_steps, step + half_steps * chip, (3 - chip) * half_steps - 1 - step)
-    odd = lax.rem(pair, 2)
-    blk = 2 * pair + odd + core - 2 * odd * core
+
+    def pair_at(idx):
+        first = jnp.where(idx < half_steps, idx, 3 * half_steps - 1 - idx)
+        second = jnp.where(idx < half_steps - 1, idx + half_steps, 2 * half_steps - 2 - idx)
+        second = jnp.where(idx == last, last, second)
+        return jnp.where(chip == 0, first, second)
+
+    def block_at(idx):
+        odd = lax.rem(pair_at(idx), 2)
+        return 2 * pair_at(idx) + odd + core - 2 * odd * core
+
+    blk = block_at(step)
     scale = inv_sqrt * LOG2E
     block_len = away_ref.shape[1]
     block_tiles = block_len // TILE
@@ -101,14 +111,14 @@
         return to_device(acc_ref.at[arr, :, cols(at)], part_ref.at[slot, arr],
                          part_send.at[slot, arr], part_recv.at[slot, arr], core_peer)
 
-    def start_parts(slot, pair_idx):
-        for arr in range(3):
-            part_copy(slot, pair_idx, arr).start()
+    def start_parts(slot, arrays):
+        for arr in arrays:
+            part_copy(slot, pair_of(slot), arr).start()
 
     def deliver(tile, stage, part, send_sem, start):
         owner = lax.div(tile, block_tiles)
         local = tile - owner * block_tiles
-        where = pl.ds(0, 2) if part == 0 else pl.ds(2, 3)
+        where = PARTS[part]
 
         @pl.when(owner == dev)
         def _():
@@ -125,20 +135,25 @@
             copy = to_device(stage, res_got_ref.at[local, where], send_sem, res_sems.at[1, part, local], owner)
             copy.start() if start else copy.wait_send()
 
-    def finish_parts(slot, pair_idx):
-        tile = 2 * pair_idx + core
-        for arr in range(3):
-            part_copy(slot, pair_idx, arr).wait_recv()
+    def finish_keys(slot):
+        tile = 2 * pair_of(slot) + core
+        for arr in range(2):
+            part_copy(slot, pair_of(slot), arr).wait_recv()
         d_key = (acc_ref[0, :, cols(tile)] + part_ref[slot, 0]) * inv_sqrt
         st_grad_ref[slot, 0] = d_key.astype(BF16).T
         d_val = acc_ref[1, :, cols(tile)] + part_ref[slot, 1]
         st_grad_ref[slot, 1] = d_val.astype(BF16).T
+        deliver(tile, st_grad_ref.at[slot, pl.ds(0, 2)], 1, grad_send.at[slot, 0], True)
+
+    def finish_offsets(slot):
+        tile = 2 * pair_of(slot) + core
+        part_copy(slot, pair_of(slot), 2).wait_recv()
         d_off = ((acc_ref[2, :, cols(num_tiles - 1 - tile)] + part_ref[slot, 2]) * inv_sqrt).astype(BF16)
         flip_rows = exchange_matrix()
         for chunk in range(NSUB):
             back = lax.dot_general(flip_rows, d_off[:, sub(chunk)], (((1,), (1,)), ((), ())), preferred_element_type=F32)
             st_grad_ref[slot, 2, sub(NSUB - 1 - chunk)] = back.astype(BF16)
-        deliver(tile, st_grad_ref.at[slot], 1, grad_send.at[slot], True)
+        deliver(tile, st_grad_ref.at[slot, pl.ds(2, 1)], 2, grad_send.at[slot, 1], True)
 
     def pair_of(idx):
         return jnp.where(idx < half_steps, (2 - chip) * half_steps - 1 - idx, idx - half_steps + half_steps * chip)
@@ -213,7 +228,7 @@
     def _():
         arrive((0, 2))
 
-    @pl.when(step == half_steps)
+    @pl.when(step == half_steps - chip)
     def _():
         arrive((3, 4))
 
@@ -351,11 +366,24 @@
         for half in range(2):
             start = pl.multiple_of(rel_tile * TILE + half * 256, 256)
             drel_ref[:, pl.ds(start, 256)] += dot(qvt_ref[...], p_ref[:, half * 256:half * 256 + 256])
+
+        @pl.when((step == last) & (chip == 1) & (lax.rem(tile, 2) == 1) & (tile < 2 * half_steps + 2))
+        def _():
+            now_pair = lax.div(tile, 2)
+
+            @pl.when(now_pair < half_steps)
+            def _():
+                start_parts(half_steps - 1 - now_pair, (0, 1))
+
+            @pl.when(now_pair > 0)
+            def _():
+                finish_keys(half_steps - now_pair)
         return 0
 
-    @pl.when(step > half_steps)
-    def _():
-        finish_parts(step - half_steps - 1, pair_of(step - half_steps - 1))
+    @pl.when((step > half_steps) & (chip == 0))
+    def _():
+        finish_offsets(step - half_steps - 1)
+        finish_keys(step - half_steps - 1)
 
     lax.fori_loop(0, blk + 1, grad_body, 0)
     grad_u = gu_ref[...] * inv_sqrt
@@ -365,31 +393,51 @@
     bias_ref[1:2, :] += jnp.sum(grad_v, axis=0, keepdims=True)
     deliver(blk, st_rows_ref.at[step], 0, rows_send.at[step], True)
 
-    @pl.when(step >= half_steps)
-    def _():
-        start_parts(step - half_steps, pair)
+    @pl.when((step >= half_steps) & (chip == 0))
+    def _():
+        start_parts(step - half_steps, (2, 0, 1))
 
     @pl.when(step == last)
     def _():
-        def start_rest(idx, _):
-            start_parts(idx, pair_of(idx))
-            return 0
-
-        def finish_rest(idx, _):
-            finish_parts(idx, pair_of(idx))
+        def start_far(idx, _):
+            start_parts(idx, (2,))
+            return 0
+
+        def start_near(idx, _):
+            start_parts(idx, (0, 1, 2))
+            return 0
+
+        def finish_far(idx, _):
+            finish_offsets(idx)
+            return 0
+
+        def finish_near(idx, _):
+            finish_offsets(idx)
+            finish_keys(idx)
             return 0
 
         def drain(idx, _):
             for arr in range(3):
                 part_copy(idx, pair_of(idx), arr).wait_send()
-            deliver(2 * pair_of(idx) + core, st_grad_ref.at[idx], 1, grad_send.at[idx], False)
-            pair_idx = jnp.where(idx < half_steps, idx + half_steps * chip, (3 - chip) * half_steps - 1 - idx)
-            odd_idx = lax.rem(pair_idx, 2)
-            deliver(2 * pair_idx + odd_idx + core - 2 * odd_idx * core, st_rows_ref.at[idx], 0, rows_send.at[idx], False)
-            return 0
-
-        lax.fori_loop(half_steps, 2 * half_steps, start_rest, 0)
-        lax.fori_loop(half_steps - 1, 2 * half_steps, finish_rest, 0)
+            tile = 2 * pair_of(idx) + core
+            deliver(tile, st_grad_ref.at[idx, pl.ds(0, 2)], 1, grad_send.at[idx, 0], False)
+            deliver(tile, st_grad_ref.at[idx, pl.ds(2, 1)], 2, grad_send.at[idx, 1], False)
+            deliver(block_at(idx), st_rows_ref.at[idx], 0, rows_send.at[idx], False)
+            return 0
+
+        @pl.when(chip == 1)
+        def _():
+            lax.fori_loop(0, half_steps, start_far, 0)
+        lax.fori_loop(half_steps, 2 * half_steps, start_near, 0)
+
+        @pl.when(chip == 1)
+        def _():
+            lax.fori_loop(0, half_steps, finish_far, 0)
+
+        @pl.when(chip == 0)
+        def _():
+            finish_near(half_steps - 1, 0)
+        lax.fori_loop(half_steps, 2 * half_steps, finish_near, 0)
         lax.fori_loop(0, 2 * half_steps, drain, 0)
         for arr in range(5):
             own_copy(arr).wait_send()
@@ -397,7 +445,7 @@
             fwd_copy(arr).wait_send()
         for which, res in enumerate((res_own_ref, res_got_ref)):
             for local in range(block_tiles):
-                for part, where in enumerate((pl.ds(0, 2), pl.ds(2, 3))):
+                for part, where in enumerate(PARTS):
                     dst = res.at[local, where]
                     pltpu.make_async_copy(dst, dst, res_sems.at[which, part, local]).wait()
 
@@ -447,7 +495,7 @@
             pltpu.VMEM(w_rel.shape, BF16),
             pltpu.VMEM((w_rel.shape[0], 2 * head_dim), BF16),
             dma((6,)), dma((5,)), dma((5,)), dma((5,)), dma((5,)), dma((5,)), dma((5,)),
-            dma((steps, 3)), dma((steps, 3)), dma((steps,)), dma((steps,)), dma((2, 2, block_tiles)),
+            dma((steps, 3)), dma((steps, 3)), dma((steps,)), dma((steps, 2)), dma((2, 3, block_tiles)),
         ],
         out_shape=[result, result, jax.ShapeDtypeStruct((2, head_dim), F32)],
         compiler_params=pltpu.CompilerParams(

time: 192 us -> 180 us (0.938)
  Pallas kernels: 182 us -> 170 us
    pallas_call x1, Pallas kernels: 161 us -> 149 us  [run_attn(): pl.pallas_call(functools.partial(attn_kernel, num_tiles, head_dim ** (-0....]
where the time goes in v4:
time: 180 us
  Pallas kernels  170 us (94%)
  local copies, waits for them, and re-layouts  9.03 us (5%)
    pallas_call x1, Pallas kernels, run_attn(): pl.pallas_call(functools.partial(attn_kernel, num_tiles, head_dim ** (-0....  149 us
    pallas_call x1, Pallas kernels, finish(): pl.pallas_call(finish_kernel, in_specs=[vmem] * 4, out_specs=[vmem] * 7,...  21.1 us
    unnamed x11, local copies, waits for them, and re-layouts  7.81 us

profile of v4, /device:TPU:0, one launch (start us, length us, event | category | flops | bytes accessed | tf_op | source)
XLA Modules:
  0.0 180.0 jit_solution(2862938069848165793)
XLA Ops:
  0.6 1.2 constant_dynamic-slice_fusion
  1.9 149.2 %attn_rows.1 = (bf16[3,5,512,128]{3,2,1,0:T(8,128)(2,1)}, bf16[3,5,512,128]{3,2,1,0:T(8,128)(2,1)}, f32[2,128]{1,0:T(2,128)}) custom-call(f32[1,128]{1,0:T(1,128)} %get-tuple-element.28.u_ref, f32[1,128]{1,0:T(1,128)} %get-tuple-element.27.v_ref, bf16[1536,2,128]{2,1,0:T(2,128)(2,1)} %kin_ref.1, bf16[1536,2,128]{2,1,0:T(2,128)(2,1)} %vin_ref.1, ...), custom_call_target="tpu_custom_call" | custom-call | tf_op jit(solution)/shard_map/attn_rows/pallas_call | solution.py:463
  151.1 0.0 copy-start
  151.1 1.5 copy-done
  152.6 0.0 copy-start.1
  152.6 0.7 copy-done.1
  153.3 21.1 %finish.1 = (bf16[1536,2,128]{2,1,0:T(2,128)(2,1)S(1)}, bf16[1536,2,128]{2,1,0:T(2,128)(2,1)S(1)}, bf16[1536,2,128]{2,1,0:T(2,128)(2,1)S(1)}, bf16[1536,2,128]{2...) custom-call(bf16[3,5,512,128]{3,2,1,0:T(8,128)(2,1)S(1)} %copy-done, ...), custom_call_target="tpu_custom_call" | custom-call | tf_op jit(solution)/shard_map/finish/pallas_call | solution.py:578
  174.4 0.9 copy.22
  175.3 0.9 copy.23
  176.2 0.9 copy.24
  177.1 0.9 copy.25
  177.9 0.6 copy.26
  178.5 0.6 copy.27
  179.1 1.0 copy.28
Async XLA Ops:
  151.1 1.5 copy-start
  152.6 0.7 copy-start.1

commit v5 on v4

--- a/solution.py
+++ b/solution.py
@@ -105,15 +105,15 @@
             if arr < 3:
                 transpose_half(arr, 1 - chip)
 
-    def part_copy(slot, pair_idx, arr):
-        tile = 2 * pair_idx + 1 - core
+    def part_copy(slot, arr):
+        tile = 2 * slot + 1 - core
         at = num_tiles - 1 - tile if arr == 2 else tile
         return to_device(acc_ref.at[arr, :, cols(at)], part_ref.at[slot, arr],
                          part_send.at[slot, arr], part_recv.at[slot, arr], core_peer)
 
     def start_parts(slot, arrays):
         for arr in arrays:
-            part_copy(slot, pair_of(slot), arr).start()
+            part_copy(slot, arr).start()
 
     def deliver(tile, stage, part, send_sem, start):
         owner = lax.div(tile, block_tiles)
@@ -136,9 +136,9 @@
             copy.start() if start else copy.wait_send()
 
     def finish_keys(slot):
-        tile = 2 * pair_of(slot) + core
+        tile = 2 * slot + core
         for arr in range(2):
-            part_copy(slot, pair_of(slot), arr).wait_recv()
+            part_copy(slot, arr).wait_recv()
         d_key = (acc_ref[0, :, cols(tile)] + part_ref[slot, 0]) * inv_sqrt
         st_grad_ref[slot, 0] = d_key.astype(BF16).T
         d_val = acc_ref[1, :, cols(tile)] + part_ref[slot, 1]
@@ -146,8 +146,8 @@
         deliver(tile, st_grad_ref.at[slot, pl.ds(0, 2)], 1, grad_send.at[slot, 0], True)
 
     def finish_offsets(slot):
-        tile = 2 * pair_of(slot) + core
-        part_copy(slot, pair_of(slot), 2).wait_recv()
+        tile = 2 * slot + core
+        part_copy(slot, 2).wait_recv()
         d_off = ((acc_ref[2, :, cols(num_tiles - 1 - tile)] + part_ref[slot, 2]) * inv_sqrt).astype(BF16)
         flip_rows = exchange_matrix()
         for chunk in range(NSUB):
@@ -155,8 +155,8 @@
             st_grad_ref[slot, 2, sub(NSUB - 1 - chunk)] = back.astype(BF16)
         deliver(tile, st_grad_ref.at[slot, pl.ds(2, 1)], 2, grad_send.at[slot, 1], True)
 
-    def pair_of(idx):
-        return jnp.where(idx < half_steps, (2 - chip) * half_steps - 1 - idx, idx - half_steps + half_steps * chip)
+    top_tile = 2 * pair_at(last) + 1
+    top_pair = pair_at(last)
 
     def put_heads(arr, start, size, first, second):
         at = 3 - dev if arr == 2 else dev
@@ -235,8 +235,8 @@
     rows_at = cols(blk)
     d_out = do_ref[rows_at, :]
     q_wide = q_ref[rows_at, :].astype(F32)
-    q_u = (q_wide + u_ref[...]).astype(BF16)
-    q_v = (q_wide + v_ref[...]).astype(BF16)
+    q_u = (q_wide + u_ref[pl.ds(chip, 1), :]).astype(BF16)
+    q_v = (q_wide + v_ref[pl.ds(chip, 1), :]).astype(BF16)
     qu_ref[...] = q_u
     qv_ref[...] = q_v
     qut_ref[...] = q_u.T
@@ -264,10 +264,7 @@
                     rot_ref[slot, sub(a), sub(half * 2 + c)] = pltpu.roll(part, 1, 1, stride=1, stride_axis=0)
 
     rotate_rel(first_rel, 0)
-
-    @pl.when(blk > 0)
-    def _():
-        rotate_rel(first_rel + 1, 1)
+    rotate_rel(jnp.minimum(first_rel + 1, num_tiles - 1), 1)
 
     def score_tile(tile, diag):
         left = lax.rem(tile, 3)
@@ -309,16 +306,21 @@
         arrive((1,))
 
     def prob_body(tile, _):
-        for a in range(NSUB):
-            run_sum = sum_ref[sub(a), :]
-            row_max = max_ref[sub(a), :]
-            for c in range(NSUB):
-                where = pl.ds(pl.multiple_of(tile * TILE + c * SUB, SUB), SUB)
-                prob = jnp.exp2(sc_ref[sub(a), where] - row_max)
-                p_ref[sub(a), sub(c)] = prob.astype(BF16)
-                run_sum = run_sum + prob
-            sum_ref[sub(a), :] = run_sum
-        gu_ref[...] += dot(p_ref[...], val_ref[cols(tile), :])
+        for top in range(0, NSUB, 2):
+            rows = slice(top * SUB, (top + 2) * SUB)
+            prob_rows = []
+            for a in range(top, top + 2):
+                run_sum = sum_ref[sub(a), :]
+                row_max = max_ref[sub(a), :]
+                prob_cols = []
+                for c in range(NSUB):
+                    where = pl.ds(pl.multiple_of(tile * TILE + c * SUB, SUB), SUB)
+                    prob = jnp.exp2(sc_ref[sub(a), where] - row_max)
+                    prob_cols.append(prob.astype(BF16))
+                    run_sum = run_sum + prob
+                sum_ref[sub(a), :] = run_sum
+                prob_rows.append(jnp.concatenate(prob_cols, axis=1))
+            gu_ref[rows, :] += dot(jnp.concatenate(prob_rows, axis=0), val_ref[cols(tile), :])
         return 0
 
     lax.fori_loop(0, blk + 1, prob_body, 0)
@@ -337,53 +339,74 @@
         old = 1 - now
         for half in range(2):
             start = pl.multiple_of(tile * TILE + half * 256, 256)
-            for a in range(NSUB):
-                if a % MROWS == 0:
-                    do_rows = pl.ds(pl.multiple_of(blk * TILE + a * SUB, SUB), MROWS * SUB)
-                    d_prob = dot(do_ref[do_rows, :], valt_ref[:, pl.ds(start, 256)])
-                log_norm = sum_ref[sub(a), :]
-                shift = row_ref[sub(a), :]
-                for c2 in range(2):
-                    c = half * 2 + c2
-                    prob = jnp.exp2(sc_ref[sub(a), pl.ds(pl.multiple_of(tile * TILE + c * SUB, SUB), SUB)] - log_norm)
-                    p_ref[sub(a), sub(c)] = prob.astype(BF16)
-                    d_score = prob * (d_prob[sub(a % MROWS), sub(c2)] - shift)
-                    dw_ref[sub(a), sub(c)] = d_score.astype(BF16)
-                    ds_ref[now, sub(a), sub(c)] = roll_left(d_score, flip)
             win = pl.ds(start, 256)
-            dv_ref[:, win] += dot(dot_ref[...], p_ref[:, half * 256:half * 256 + 256])
-            dk_ref[:, win] += dot(qut_ref[...], dw_ref[:, half * 256:half * 256 + 256])
-        gu_ref[...] += dot(dw_ref[...], k_ref[cols(tile), :])
-        for a in range(NSUB):
-            for y in range(NSUB):
-                c_lo = y + a - NSUB
-                c_hi = c_lo + 1
-                lo_part = ds_ref[now if c_lo >= 0 else old, sub(a), sub(c_lo % NSUB)]
-                hi_part = ds_ref[now if c_hi >= 0 else old, sub(a), sub(c_hi % NSUB)]
-                p_ref[sub(a), sub(y)] = jnp.where(lower, lo_part, hi_part).astype(BF16)
+            d_val = d_key = None
+            for top in range(0, NSUB, 2):
+                rows = slice(top * SUB, (top + 2) * SUB)
+                do_rows = pl.ds(pl.multiple_of(blk * TILE + top * SUB, SUB), 2 * SUB)
+                d_prob = dot(do_ref[do_rows, :], valt_ref[:, win])
+                prob_rows, score_rows = [], []
+                for a in range(top, top + 2):
+                    log_norm = sum_ref[sub(a), :]
+                    shift = row_ref[sub(a), :]
+                    prob_cols, score_cols = [], []
+                    for c2 in range(2):
+                        c = half * 2 + c2
+                        prob = jnp.exp2(sc_ref[sub(a), pl.ds(pl.multiple_of(tile * TILE + c * SUB, SUB), SUB)] - log_norm)
+                        d_score = prob * (d_prob[sub(a - top), sub(c2)] - shift)
+                        ds_ref[now, sub(a), sub(c)] = roll_left(d_score, flip)
+                        prob_cols.append(prob.astype(BF16))
+                        score_cols.append(d_score.astype(BF16))
+                    prob_rows.append(jnp.concatenate(prob_cols, axis=1))
+                    score_rows.append(jnp.concatenate(score_cols, axis=1))
+                probs = jnp.concatenate(prob_rows, axis=0)
+                scores = jnp.concatenate(score_rows, axis=0)
+                more_val, more_key = dot(dot_ref[:, rows], probs), dot(qut_ref[:, rows], scores)
+                d_val = more_val if d_val is None else d_val + more_val
+                d_key = more_key if d_key is None else d_key + more_key
+                gu_ref[rows, :] += dot(scores, k_ref[win, :])
+            dv_ref[:, win] += d_val
+            dk_ref[:, win] += d_key
         rel_tile = first_rel + tile
-        gv_ref[...] += dot(p_ref[...], rel_ref[cols(rel_tile), :])
+        d_off = [None, None]
+        for top in range(0, NSUB, 2):
+            rows = slice(top * SUB, (top + 2) * SUB)
+            wide_rows = []
+            for a in range(top, top + 2):
+                wide_cols = []
+                for y in range(NSUB):
+                    c_lo = y + a - NSUB
+                    c_hi = c_lo + 1
+                    lo_part = ds_ref[now if c_lo >= 0 else old, sub(a), sub(c_lo % NSUB)]
+                    hi_part = ds_ref[now if c_hi >= 0 else old, sub(a), sub(c_hi % NSUB)]
+                    wide_cols.append(jnp.where(lower, lo_part, hi_part).astype(BF16))
+                wide_rows.append(jnp.concatenate(wide_cols, axis=1))
+            by_off = jnp.concatenate(wide_rows, axis=0)
+            gv_ref[rows, :] += dot(by_off, rel_ref[cols(rel_tile), :])
+            for half in range(2):
+                more = dot(qvt_ref[:, rows], by_off[:, half * 256:half * 256 + 256])
+                d_off[half] = more if d_off[half] is None else d_off[half] + more
         for half in range(2):
             start = pl.multiple_of(rel_tile * TILE + half * 256, 256)
-            drel_ref[:, pl.ds(start, 256)] += dot(qvt_ref[...], p_ref[:, half * 256:half * 256 + 256])
-
-        @pl.when((step == last) & (chip == 1) & (lax.rem(tile, 2) == 1) & (tile < 2 * half_steps + 2))
+            drel_ref[:, pl.ds(start, 256)] += d_off[half]
+
+        @pl.when((step == last) & (lax.rem(tile, 2) == 1) & (tile < top_tile))
         def _():
-            now_pair = lax.div(tile, 2)
-
-            @pl.when(now_pair < half_steps)
+            key_pair = lax.div(tile, 2)
+            off_pair = lax.div(top_tile - tile, 2)
+            start_parts(off_pair, (2,))
+            start_parts(key_pair, (0, 1))
+
+            @pl.when(key_pair > 0)
             def _():
-                start_parts(half_steps - 1 - now_pair, (0, 1))
-
-            @pl.when(now_pair > 0)
-            def _():
-                finish_keys(half_steps - now_pair)
+                finish_offsets(off_pair + 1)
+                finish_keys(key_pair - 1)
         return 0
 
     @pl.when((step > half_steps) & (chip == 0))
     def _():
-        finish_offsets(step - half_steps - 1)
-        finish_keys(step - half_steps - 1)
+        finish_offsets(pair_at(step - 1))
+        finish_keys(pair_at(step - 1))
 
     lax.fori_loop(0, blk + 1, grad_body, 0)
     grad_u = gu_ref[...] * inv_sqrt
@@ -393,51 +416,30 @@
     bias_ref[1:2, :] += jnp.sum(grad_v, axis=0, keepdims=True)
     deliver(blk, st_rows_ref.at[step], 0, rows_send.at[step], True)
 
-    @pl.when((step >= half_steps) & (chip == 0))
+    @pl.when((step >= half_steps) & (step < last) & (chip == 0))
     def _():
-        start_parts(step - half_steps, (2, 0, 1))
+        start_parts(pair_at(step), (2, 0, 1))
 
     @pl.when(step == last)
     def _():
-        def start_far(idx, _):
-            start_parts(idx, (2,))
-            return 0
-
-        def start_near(idx, _):
-            start_parts(idx, (0, 1, 2))
-            return 0
-
-        def finish_far(idx, _):
-            finish_offsets(idx)
-            return 0
-
-        def finish_near(idx, _):
-            finish_offsets(idx)
-            finish_keys(idx)
+        start_parts(0, (2,))
+        start_parts(top_pair, (0, 1))
+
+        def finish_rest(idx, _):
+            finish_offsets(1 - idx)
+            finish_keys(top_pair - 1 + idx)
             return 0
 
         def drain(idx, _):
             for arr in range(3):
-                part_copy(idx, pair_of(idx), arr).wait_send()
-            tile = 2 * pair_of(idx) + core
+                part_copy(idx, arr).wait_send()
+            tile = 2 * idx + core
             deliver(tile, st_grad_ref.at[idx, pl.ds(0, 2)], 1, grad_send.at[idx, 0], False)
             deliver(tile, st_grad_ref.at[idx, pl.ds(2, 1)], 2, grad_send.at[idx, 1], False)
             deliver(block_at(idx), st_rows_ref.at[idx], 0, rows_send.at[idx], False)
             return 0
 
-        @pl.when(chip == 1)
-        def _():
-            lax.fori_loop(0, half_steps, start_far, 0)
-        lax.fori_loop(half_steps, 2 * half_steps, start_near, 0)
-
-        @pl.when(chip == 1)
-        def _():
-            lax.fori_loop(0, half_steps, finish_far, 0)
-
-        @pl.when(chip == 0)
-        def _():
-            finish_near(half_steps - 1, 0)
-        lax.fori_loop(half_steps, 2 * half_steps, finish_near, 0)
+        lax.fori_loop(0, 2, finish_rest, 0)
         lax.fori_loop(0, 2 * half_steps, drain, 0)
         for arr in range(5):
             own_copy(arr).wait_send()
@@ -510,8 +512,9 @@
     return jnp.where(row + col == SUB - 1, 1.0, 0.0).astype(BF16)
 
 
-def finish_kernel(own_ref, got_ref, table_ref, bias_ref, o_ref, dq_ref, dk_ref, dv_ref, dw_ref, du_ref, dvb_ref,
-                  rel_ref, part_ref, core_ref, sum_ref, chip_ref, final_ref, send_sems, recv_sems):
+def finish_kernel(own_in, got_in, table_in, bias_ref, o_ref, dq_ref, dk_ref, dv_ref, dw_ref, du_ref, dvb_ref,
+                  own_ref, got_ref, table_ref, rel_ref, part_ref, core_ref, sum_ref, chip_ref, final_ref,
+                  send_sems, recv_sems, load_sems):
     dev = lax.axis_index('cp')
     chip, core = lax.div(dev, 2), lax.rem(dev, 2)
     core_peer, chip_peer = dev + 1 - 2 * core, dev + 2 - 4 * chip
@@ -520,6 +523,17 @@
         pl.semaphore_signal(barrier, inc=1, device_id={'cp': peer}, device_id_type=pl.DeviceIdType.MESH)
     tiles = own_ref.shape[0]
     half = table_ref.shape[1] // 2
+    loads = [pltpu.make_async_copy(src.at[:, where], dst.at[:, where], load_sems.at[idx]) for idx, (src, dst, where) in enumerate((
+        (own_in, own_ref, pl.ds(4, 1)), (got_in, got_ref, pl.ds(4, 1)),
+        (own_in, own_ref, pl.ds(0, 4)), (got_in, got_ref, pl.ds(0, 4))))]
+    table_load = pltpu.make_async_copy(table_in, table_ref, load_sems.at[4])
+    loads[0].start()
+    loads[1].start()
+    table_load.start()
+    loads[2].start()
+    loads[3].start()
+    loads[0].wait()
+    loads[1].wait()
 
     def heads(arr, tile):
         own, got = own_ref[tile, arr], got_ref[tile, arr]
@@ -546,6 +560,7 @@
         copy.start()
         return copy
 
+    table_load.wait()
     partial(1 - core)
     pl.semaphore_wait(barrier, 2)
     first = swap(0, part_ref.at[1 - core], core_ref, core_peer)
@@ -553,6 +568,8 @@
     first.wait()
     sum_ref[...] = part_ref[core] + core_ref[...]
     second = swap(1, sum_ref, chip_ref, chip_peer)
+    loads[2].wait()
+    loads[3].wait()
     for tile in range(tiles):
         rows = slice(tile * TILE, (tile + 1) * TILE)
         for arr, dst in enumerate((o_ref, dq_ref, dk_ref, dv_ref)):
@@ -577,10 +594,13 @@
     seq = jax.ShapeDtypeStruct(seq_shape, BF16)
     return pl.pallas_call(
         finish_kernel,
-        in_specs=[vmem] * 4,
+        in_specs=[pl.BlockSpec(memory_space=pl.ANY)] * 3 + [vmem],
         out_specs=[vmem] * 7,
         out_shape=[seq, seq, seq, seq, jax.ShapeDtypeStruct(w_shape, F32), bias, bias],
         scratch_shapes=[
+            pltpu.VMEM(own.shape, BF16),
+            pltpu.VMEM(got.shape, BF16),
+            pltpu.VMEM(rel_table.shape, BF16),
             pltpu.VMEM((rel_table.shape[0], wide), BF16),
             pltpu.VMEM((2, half_rows, wide), F32),
             pltpu.VMEM((half_rows, wide), F32),
@@ -589,6 +609,7 @@
             pltpu.VMEM((2, half_rows, wide), F32),
             pltpu.SemaphoreType.DMA((3,)),
             pltpu.SemaphoreType.DMA((3,)),
+            pltpu.SemaphoreType.DMA((5,)),
         ],
         compiler_params=pltpu.CompilerParams(vmem_limit_bytes=48 * 1024 * 1024, collective_id=1, has_side_effects=True),
         name="finish",
@@ -601,10 +622,7 @@
     weight_spec = P(None, 'hp', None)
 
     def local_fn(q, k, v, u_bias, v_bias, rel_table, w_rel, d_out):
-        chip = lax.axis_index('cp') // 2
-        u_mine = lax.dynamic_slice_in_dim(u_bias, chip, 1)
-        v_mine = lax.dynamic_slice_in_dim(v_bias, chip, 1)
-        res_own, res_got, bias_grad = run_attn(u_mine, v_mine, k, v, q, d_out, rel_table, w_rel)
+        res_own, res_got, bias_grad = run_attn(u_bias, v_bias, k, v, q, d_out, rel_table, w_rel)
         out, dq, dk, dv, d_w_rel, d_u, d_v = finish(res_own, res_got, rel_table, bias_grad, q.shape, w_rel.shape)
         return out, dq, dk, dv, d_u, d_v, d_w_rel
 

time: 180 us -> 170 us (0.944)
  Pallas kernels: 170 us -> 161 us
    pallas_call x1, Pallas kernels: 149 us -> 142 us  [run_attn(): pl.pallas_call(functools.partial(attn_kernel, num_tiles, head_dim ** (-0....]
    pallas_call x1, Pallas kernels: 21.1 us -> 19.1 us  [finish(): pl.pallas_call(finish_kernel, in_specs=[pl.BlockSpec(memory_space=pl.ANY)...]
where the time goes in v5:
time: 170 us; the launch traced here: 169 us
  Pallas kernels  161 us (95%)
  local copies, waits for them, and re-layouts  7.78 us (5%)
    pallas_call x1, Pallas kernels, run_attn(): pl.pallas_call(functools.partial(attn_kernel, num_tiles, head_dim ** (-0....  142 us
    pallas_call x1, Pallas kernels, finish(): pl.pallas_call(finish_kernel, in_specs=[pl.BlockSpec(memory_space=pl.ANY)...  19.1 us
    unnamed x11, local copies, waits for them, and re-layouts  7.78 us

profile of v5, /device:TPU:0, one launch (start us, length us, event | category | flops | bytes accessed | tf_op | source)
XLA Modules:
  0.0 169.4 jit_solution(5920785497883390074)
XLA Ops:
  0.6 141.8 %attn_rows.1 = (bf16[3,5,512,128]{3,2,1,0:T(8,128)(2,1)}, bf16[3,5,512,128]{3,2,1,0:T(8,128)(2,1)}, f32[2,128]{1,0:T(2,128)}) custom-call(f32[2,128]{1,0:T(2,128)} %u_ref.1, f32[2,128]{1,0:T(2,128)} %v_ref.1, bf16[1536,2,128]{2,1,0:T(2,128)(2,1)} %kin_ref.1, bf16[1536,2,128]{2,1,0:T(2,128)(2,1)} %vin_ref.1, bf16[1536,2,128]{2,1,0:T(2,128)(2,1)} %qin_ref.1, ...), custom_call_target="tpu_custom_call" | custom-call | tf_op jit(solution)/shard_map/attn_rows/pallas_call | solution.py:465
  142.4 0.0 copy-start
  142.5 1.5 copy-done
  144.0 0.0 copy-start.1
  144.0 0.6 copy-done.1
  144.6 19.1 %finish.1 = (bf16[1536,2,128]{2,1,0:T(2,128)(2,1)S(1)}, bf16[1536,2,128]{2,1,0:T(2,128)(2,1)S(1)}, bf16[1536,2,128]{2,1,0:T(2,128)(2,1)S(1)}, bf16[1536,2,128]{2...) custom-call(bf16[3,5,512,128]{3,2,1,0:T(8,128)(2,1)S(1)} %copy-done, ...), custom_call_target="tpu_custom_call" | custom-call | tf_op jit(solution)/shard_map/finish/pallas_call | solution.py:595
  163.7 0.9 copy.22
  164.6 0.9 copy.23
  165.5 0.9 copy.24
  166.4 0.9 copy.25
  167.3 0.6 copy.26
  167.8 0.6 copy.27
  168.4 1.0 copy.28
Async XLA Ops:
  142.4 1.5 copy-start
  144.0 0.6 copy-start.1

commit v6 on v5

--- a/solution.py
+++ b/solution.py
@@ -35,12 +35,13 @@
 
 
 def attn_kernel(num_tiles, inv_sqrt, u_ref, v_ref, kin_ref, vin_ref, qin_ref, doin_ref, table_in_ref, w_in_ref,
-                res_own_ref, res_got_ref, bias_ref,
+                o_ref, dq_ref, dk_out_ref, dv_out_ref, dw_out_ref, du_ref, dvb_ref, res_own_ref, res_got_ref,
                 full_ref, acc_ref, kt_ref, valt_ref, relt_ref, sc_ref, rot_ref, ds_ref, dw_ref, p_ref,
                 qu_ref, qv_ref, qut_ref, qvt_ref, dot_ref, max_ref, sum_ref, gu_ref, gv_ref, row_ref,
-                st_rows_ref, st_grad_ref, part_ref, away_ref, raw_ref, table_ref, w_ref, wide_ref,
+                st_rows_ref, st_grad_ref, part_ref, away_ref, raw_ref, table_ref, w_ref, wide_ref, bias_ref, res_rel_ref,
+                core_ref, chip_ref, final_ref, sum_send, sum_recv,
                 local_sems, own_send, own_recv, cross_send, cross_recv, fwd_send, fwd_recv,
-                part_send, part_recv, rows_send, grad_send, res_sems):
+                part_send, part_recv, rows_send, grad_send, res_sems, load_sems, out_sems):
     step = pl.program_id(0)
     last = pl.num_programs(0) - 1
     dev = lax.axis_index('cp')
@@ -118,21 +119,24 @@
     def deliver(tile, stage, part, send_sem, start):
         owner = lax.div(tile, block_tiles)
         local = tile - owner * block_tiles
-        where = PARTS[part]
+        if part == 2:
+            own_dst, got_dst = res_rel_ref.at[0, pl.ds(local, 1)], res_rel_ref.at[1, pl.ds(local, 1)]
+        else:
+            own_dst, got_dst = res_own_ref.at[local, PARTS[part]], res_got_ref.at[local, PARTS[part]]
 
         @pl.when(owner == dev)
         def _():
             if start:
-                pltpu.make_async_copy(stage, res_own_ref.at[local, where], res_sems.at[0, part, local]).start()
+                pltpu.make_async_copy(stage, own_dst, res_sems.at[0, part, local]).start()
 
         @pl.when(owner == core_peer)
         def _():
-            copy = to_device(stage, res_own_ref.at[local, where], send_sem, res_sems.at[0, part, local], owner)
+            copy = to_device(stage, own_dst, send_sem, res_sems.at[0, part, local], owner)
             copy.start() if start else copy.wait_send()
 
         @pl.when(lax.div(owner, 2) != chip)
         def _():
-            copy = to_device(stage, res_got_ref.at[local, where], send_sem, res_sems.at[1, part, local], owner)
+            copy = to_device(stage, got_dst, send_sem, res_sems.at[1, part, local], owner)
             copy.start() if start else copy.wait_send()
 
     def finish_keys(slot):
@@ -158,6 +162,100 @@
     top_tile = 2 * pair_at(last) + 1
     top_pair = pair_at(last)
 
+    def finish_all():
+        model_dim = table_ref.shape[1]
+        half = model_dim // 2
+        quarter = half // 2
+        size = quarter + 8
+
+        def piece(which, chunk):
+            return rot_ref.at[which, pl.ds(0, size), pl.ds(chunk * 256, 256)]
+
+        def total_piece(chunk):
+            return rot_ref.at[2, pl.ds(0, size), pl.ds(chunk * 256, 256)]
+
+        def wait_res(which, part):
+            for local in range(block_tiles):
+                if part == 2:
+                    dst = res_rel_ref.at[which, pl.ds(local, 1)]
+                else:
+                    dst = (res_own_ref, res_got_ref)[which].at[local, PARTS[part]]
+                pltpu.make_async_copy(dst, dst, res_sems.at[which, part, local]).wait()
+
+        def partial(which, chunk, src):
+            head = chip if src == 0 else 1 - chip
+            lanes = pl.ds(pl.multiple_of(head * SUB, SUB), SUB)
+            at = pl.ds(pl.multiple_of(which * half + chunk * quarter, 256), quarter)
+            d_rel = jnp.concatenate([res_rel_ref[src, tile] for tile in range(block_tiles)], axis=0)
+            piece(which, chunk)[pl.ds(0, quarter), lanes] = lax.dot_general(
+                table_ref[:, at], d_rel, (((0,), (0,)), ((), ())), preferred_element_type=F32)
+            bias = bias_ref[...] if src == 0 else jnp.zeros_like(bias_ref)
+            piece(which, chunk)[pl.ds(quarter, 8), lanes] = jnp.concatenate([bias, jnp.zeros((6, SUB), F32)], axis=0)
+
+        def swap(idx, src, dst, peer):
+            copy = to_device(src, dst, sum_send.at[idx], sum_recv.at[idx], peer)
+            copy.start()
+            return copy
+
+        order = ((1 - core, 0), (core, 0), (1 - core, 1), (core, 1))
+        wait_res(0, 2)
+        for which, chunk in order:
+            partial(which, chunk, 0)
+        wait_res(1, 2)
+        first, second, third = [], [], []
+        for chunk in range(2):
+            partial(1 - core, chunk, 1)
+            first.append(swap(chunk, piece(1 - core, chunk), core_ref.at[chunk], core_peer))
+            partial(core, chunk, 1)
+            first[chunk].wait()
+            total_piece(chunk)[...] = piece(core, chunk)[...] + core_ref[chunk]
+            second.append(swap(2 + chunk, total_piece(chunk), chip_ref.at[chunk], chip_peer))
+        for part in range(2):
+            wait_res(0, part)
+            wait_res(1, part)
+        loads = []
+        for tile in range(block_tiles):
+            for which, res in enumerate((res_own_ref, res_got_ref)):
+                dst = full_ref.at[pl.ds(0, 4), pl.ds((which * block_tiles + tile) * TILE, TILE)]
+                loads.append(pltpu.make_async_copy(res.at[tile], dst, load_sems.at[tile, which]))
+        for load in loads:
+            load.start()
+        for tile in range(block_tiles):
+            loads[2 * tile].wait()
+            loads[2 * tile + 1].wait()
+            rows = slice(tile * TILE, (tile + 1) * TILE)
+            for arr in range(4):
+                own = full_ref[arr, rows]
+                got = full_ref[arr, (block_tiles + tile) * TILE:(block_tiles + tile + 1) * TILE]
+                raw_ref[arr, rows] = jnp.stack([jnp.where(chip == 0, own, got), jnp.where(chip == 0, got, own)], axis=1)
+        stores = [pltpu.make_async_copy(raw_ref.at[arr], dst, local_sems.at[arr])
+                  for arr, dst in enumerate((o_ref, dq_ref, dk_out_ref, dv_out_ref))]
+        for store in stores:
+            store.start()
+
+        def put(which, chunk):
+            base = pl.multiple_of(which * half + chunk * quarter, 256)
+            for head in range(2):
+                store = pltpu.make_async_copy(
+                    final_ref.at[which, chunk, pl.ds(0, quarter), pl.ds(head * SUB, SUB)],
+                    dw_out_ref.at[head, pl.ds(base, quarter)], out_sems.at[len(stores) - 4])
+                store.start()
+                stores.append(store)
+
+        for chunk in range(2):
+            second[chunk].wait()
+            final_ref[core, chunk] = total_piece(chunk)[...] + chip_ref[chunk]
+            third.append(swap(4 + chunk, final_ref.at[core, chunk], final_ref.at[core, chunk], core_peer))
+            put(core, chunk)
+        for chunk in range(2):
+            third[chunk].wait()
+            put(1 - core, chunk)
+        sums = final_ref[0, 0, quarter:]
+        du_ref[...] = jnp.concatenate([sums[0:1, :SUB], sums[0:1, SUB:]], axis=0)
+        dvb_ref[...] = jnp.concatenate([sums[1:2, :SUB], sums[1:2, SUB:]], axis=0)
+        for store in stores:
+            store.wait()
+
     def put_heads(arr, start, size, first, second):
         at = 3 - dev if arr == 2 else dev
         own_at = pl.ds(pl.multiple_of(at * block_len + start, SUB), size)
@@ -194,8 +292,7 @@
         loads = [pltpu.make_async_copy(src, dst, local_sems.at[idx]) for idx, (src, dst) in enumerate((
             (kin_ref, raw_ref.at[0]), (w_in_ref, w_ref), (table_in_ref, table_ref),
             (vin_ref, raw_ref.at[1]), (qin_ref, raw_ref.at[2]), (doin_ref, raw_ref.at[3])))]
-        for load in loads:
-            load.start()
+        loads[0].start()
 
         def clear(tile, _):
             acc_ref[:, :, cols(tile)] = jnp.zeros((3, SUB, TILE), F32)
@@ -206,6 +303,8 @@
             own_copy(arr).start()
 
         loads[0].wait()
+        for load in loads[1:]:
+            load.start()
         pack_seq(0, 0)
         pl.semaphore_wait(barrier, 3)
         ship(0)
@@ -213,10 +312,21 @@
         loads[2].wait()
         pack_rel()
         ship(2)
-        for idx, arr in enumerate((1, 3, 4)):
+        def load_and_ship(arr):
+            idx = (1, 3, 4).index(arr)
             loads[3 + idx].wait()
             pack_seq(arr, idx + 1)
             ship(arr)
+
+        @pl.when(chip == 0)
+        def _():
+            load_and_ship(1)
+        load_and_ship(3)
+
+        @pl.when(chip == 1)
+        def _():
+            load_and_ship(1)
+        load_and_ship(4)
         lax.fori_loop(0, num_tiles, clear, 0)
         bias_ref[...] = jnp.zeros_like(bias_ref)
         for arr in (0, 2, 1, 3, 4):
@@ -230,10 +340,9 @@
 
     @pl.when(step == half_steps - chip)
     def _():
-        arrive((3, 4))
+        arrive((3,))
 
     rows_at = cols(blk)
-    d_out = do_ref[rows_at, :]
     q_wide = q_ref[rows_at, :].astype(F32)
     q_u = (q_wide + u_ref[pl.ds(chip, 1), :]).astype(BF16)
     q_v = (q_wide + v_ref[pl.ds(chip, 1), :]).astype(BF16)
@@ -241,7 +350,6 @@
     qv_ref[...] = q_v
     qut_ref[...] = q_u.T
     qvt_ref[...] = q_v.T
-    dot_ref[...] = d_out.T
     max_ref[...] = jnp.full_like(max_ref, -jnp.inf)
     sum_ref[...] = jnp.zeros_like(sum_ref)
     gu_ref[...] = jnp.zeros_like(gu_ref)
@@ -324,6 +432,11 @@
         return 0
 
     lax.fori_loop(0, blk + 1, prob_body, 0)
+    @pl.when(step == half_steps - chip)
+    def _():
+        arrive((4,))
+
+    dot_ref[...] = do_ref[rows_at, :].T
     total = jnp.sum(sum_ref[...], axis=1, keepdims=True)
     inv_sum = 1.0 / total
     out = gu_ref[...] * inv_sum
@@ -440,16 +553,12 @@
             return 0
 
         lax.fori_loop(0, 2, finish_rest, 0)
-        lax.fori_loop(0, 2 * half_steps, drain, 0)
         for arr in range(5):
             own_copy(arr).wait_send()
             cross_copy(arr).wait_send()
             fwd_copy(arr).wait_send()
-        for which, res in enumerate((res_own_ref, res_got_ref)):
-            for local in range(block_tiles):
-                for part, where in enumerate(PARTS):
-                    dst = res.at[local, where]
-                    pltpu.make_async_copy(dst, dst, res_sems.at[which, part, local]).wait()
+        finish_all()
+        lax.fori_loop(0, 2 * half_steps, drain, 0)
 
 
 def run_attn(u_bias, v_bias, k, v, q, d_out, rel_table, w_rel):
@@ -460,13 +569,17 @@
     block_tiles = block_len // TILE
     vec = pl.BlockSpec(memory_space=pltpu.VMEM)
     hbm = pl.BlockSpec(memory_space=pl.ANY)
-    result = jax.ShapeDtypeStruct((block_tiles, 5, TILE, head_dim), BF16)
+    result = jax.ShapeDtypeStruct((block_tiles, 4, TILE, head_dim), BF16)
+    seq = jax.ShapeDtypeStruct(k.shape, BF16)
+    bias = jax.ShapeDtypeStruct((2, head_dim), F32)
+    d_weights = jax.ShapeDtypeStruct((2, w_rel.shape[0], head_dim), F32)
+    size = w_rel.shape[0] // 4 + 8
     dma = pltpu.SemaphoreType.DMA
     return pl.pallas_call(
         functools.partial(attn_kernel, num_tiles, head_dim ** -0.5),
         grid=(steps,),
         in_specs=[vec, vec] + [hbm] * 6,
-        out_specs=[hbm, hbm, vec],
+        out_specs=[hbm] * 5 + [vec, vec, hbm, hbm],
         scratch_shapes=[
             pltpu.VMEM((5, seq_len, head_dim), BF16),
             pltpu.VMEM((3, head_dim, seq_len), F32),
@@ -496,10 +609,16 @@
             pltpu.VMEM(rel_table.shape, BF16),
             pltpu.VMEM(w_rel.shape, BF16),
             pltpu.VMEM((w_rel.shape[0], 2 * head_dim), BF16),
+            pltpu.VMEM((2, head_dim), F32),
+            pltpu.VMEM((2, block_tiles, TILE, head_dim), BF16),
+            pltpu.VMEM((2, size, 2 * head_dim), F32),
+            pltpu.VMEM((2, size, 2 * head_dim), F32),
+            pltpu.VMEM((2, 2, size, 2 * head_dim), F32),
+            dma((6,)), dma((6,)),
             dma((6,)), dma((5,)), dma((5,)), dma((5,)), dma((5,)), dma((5,)), dma((5,)),
-            dma((steps, 3)), dma((steps, 3)), dma((steps,)), dma((steps, 2)), dma((2, 3, block_tiles)),
+            dma((steps, 3)), dma((steps, 3)), dma((steps,)), dma((steps, 2)), dma((2, 3, block_tiles)), dma((block_tiles, 2)), dma((8,)),
         ],
-        out_shape=[result, result, jax.ShapeDtypeStruct((2, head_dim), F32)],
+        out_shape=[seq, seq, seq, seq, d_weights, bias, bias, result, result],
         compiler_params=pltpu.CompilerParams(
             dimension_semantics=("arbitrary",), vmem_limit_bytes=67043328, collective_id=0, has_side_effects=True),
         name="attn_rows",
@@ -512,119 +631,14 @@
     return jnp.where(row + col == SUB - 1, 1.0, 0.0).astype(BF16)
 
 
-def finish_kernel(own_in, got_in, table_in, bias_ref, o_ref, dq_ref, dk_ref, dv_ref, dw_ref, du_ref, dvb_ref,
-                  own_ref, got_ref, table_ref, rel_ref, part_ref, core_ref, sum_ref, chip_ref, final_ref,
-                  send_sems, recv_sems, load_sems):
-    dev = lax.axis_index('cp')
-    chip, core = lax.div(dev, 2), lax.rem(dev, 2)
-    core_peer, chip_peer = dev + 1 - 2 * core, dev + 2 - 4 * chip
-    barrier = pltpu.get_barrier_semaphore()
-    for peer in (core_peer, chip_peer):
-        pl.semaphore_signal(barrier, inc=1, device_id={'cp': peer}, device_id_type=pl.DeviceIdType.MESH)
-    tiles = own_ref.shape[0]
-    half = table_ref.shape[1] // 2
-    loads = [pltpu.make_async_copy(src.at[:, where], dst.at[:, where], load_sems.at[idx]) for idx, (src, dst, where) in enumerate((
-        (own_in, own_ref, pl.ds(4, 1)), (got_in, got_ref, pl.ds(4, 1)),
-        (own_in, own_ref, pl.ds(0, 4)), (got_in, got_ref, pl.ds(0, 4))))]
-    table_load = pltpu.make_async_copy(table_in, table_ref, load_sems.at[4])
-    loads[0].start()
-    loads[1].start()
-    table_load.start()
-    loads[2].start()
-    loads[3].start()
-    loads[0].wait()
-    loads[1].wait()
-
-    def heads(arr, tile):
-        own, got = own_ref[tile, arr], got_ref[tile, arr]
-        return jnp.where(chip == 0, own, got), jnp.where(chip == 0, got, own)
-
-    for tile in range(tiles):
-        rows = slice(tile * TILE, (tile + 1) * TILE)
-        rel_ref[rows, :SUB], rel_ref[rows, SUB:] = heads(4, tile)
-
-    def partial(which):
-        for start in range(0, half, 256):
-            at = pl.ds(pl.multiple_of(which * half + start, 256), 256)
-            part_ref[which, start:start + 256] = lax.dot_general(
-                table_ref[:, at], rel_ref[...], (((0,), (0,)), ((), ())), preferred_element_type=F32)
-        bias = bias_ref[...]
-        zero = jnp.zeros_like(bias)
-        both = jnp.concatenate([jnp.where(chip == 0, bias, zero), jnp.where(chip == 0, zero, bias)], axis=1)
-        part_ref[which, half:] = jnp.concatenate([both, jnp.zeros((6, both.shape[1]), F32)], axis=0)
-
-    def swap(idx, src, dst, peer):
-        copy = pltpu.make_async_remote_copy(
-            src_ref=src, dst_ref=dst, send_sem=send_sems.at[idx], recv_sem=recv_sems.at[idx],
-            device_id={'cp': peer}, device_id_type=pl.DeviceIdType.MESH)
-        copy.start()
-        return copy
-
-    table_load.wait()
-    partial(1 - core)
-    pl.semaphore_wait(barrier, 2)
-    first = swap(0, part_ref.at[1 - core], core_ref, core_peer)
-    partial(core)
-    first.wait()
-    sum_ref[...] = part_ref[core] + core_ref[...]
-    second = swap(1, sum_ref, chip_ref, chip_peer)
-    loads[2].wait()
-    loads[3].wait()
-    for tile in range(tiles):
-        rows = slice(tile * TILE, (tile + 1) * TILE)
-        for arr, dst in enumerate((o_ref, dq_ref, dk_ref, dv_ref)):
-            dst[rows] = jnp.stack(heads(arr, tile), axis=1)
-    second.wait()
-    final_ref[core] = sum_ref[...] + chip_ref[...]
-    third = swap(2, final_ref.at[core], final_ref.at[core], core_peer)
-    third.wait()
-    for which in range(2):
-        dw_ref[which * half:(which + 1) * half] = jnp.stack(
-            [final_ref[which, :half, :SUB], final_ref[which, :half, SUB:]], axis=1)
-    tail = final_ref[0, half:]
-    du_ref[...] = jnp.concatenate([tail[0:1, :SUB], tail[0:1, SUB:]], axis=0)
-    dvb_ref[...] = jnp.concatenate([tail[1:2, :SUB], tail[1:2, SUB:]], axis=0)
-
-
-def finish(own, got, rel_table, bias_grad, seq_shape, w_shape):
-    half_rows = w_shape[0] // 2 + 8
-    wide = 2 * SUB
-    vmem = pl.BlockSpec(memory_space=pltpu.VMEM)
-    bias = jax.ShapeDtypeStruct((2, SUB), F32)
-    seq = jax.ShapeDtypeStruct(seq_shape, BF16)
-    return pl.pallas_call(
-        finish_kernel,
-        in_specs=[pl.BlockSpec(memory_space=pl.ANY)] * 3 + [vmem],
-        out_specs=[vmem] * 7,
-        out_shape=[seq, seq, seq, seq, jax.ShapeDtypeStruct(w_shape, F32), bias, bias],
-        scratch_shapes=[
-            pltpu.VMEM(own.shape, BF16),
-            pltpu.VMEM(got.shape, BF16),
-            pltpu.VMEM(rel_table.shape, BF16),
-            pltpu.VMEM((rel_table.shape[0], wide), BF16),
-            pltpu.VMEM((2, half_rows, wide), F32),
-            pltpu.VMEM((half_rows, wide), F32),
-            pltpu.VMEM((half_rows, wide), F32),
-            pltpu.VMEM((half_rows, wide), F32),
-            pltpu.VMEM((2, half_rows, wide), F32),
-            pltpu.SemaphoreType.DMA((3,)),
-            pltpu.SemaphoreType.DMA((3,)),
-            pltpu.SemaphoreType.DMA((5,)),
-        ],
-        compiler_params=pltpu.CompilerParams(vmem_limit_bytes=48 * 1024 * 1024, collective_id=1, has_side_effects=True),
-        name="finish",
-    )(own, got, rel_table, bias_grad)
-
-
 def solution(mesh):
     seq_spec = P('cp', 'hp', None)
     head_spec = P('hp', None)
     weight_spec = P(None, 'hp', None)
 
     def local_fn(q, k, v, u_bias, v_bias, rel_table, w_rel, d_out):
-        res_own, res_got, bias_grad = run_attn(u_bias, v_bias, k, v, q, d_out, rel_table, w_rel)
-        out, dq, dk, dv, d_w_rel, d_u, d_v = finish(res_own, res_got, rel_table, bias_grad, q.shape, w_rel.shape)
-        return out, dq, dk, dv, d_u, d_v, d_w_rel
+        out, dq, dk, dv, d_w_rel, d_u, d_v, _, _ = run_attn(u_bias, v_bias, k, v, q, d_out, rel_table, w_rel)
+        return out, dq, dk, dv, d_u, d_v, jnp.swapaxes(d_w_rel, 0, 1)
 
     return jax.shard_map(
         local_fn,

time: 170 us -> 169 us (level)
    pallas_call x1 -> x0, Pallas kernels: 19.1 us -> none  [finish(): pl.pallas_call(finish_kernel, in_specs=[pl.BlockSpec(memory_space=pl.ANY)...]
    pallas_call x1, Pallas kernels: 142 us -> 160 us  [run_attn(): pl.pallas_call(functools.partial(attn_kernel, num_tiles, head_dim ** (-0....]
    unnamed x11 -> x19, local copies, waits for them, and re-layouts: 7.78 us -> 7.79 us
where the time goes in v6:
time: 169 us; the launch traced here: 168 us
  Pallas kernels  160 us (95%)
  local copies, waits for them, and re-layouts  7.79 us (5%)
    pallas_call x1, Pallas kernels, run_attn(): pl.pallas_call(functools.partial(attn_kernel, num_tiles, head_dim ** (-0....  160 us
    unnamed x19, local copies, waits for them, and re-layouts  7.79 us

profile of v6, /device:TPU:0, one launch (start us, length us, event | category | flops | bytes accessed | tf_op | source)
XLA Modules:
  0.0 168.1 jit_solution(15770763894256866101)
XLA Ops:
  0.6 159.7 %attn_rows.1 = (bf16[1536,2,128]{2,1,0:T(2,128)(2,1)}, bf16[1536,2,128]{2,1,0:T(2,128)(2,1)}, bf16[1536,2,128]{2,1,0:T(2,128)(2,1)}, bf16[1536,2,128]{2,1,0:T(2,...) custom-call(f32[2,128]{1,0:T(2,128)} %u_ref.1, ...), custom_call_target="tpu_custom_call" | custom-call | tf_op jit(solution)/shard_map/attn_rows/pallas_call | solution.py:578
  160.3 0.0 copy-start.3
  160.3 0.0 copy-start.2
  160.3 3.1 %copy.15 = f32[1024,2,128]{2,1,0:T(2,128)} copy(f32[1024,2,128]{2,0,1:T(8,128)} %bitcast.1) | data formatting | bytes 2097152
  163.5 0.0 copy-done.3
  163.5 0.0 copy-start.1
  163.5 0.9 copy.22
  164.3 0.0 copy-done.2
  164.4 0.0 copy-start
  164.4 0.9 copy.23
  165.2 0.0 copy-done.1
  165.2 0.0 copy-start.5
  165.2 0.0 copy-start.4
  165.2 0.9 copy.24
  166.1 0.0 copy-done
  166.1 0.9 copy.25
  167.0 0.0 copy-done.5
  167.0 0.6 copy.26
  167.6 0.0 copy-done.4
  167.6 0.6 copy.27
Async XLA Ops:
  160.3 3.1 %copy-start.3 = (bf16[1536,2,128]{2,1,0:T(2,128)(2,1)S(1)}, bf16[1536,2,128]{2,1,0:T(2,128)(2,1)}, u32[]{:S(2)}) copy-start(bf16[1536,2,128]{2,1,0:T(2,128)(2,1)} %get-tuple-element.35) | copy-start | bytes 2359300
  160.3 4.0 %copy-start.2 = (bf16[1536,2,128]{2,1,0:T(2,128)(2,1)S(1)}, bf16[1536,2,128]{2,1,0:T(2,128)(2,1)}, u32[]{:S(2)}) copy-start(bf16[1536,2,128]{2,1,0:T(2,128)(2,1)} %get-tuple-element.36) | copy-start | bytes 2359300
  163.5 1.8 %copy-start.1 = (bf16[1536,2,128]{2,1,0:T(2,128)(2,1)S(1)}, bf16[1536,2,128]{2,1,0:T(2,128)(2,1)}, u32[]{:S(2)}) copy-start(bf16[1536,2,128]{2,1,0:T(2,128)(2,1)} %get-tuple-element.37) | copy-start | bytes 2359300
  164.4 1.8 %copy-start = (bf16[1536,2,128]{2,1,0:T(2,128)(2,1)S(1)}, bf16[1536,2,128]{2,1,0:T(2,128)(2,1)}, u32[]{:S(2)}) copy-start(bf16[1536,2,128]{2,1,0:T(2,128)(2,1)} %get-tuple-element.38) | copy-start | bytes 2359300
  165.2 1.8 %copy-start.5 = (f32[2,128]{1,0:T(2,128)S(1)}, f32[2,128]{1,0:T(2,128)}, u32[]{:S(2)}) copy-start(f32[2,128]{1,0:T(2,128)} %get-tuple-element.39) | copy-start | bytes 3076
  165.2 2.3 %copy-start.4 = (f32[2,128]{1,0:T(2,128)S(1)}, f32[2,128]{1,0:T(2,128)}, u32[]{:S(2)}) copy-start(f32[2,128]{1,0:T(2,128)} %get-tuple-element.40) | copy-start | bytes 3076

commit v7 on v6

--- a/solution.py
+++ b/solution.py
@@ -36,10 +36,10 @@
 
 def attn_kernel(num_tiles, inv_sqrt, u_ref, v_ref, kin_ref, vin_ref, qin_ref, doin_ref, table_in_ref, w_in_ref,
                 o_ref, dq_ref, dk_out_ref, dv_out_ref, dw_out_ref, du_ref, dvb_ref, res_own_ref, res_got_ref,
-                full_ref, acc_ref, kt_ref, valt_ref, relt_ref, sc_ref, rot_ref, ds_ref, dw_ref, p_ref,
+                full_ref, acc_ref, kt_ref, valt_ref, relt_ref, sc_ref, rot_ref, ds_ref,
                 qu_ref, qv_ref, qut_ref, qvt_ref, dot_ref, max_ref, sum_ref, gu_ref, gv_ref, row_ref,
                 st_rows_ref, st_grad_ref, part_ref, away_ref, raw_ref, table_ref, w_ref, wide_ref, bias_ref, res_rel_ref,
-                core_ref, chip_ref, final_ref, sum_send, sum_recv,
+                core_ref, chip_ref, final_ref, dw_stage_ref, sum_send, sum_recv,
                 local_sems, own_send, own_recv, cross_send, cross_recv, fwd_send, fwd_recv,
                 part_send, part_recv, rows_send, grad_send, res_sems, load_sems, out_sems):
     step = pl.program_id(0)
@@ -168,11 +168,11 @@
         quarter = half // 2
         size = quarter + 8
 
-        def piece(which, chunk):
-            return rot_ref.at[which, pl.ds(0, size), pl.ds(chunk * 256, 256)]
-
-        def total_piece(chunk):
-            return rot_ref.at[2, pl.ds(0, size), pl.ds(chunk * 256, 256)]
+        def piece(which, src):
+            return rot_ref.at[which, pl.ds(0, size), pl.ds(src * 256, 256)]
+
+        def total_piece(src):
+            return rot_ref.at[2, pl.ds(0, size), pl.ds(src * 256, 256)]
 
         def wait_res(which, part):
             for local in range(block_tiles):
@@ -182,34 +182,30 @@
                     dst = (res_own_ref, res_got_ref)[which].at[local, PARTS[part]]
                 pltpu.make_async_copy(dst, dst, res_sems.at[which, part, local]).wait()
 
-        def partial(which, chunk, src):
-            head = chip if src == 0 else 1 - chip
-            lanes = pl.ds(pl.multiple_of(head * SUB, SUB), SUB)
-            at = pl.ds(pl.multiple_of(which * half + chunk * quarter, 256), quarter)
+        def partial(which, src):
             d_rel = jnp.concatenate([res_rel_ref[src, tile] for tile in range(block_tiles)], axis=0)
-            piece(which, chunk)[pl.ds(0, quarter), lanes] = lax.dot_general(
-                table_ref[:, at], d_rel, (((0,), (0,)), ((), ())), preferred_element_type=F32)
-            bias = bias_ref[...] if src == 0 else jnp.zeros_like(bias_ref)
-            piece(which, chunk)[pl.ds(quarter, 8), lanes] = jnp.concatenate([bias, jnp.zeros((6, SUB), F32)], axis=0)
-
-        def swap(idx, src, dst, peer):
-            copy = to_device(src, dst, sum_send.at[idx], sum_recv.at[idx], peer)
+            for side in range(2):
+                at = pl.ds(pl.multiple_of(which * half + side * quarter, 256), quarter)
+                piece(which, src)[pl.ds(0, quarter), sub(side)] = lax.dot_general(
+                    table_ref[:, at], d_rel, (((0,), (0,)), ((), ())), preferred_element_type=F32)
+            bias = bias_ref[...] if src == 0 else jnp.zeros(bias_ref.shape, F32)
+            rows = jnp.concatenate([bias, jnp.zeros((6, SUB), F32)], axis=0)
+            piece(which, src)[pl.ds(quarter, 8), :] = jnp.concatenate([rows, rows], axis=1)
+
+        def swap(src, dst, send_idx, recv_idx, peer):
+            copy = to_device(src, dst, sum_send.at[send_idx], sum_recv.at[recv_idx], peer)
             copy.start()
             return copy
 
-        order = ((1 - core, 0), (core, 0), (1 - core, 1), (core, 1))
-        wait_res(0, 2)
-        for which, chunk in order:
-            partial(which, chunk, 0)
-        wait_res(1, 2)
         first, second, third = [], [], []
-        for chunk in range(2):
-            partial(1 - core, chunk, 1)
-            first.append(swap(chunk, piece(1 - core, chunk), core_ref.at[chunk], core_peer))
-            partial(core, chunk, 1)
-            first[chunk].wait()
-            total_piece(chunk)[...] = piece(core, chunk)[...] + core_ref[chunk]
-            second.append(swap(2 + chunk, total_piece(chunk), chip_ref.at[chunk], chip_peer))
+        for src in range(2):
+            wait_res(src, 2)
+            partial(1 - core, src)
+            first.append(swap(piece(1 - core, src), core_ref.at[src], src, src, core_peer))
+            partial(core, src)
+            first[src].wait()
+            total_piece(src)[...] = piece(core, src)[...] + core_ref[src]
+            second.append(swap(total_piece(src), chip_ref.at[1 - src], 2 + src, 3 - src, chip_peer))
         for part in range(2):
             wait_res(0, part)
             wait_res(1, part)
@@ -232,28 +228,36 @@
                   for arr, dst in enumerate((o_ref, dq_ref, dk_out_ref, dv_out_ref))]
         for store in stores:
             store.start()
-
-        def put(which, chunk):
-            base = pl.multiple_of(which * half + chunk * quarter, 256)
-            for head in range(2):
-                store = pltpu.make_async_copy(
-                    final_ref.at[which, chunk, pl.ds(0, quarter), pl.ds(head * SUB, SUB)],
-                    dw_out_ref.at[head, pl.ds(base, quarter)], out_sems.at[len(stores) - 4])
+        stores_rows, stores = stores, []
+
+        def put(which):
+            own, got = final_ref.at[which, 0], final_ref.at[which, 1]
+            for side in range(2):
+                own_part, got_part = own[pl.ds(0, quarter), sub(side)], got[pl.ds(0, quarter), sub(side)]
+                at = pl.ds(pl.multiple_of(which * half + side * quarter, 256), quarter)
+                stage = dw_stage_ref.at[pl.ds(side * quarter, quarter)]
+                stage[...] = jnp.stack([jnp.where(chip == 0, own_part, got_part), jnp.where(chip == 0, got_part, own_part)], axis=1)
+                store = pltpu.make_async_copy(stage, dw_out_ref.at[at], out_sems.at[len(stores)])
                 store.start()
                 stores.append(store)
 
-        for chunk in range(2):
-            second[chunk].wait()
-            final_ref[core, chunk] = total_piece(chunk)[...] + chip_ref[chunk]
-            third.append(swap(4 + chunk, final_ref.at[core, chunk], final_ref.at[core, chunk], core_peer))
-            put(core, chunk)
-        for chunk in range(2):
-            third[chunk].wait()
-            put(1 - core, chunk)
-        sums = final_ref[0, 0, quarter:]
-        du_ref[...] = jnp.concatenate([sums[0:1, :SUB], sums[0:1, SUB:]], axis=0)
-        dvb_ref[...] = jnp.concatenate([sums[1:2, :SUB], sums[1:2, SUB:]], axis=0)
+        for src in (1, 0):
+            second[src].wait_send()
+            to_device(total_piece(src), chip_ref.at[src], sum_send.at[2 + src], sum_recv.at[2 + src], chip_peer).wait_recv()
+            final_ref[core, src] = total_piece(src)[...] + chip_ref[src]
+            third.append(swap(final_ref.at[core, src], final_ref.at[core, src], 4 + src, 4 + src, core_peer))
+        put(core)
+        third[0].wait()
+        third[1].wait()
         for store in stores:
+            store.wait()
+        stores.clear()
+        put(1 - core)
+        own, got = final_ref[0, 0, quarter:, :SUB], final_ref[0, 1, quarter:, :SUB]
+        head0, head1 = jnp.where(chip == 0, own, got), jnp.where(chip == 0, got, own)
+        du_ref[...] = jnp.concatenate([head0[0:1], head1[0:1]], axis=0)
+        dvb_ref[...] = jnp.concatenate([head0[1:2], head1[1:2]], axis=0)
+        for store in stores + stores_rows:
             store.wait()
 
     def put_heads(arr, start, size, first, second):
@@ -413,25 +417,35 @@
     def _():
         arrive((1,))
 
-    def prob_body(tile, _):
+    def prob_tile(tile, diag):
         for top in range(0, NSUB, 2):
             rows = slice(top * SUB, (top + 2) * SUB)
+            width = top + 2 if diag else NSUB
             prob_rows = []
             for a in range(top, top + 2):
                 run_sum = sum_ref[sub(a), :]
                 row_max = max_ref[sub(a), :]
                 prob_cols = []
-                for c in range(NSUB):
+                for c in range(width):
+                    if diag and c > a:
+                        prob_cols.append(jnp.zeros((SUB, SUB), BF16))
+                        continue
                     where = pl.ds(pl.multiple_of(tile * TILE + c * SUB, SUB), SUB)
                     prob = jnp.exp2(sc_ref[sub(a), where] - row_max)
                     prob_cols.append(prob.astype(BF16))
                     run_sum = run_sum + prob
                 sum_ref[sub(a), :] = run_sum
                 prob_rows.append(jnp.concatenate(prob_cols, axis=1))
-            gu_ref[rows, :] += dot(jnp.concatenate(prob_rows, axis=0), val_ref[cols(tile), :])
+            keys = pl.ds(pl.multiple_of(tile * TILE, TILE), width * SUB)
+            gu_ref[rows, :] += dot(jnp.concatenate(prob_rows, axis=0), val_ref[keys, :])
+
+    def prob_body(tile, _):
+        prob_tile(tile, False)
         return 0
 
-    lax.fori_loop(0, blk + 1, prob_body, 0)
+    lax.fori_loop(0, blk, prob_body, 0)
+    prob_tile(blk, True)
+
     @pl.when(step == half_steps - chip)
     def _():
         arrive((4,))
@@ -447,7 +461,7 @@
     gu_ref[...] = jnp.zeros_like(gu_ref)
     ds_ref[1, :, :] = jnp.zeros((TILE, TILE), F32)
 
-    def grad_body(tile, _):
+    def grad_tile(tile, diag):
         now = lax.rem(tile, 2)
         old = 1 - now
         for half in range(2):
@@ -455,6 +469,8 @@
             win = pl.ds(start, 256)
             d_val = d_key = None
             for top in range(0, NSUB, 2):
+                if diag and 2 * half > top:
+                    continue
                 rows = slice(top * SUB, (top + 2) * SUB)
                 do_rows = pl.ds(pl.multiple_of(blk * TILE + top * SUB, SUB), 2 * SUB)
                 d_prob = dot(do_ref[do_rows, :], valt_ref[:, win])
@@ -465,6 +481,10 @@
                     prob_cols, score_cols = [], []
                     for c2 in range(2):
                         c = half * 2 + c2
+                        if diag and c > a:
+                            prob_cols.append(jnp.zeros((SUB, SUB), BF16))
+                            score_cols.append(jnp.zeros((SUB, SUB), BF16))
+                            continue
                         prob = jnp.exp2(sc_ref[sub(a), pl.ds(pl.multiple_of(tile * TILE + c * SUB, SUB), SUB)] - log_norm)
                         d_score = prob * (d_prob[sub(a - top), sub(c2)] - shift)
                         ds_ref[now, sub(a), sub(c)] = roll_left(d_score, flip)
@@ -503,6 +523,9 @@
             start = pl.multiple_of(rel_tile * TILE + half * 256, 256)
             drel_ref[:, pl.ds(start, 256)] += d_off[half]
 
+    def grad_body(tile, _):
+        grad_tile(tile, False)
+
         @pl.when((step == last) & (lax.rem(tile, 2) == 1) & (tile < top_tile))
         def _():
             key_pair = lax.div(tile, 2)
@@ -521,7 +544,8 @@
         finish_offsets(pair_at(step - 1))
         finish_keys(pair_at(step - 1))
 
-    lax.fori_loop(0, blk + 1, grad_body, 0)
+    lax.fori_loop(0, blk, grad_body, 0)
+    grad_tile(blk, True)
     grad_u = gu_ref[...] * inv_sqrt
     grad_v = gv_ref[...] * inv_sqrt
     st_rows_ref[step, 1] = (grad_u + grad_v).astype(BF16)
@@ -572,7 +596,7 @@
     result = jax.ShapeDtypeStruct((block_tiles, 4, TILE, head_dim), BF16)
     seq = jax.ShapeDtypeStruct(k.shape, BF16)
     bias = jax.ShapeDtypeStruct((2, head_dim), F32)
-    d_weights = jax.ShapeDtypeStruct((2, w_rel.shape[0], head_dim), F32)
+    d_weights = jax.ShapeDtypeStruct(w_rel.shape, F32)
     size = w_rel.shape[0] // 4 + 8
     dma = pltpu.SemaphoreType.DMA
     return pl.pallas_call(
@@ -589,8 +613,6 @@
             pltpu.VMEM((TILE, seq_len), F32),
             pltpu.VMEM((3, TILE, TILE), F32),
             pltpu.VMEM((2, TILE, TILE), F32),
-            pltpu.VMEM((TILE, TILE), BF16),
-            pltpu.VMEM((TILE, TILE), BF16),
             pltpu.VMEM((TILE, head_dim), BF16),
             pltpu.VMEM((TILE, head_dim), BF16),
             pltpu.VMEM((head_dim, TILE), BF16),
@@ -614,9 +636,10 @@
             pltpu.VMEM((2, size, 2 * head_dim), F32),
             pltpu.VMEM((2, size, 2 * head_dim), F32),
             pltpu.VMEM((2, 2, size, 2 * head_dim), F32),
+            pltpu.VMEM((w_rel.shape[0] // 2,) + w_rel.shape[1:], F32),
             dma((6,)), dma((6,)),
             dma((6,)), dma((5,)), dma((5,)), dma((5,)), dma((5,)), dma((5,)), dma((5,)),
-            dma((steps, 3)), dma((steps, 3)), dma((steps,)), dma((steps, 2)), dma((2, 3, block_tiles)), dma((block_tiles, 2)), dma((8,)),
+            dma((steps, 3)), dma((steps, 3)), dma((steps,)), dma((steps, 2)), dma((2, 3, block_tiles)), dma((block_tiles, 2)), dma((2,)),
         ],
         out_shape=[seq, seq, seq, seq, d_weights, bias, bias, result, result],
         compiler_params=pltpu.CompilerParams(
@@ -638,7 +661,7 @@
 
     def local_fn(q, k, v, u_bias, v_bias, rel_table, w_rel, d_out):
         out, dq, dk, dv, d_w_rel, d_u, d_v, _, _ = run_attn(u_bias, v_bias, k, v, q, d_out, rel_table, w_rel)
-        return out, dq, dk, dv, d_u, d_v, jnp.swapaxes(d_w_rel, 0, 1)
+        return out, dq, dk, dv, d_u, d_v, d_w_rel
 
     return jax.shard_map(
         local_fn,

time: 169 us -> 164 us (0.970)
  Pallas kernels: 160 us -> 155 us
    pallas_call x1, Pallas kernels: 160 us -> 155 us  [run_attn(): pl.pallas_call(functools.partial(attn_kernel, num_tiles, head_dim ** (-0....]
where the time goes in v7:
time: 164 us; the launch traced here: 163 us
  Pallas kernels  155 us (95%)
  local copies, waits for them, and re-layouts  7.18 us (4%)
    pallas_call x1, Pallas kernels, run_attn(): pl.pallas_call(functools.partial(attn_kernel, num_tiles, head_dim ** (-0....  155 us
    unnamed x19, local copies, waits for them, and re-layouts  7.18 us

profile of v7, /device:TPU:0, one launch (start us, length us, event | category | flops | bytes accessed | tf_op | source)
XLA Modules:
  0.0 163.3 jit_solution(3206066952036056715)
XLA Ops:
  0.6 155.5 %attn_rows.1 = (bf16[1536,2,128]{2,1,0:T(2,128)(2,1)}, bf16[1536,2,128]{2,1,0:T(2,128)(2,1)}, bf16[1536,2,128]{2,1,0:T(2,128)(2,1)}, bf16[1536,2,128]{2,1,0:T(2,...) custom-call(f32[2,128]{1,0:T(2,128)} %u_ref.1, ...), custom_call_target="tpu_custom_call" | custom-call | tf_op jit(solution)/shard_map/attn_rows/pallas_call | solution.py:602
  156.1 0.0 copy-start.3
  156.1 0.0 copy-start.2
  156.1 2.4 %copy.22 = bf16[1536,2,128]{2,1,0:T(2,128)(2,1)} copy(bf16[1536,2,128]{2,1,0:T(2,128)(2,1)} %get-tuple-element.28) | data formatting | bytes 1572864
  158.6 0.0 copy-done.3
  158.6 0.0 copy-start.1
  158.6 0.9 copy.23
  159.4 0.0 copy-done.2
  159.4 0.0 copy-start.5
  159.4 0.0 copy-start.4
  159.5 0.0 copy-start
  159.5 0.9 copy.24
  160.3 0.0 copy-done.1
  160.3 0.9 copy.25
  161.2 0.0 copy-done.5
  161.2 0.6 copy.26
  161.8 0.0 copy-done.4
  161.8 0.6 copy.27
  162.4 0.0 copy-done
  162.4 1.0 copy.28
Async XLA Ops:
  156.1 2.4 %copy-start.3 = (bf16[1536,2,128]{2,1,0:T(2,128)(2,1)S(1)}, bf16[1536,2,128]{2,1,0:T(2,128)(2,1)}, u32[]{:S(2)}) copy-start(bf16[1536,2,128]{2,1,0:T(2,128)(2,1)} %get-tuple-element.29) | copy-start | bytes 2359300
  156.1 3.3 %copy-start.2 = (bf16[1536,2,128]{2,1,0:T(2,128)(2,1)S(1)}, bf16[1536,2,128]{2,1,0:T(2,128)(2,1)}, u32[]{:S(2)}) copy-start(bf16[1536,2,128]{2,1,0:T(2,128)(2,1)} %get-tuple-element.30) | copy-start | bytes 2359300
  158.6 1.8 %copy-start.1 = (bf16[1536,2,128]{2,1,0:T(2,128)(2,1)S(1)}, bf16[1536,2,128]{2,1,0:T(2,128)(2,1)}, u32[]{:S(2)}) copy-start(bf16[1536,2,128]{2,1,0:T(2,128)(2,1)} %get-tuple-element.31) | copy-start | bytes 2359300
  159.4 1.8 %copy-start.5 = (f32[2,128]{1,0:T(2,128)S(1)}, f32[2,128]{1,0:T(2,128)}, u32[]{:S(2)}) copy-start(f32[2,128]{1,0:T(2,128)} %get-tuple-element.32) | copy-start | bytes 3076
  159.4 2.3 %copy-start.4 = (f32[2,128]{1,0:T(2,128)S(1)}, f32[2,128]{1,0:T(2,128)}, u32[]{:S(2)}) copy-start(f32[2,128]{1,0:T(2,128)} %get-tuple-element.33) | copy-start | bytes 3076
  159.5 2.9 %copy-start = (f32[1024,2,128]{2,1,0:T(2,128)S(1)}, f32[1024,2,128]{2,1,0:T(2,128)}, u32[]{:S(2)}) copy-start(f32[1024,2,128]{2,1,0:T(2,128)} %get-tuple-element.34) | copy-start | bytes 3145732
